TPU v7x, 32 devices: a whole 2x2x4 slice. The times are simulated.
32 devices in a mesh: gx: 8 (over z, x), gy: 4 (over y, core).
Axes of the slice: x: 2, y: 2, z: 4, core: 2. Of those that a mesh axis runs over, the one named last changes fastest.
Arguments:
- map_codes: int32 [1024, 2048], P('gy', 'gx'), may hold values from 0 to 63
- reward_table: float32 [4, 64], replicated, may hold values from -1 to 1
- start_cell: int32 [65536], P(('gx', 'gy')), may hold values from 0 to 65535, as said below
- agent_task: int32 [65536], P(('gx', 'gy')), may hold values from 0 to 3
- actions: int32 [16, 65536], P(None, ('gx', 'gy')), may hold values from 0 to 4, as said below
Outputs:
- values: float32 [4, 1024, 2048], P(None, 'gy', 'gx')
- agent_value: float32 [65536], P(('gx', 'gy'))
Inputs may be any that keep to these rules, and one draw needn't show every extreme that they name: `start_cell`: each agent starts inside the tile of its block. `actions`: 0 stays, 1 and 2 move one row up and down, 3 and 4 one column left and right. After its moves every agent stands in its starting tile or in one of the eight tiles around it (diagonal ones included); at most 128 agents of one block stand in any one of those eight tiles, and for every block exactly 128 stand in one of them.
All inputs are finite; a program needn't handle non-finite values.
Results may differ from a plain program's by a relative error of at most 0.00026.
Values sent between devices are 32-bit elements; how exact they have to be, the bound alone decides.
No kernel may reach another device: no remote copies, remote signals or barrier semaphores. Data moves between devices by JAX's collectives and lax.ppermute only.
A program may use at most 64 MiB of HBM per device.

v0:
```python
import math

import jax
import jax.numpy as jnp
from jax import lax
from jax.sharding import PartitionSpec as P

CAP = 128
SWEEPS = 16
CODES = 64
TERMINAL = 2


GAMMA = 0.95
PENALTY = 0.5
NEIGHBOURS = ((-1, -1), (-1, 0), (-1, 1), (0, -1), (0, 1), (1, -1), (1, 0), (1, 1))


def from_behind(value, axis, steps):
    count = lax.axis_size(axis)
    pairs = [(source, (source + steps) % count) for source in range(count)]
    return lax.ppermute(value, axis, pairs)


def with_halo(block, sides, width):
    for axis, dim in sides:
        count = lax.axis_size(axis)
        forward = [(i, i + 1) for i in range(count - 1)]
        forward.append((count - 1, 0))
        backward = [(target, source) for source, target in forward]
        low = lax.ppermute(
            lax.slice_in_dim(block, block.shape[dim] - width, None, axis=dim), axis, forward
        )
        high = lax.ppermute(lax.slice_in_dim(block, 0, width, axis=dim), axis, backward)
        block = jnp.concatenate([low, block, high], axis=dim)
    return block


def sweep_cells(reward, living, padded):
    from_above = padded[..., :-2, 1:-1]
    from_below = padded[..., 2:, 1:-1]
    from_left = padded[..., 1:-1, :-2]
    from_right = padded[..., 1:-1, 2:]
    highest = jnp.maximum(jnp.maximum(from_above, from_below), jnp.maximum(from_left, from_right))
    return reward + GAMMA * living * highest


def margin_part(padded, margin):
    offset = 4 - margin
    return padded[..., offset : padded.shape[-2] - offset, offset : padded.shape[-1] - offset]


def deliver(parcels):
    arrived = {}
    for offset_pair in NEIGHBOURS:
        moving = parcels[offset_pair]
        if offset_pair[1] != 0:
            moving = from_behind(moving, "gx", offset_pair[1])
        if offset_pair[0] != 0:
            moving = from_behind(moving, "gy", offset_pair[0])
        arrived[offset_pair] = moving
    return arrived


def on_device(map_codes, reward_table, start_cell, agent_task, actions):
    tile_rows, tile_cols = map_codes.shape
    cell_count = tile_rows * tile_cols
    row_moves = jnp.sum((actions == 2).astype(jnp.int32) - (actions == 1).astype(jnp.int32), axis=0)
    col_moves = jnp.sum((actions == 4).astype(jnp.int32) - (actions == 3).astype(jnp.int32), axis=0)
    local_row = start_cell // tile_cols + row_moves
    local_col = start_cell % tile_cols + col_moves
    row_owner = jnp.where(local_row < 0, -1, jnp.where(local_row >= tile_rows, 1, 0))
    col_owner = jnp.where(local_col < 0, -1, jnp.where(local_col >= tile_cols, 1, 0))
    owner_cell = (local_row - row_owner * tile_rows) * tile_cols + (
        local_col - col_owner * tile_cols
    )
    heading = ((row_owner + 1) * 3 + col_owner + 1).astype(jnp.int32)
    heading_hot = (heading[None, :] == jnp.arange(9, dtype=jnp.int32)[:, None]).astype(jnp.int32)
    ranking = jnp.sum(heading_hot * (jnp.cumsum(heading_hot, axis=1) - 1), axis=0)
    payload = jnp.stack([owner_cell, agent_task]).astype(jnp.float32).T
    blank = jnp.stack(
        [jnp.full((9, CAP), -1.0, jnp.float32), jnp.zeros((9, CAP), jnp.float32)], axis=1
    )
    packed = blank.at[heading, :, ranking].set(payload, mode="drop")
    parcels = {
        offset_pair: packed[(offset_pair[0] + 1) * 3 + offset_pair[1] + 1]
        for offset_pair in NEIGHBOURS
    }
    arrived = deliver(parcels)
    arrivals = jnp.stack([arrived[offset_pair] for offset_pair in NEIGHBOURS])
    foreign_cell = arrivals[:, 0].astype(jnp.int32).reshape(-1)
    foreign_task = arrivals[:, 1].astype(jnp.int32).reshape(-1)
    foreign_live = foreign_cell >= 0
    staying = heading == 4
    landing = jnp.concatenate(
        [
            jnp.where(staying, owner_cell, cell_count),
            jnp.where(foreign_live, foreign_cell, cell_count),
        ]
    )
    crowding = jnp.zeros((cell_count + 1,), jnp.float32).at[landing].add(1.0)[:cell_count]
    band_rows = math.gcd(tile_rows, max(1, 8192 // tile_cols))
    code_bands = map_codes.reshape(tile_rows // band_rows, band_rows * tile_cols)

    def lookup_band(band):
        band_hot = (jnp.arange(CODES, dtype=jnp.int32)[:, None] == band[None, :]).astype(
            jnp.float32
        )
        return jnp.dot(reward_table, band_hot, precision=lax.Precision.HIGHEST)

    looked = lax.map(lookup_band, code_bands)
    looked = jnp.transpose(looked, (1, 0, 2)).reshape(reward_table.shape[0], cell_count)
    reward = looked - PENALTY * crowding[None, :]
    reward = reward.reshape(reward_table.shape[0], tile_rows, tile_cols)
    living = (map_codes < CODES - TERMINAL).astype(jnp.float32)[None]
    padded_reward, padded_living = (
        with_halo(reward, (("gx", 2), ("gy", 1)), 4),
        with_halo(living, (("gx", 2), ("gy", 1)), 4),
    )

    def four_sweeps(block_index, current):
        widened = with_halo(current, (("gx", 2), ("gy", 1)), 4)
        for margin in (3, 2, 1, 0):
            widened = sweep_cells(
                margin_part(padded_reward, margin), margin_part(padded_living, margin), widened
            )
        return widened

    values = lax.fori_loop(0, SWEEPS // 4, four_sweeps, reward)
    flat_values = values.reshape(values.shape[0], cell_count)
    answers = flat_values[foreign_task, jnp.where(foreign_live, foreign_cell, 0)]
    answers = jnp.where(foreign_live, answers, 0.0).reshape(8, 1, CAP)
    replies = {}
    for order_index, offset_pair in enumerate(NEIGHBOURS):
        replies[-offset_pair[0], -offset_pair[1]] = answers[order_index]
    returned = deliver(replies)
    back_rows = []
    for heading_index in range(9):
        row_step = heading_index // 3 - 1
        col_step = heading_index % 3 - 1
        if row_step == 0 and col_step == 0:
            back_rows.append(jnp.zeros((CAP,), jnp.float32))
        else:
            back_rows.append(returned[-row_step, -col_step][0])
    back_table = jnp.stack(back_rows)
    far_value = back_table[heading, jnp.minimum(ranking, CAP - 1)]
    own_value = flat_values[agent_task, jnp.clip(owner_cell, 0, cell_count - 1)]
    agent_value = jnp.where(staying, own_value, far_value)
    return (values, agent_value)


def solution(mesh):
    placed = (P("gy", "gx"), P(), P(("gx", "gy")), P(("gx", "gy")), P(None, ("gx", "gy")))
    return jax.shard_map(
        on_device,
        mesh=mesh,
        in_specs=placed,
        out_specs=(P(None, "gy", "gx"), P(("gx", "gy"))),
        check_vma=False,
    )
```

profile of v0, /device:TPU:0, one launch (start us, length us, event | category | flops | bytes accessed | tf_op | source)
XLA Modules:
  0.0 314.0 jit_solution(13193085942918268071)
XLA Ops:
  3.2 2.6 reduce-window.6
  9.1 5.8 %scatter_fusion = f32[1152,2]{1,0:T(8,128)S(1)} fusion(f32[1152,2]{1,0:T(8,128)S(1)} %copy-done.10, s32[2048]{0:T(1024)S(1)} %broadcast_select_fusion.1, f32[2048,2]{1,0:T(8,128)S(1)} %copy.9), kind=kCustom, calls=%fused_computation.4 | custom fusion | bytes 57344
  15.2 6.1 %collective-permute-start.4 = (f32[2,128]{1,0:T(2,128)S(1)}, f32[2,128]{1,0:T(2,128)S(1)}, u32[]{:S(2)}, u32[]{:S(2)}) collective-permute-start(f32[2,128]{1,0:T(2,128)S(1)} %get-tuple-element.104), channel_id=1, source_target_pairs={{0,28},{4,0},{8,4},{12,8},{16,12},{20,16},{24,20},{28,24},{1,29},{... | collective-permute-start | bytes 3080 | tf_op jit(solution)/shard_map/ppermute | solution.py:22
  21.2 4.7 %collective-permute-start.11 = (f32[2,128]{1,0:T(2,128)S(1)}, f32[2,128]{1,0:T(2,128)S(1)}, u32[]{:S(2)}, u32[]{:S(2)}) collective-permute-start(f32[2,128]{1,0:T(2,128)S(1)} %get-tuple-element.99), channel_id=1, source_target_pairs={{0,28},{4,0},{8,4},{12,8},{16,12},{20,16},{24,20},{28,24},{1,29},{... | collective-permute-start | bytes 3080 | tf_op jit(solution)/shard_map/ppermute | solution.py:22
  26.0 6.6 %while.20 = (s32[]{:T(128)}, f32[8,4,8192]{2,1,0:T(4,128)S(1)}, s32[8,8192]{1,0:T(8,128)S(1)}, f32[4,64]{1,0:T(4,128)S(1)}, s32[]{:T(128)}) while((s32[]{:T(128)}, f32[8,4,8192]{2,1,0:T(4,128)S(1)}, s32[8,8192]{1,0:T(8,128)S(1)}, f32[4,64]{1,0:T(4,128)S(1)}, s32[]{:T(128)}) %tuple.74), condition=%wide.region_1.0_spmd, body=%wide.region_0.0_spmd.sunk | while | flops 25690112 | bytes 231493 | solution.py:111
  32.8 4.7 %collective-permute-start.9 = (f32[2,128]{1,0:T(2,128)S(1)}, f32[2,128]{1,0:T(2,128)S(1)}, u32[]{:S(2)}, u32[]{:S(2)}) collective-permute-start(f32[2,128]{1,0:T(2,128)S(1)} %get-tuple-element.101), channel_id=1, source_target_pairs={{0,28},{4,0},{8,4},{12,8},{16,12},{20,16},{24,20},{28,24},{1,29},{... | collective-permute-start | bytes 3080 | tf_op jit(solution)/shard_map/ppermute | solution.py:22
  39.8 3.9 %collective-permute-done.10 = f32[2,128]{1,0:T(2,128)S(1)} collective-permute-done((f32[2,128]{1,0:T(2,128)S(1)}, f32[2,128]{1,0:T(2,128)S(1)}, u32[]{:S(2)}, u32[]{:S(2)}) %collective-permute-start.10) | collective-permute-done | bytes 1056 | tf_op jit(solution)/shard_map/ppermute | solution.py:22
  44.7 4.7 %collective-permute-start.21 = (f32[1,256,4]{2,1,0:T(8,128)S(1)}, f32[1,256,4]{2,1,0:T(8,128)S(1)}, u32[]{:S(2)}, u32[]{:S(2)}) collective-permute-start(f32[1,256,4]{2,1,0:T(8,128)S(1)} %get-tuple-element.96), channel_id=1, source_target_pairs={{4,0},{8,4},{12,8},{16,12},{20,16},{24,20},{28,24},{0,28},{5,1},{9... | collective-permute-start | bytes 12296 | tf_op jit(solution)/shard_map/ppermute | solution.py:34
  49.5 18.0 %scatter_custom_fusion = f32[65537]{0:T(1024)S(1)} fusion(s32[3072]{0:T(1024)S(1)} %bitcast.130, f32[3072]{0:T(1024)S(1)} %broadcast.245, f32[]{:T(128)} %constant.33.clone.1), kind=kCustom, calls=%fused_computation.43 | custom fusion | flops 3072 | bytes 262152 | tf_op jit(solution)/shard_map/scatter-add | solution.py:101
  68.2 4.8 %collective-permute-start.17 = (f32[4,256,4]{2,1,0:T(8,128)S(1)}, f32[4,256,4]{2,1,0:T(8,128)S(1)}, u32[]{:S(2)}, u32[]{:S(2)}) collective-permute-start(f32[4,256,4]{2,1,0:T(8,128)S(1)} %get-tuple-element.92), channel_id=1, source_target_pairs={{4,0},{8,4},{12,8},{16,12},{20,16},{24,20},{28,24},{0,28},{5,1},{9... | collective-permute-start | bytes 49160 | tf_op jit(solution)/shard_map/ppermute | solution.py:34
  74.7 15.3 %collective-permute-done.16 = f32[4,256,4]{2,1,0:T(8,128)S(1)} collective-permute-done((f32[4,256,4]{2,1,0:T(8,128)S(1)}, f32[4,256,4]{2,1,0:T(8,128)S(1)}, u32[]{:S(2)}, u32[]{:S(2)}) %collective-permute-start.16) | collective-permute-done | bytes 16416 | tf_op jit(solution)/shard_map/ppermute | solution.py:31
  90.0 4.1 %collective-permute-done.17 = f32[4,256,4]{2,1,0:T(8,128)S(1)} collective-permute-done((f32[4,256,4]{2,1,0:T(8,128)S(1)}, f32[4,256,4]{2,1,0:T(8,128)S(1)}, u32[]{:S(2)}, u32[]{:S(2)}) %collective-permute-start.17) | collective-permute-done | bytes 16416 | tf_op jit(solution)/shard_map/ppermute | solution.py:34
  94.4 1.6 collective-permute-start.19
  98.2 156.7 %while.21 = (s32[]{:T(128)}, f32[4,256,256]{2,1,0:T(8,128)S(1)}, f32[1,256,256]{2,1,0:T(8,128)}, f32[4,264,264]{2,1,0:T(8,128)S(1)}, f32[1,264,264]{2,1,0:T(8,128)S(1)}, /*index=5*/f32[4,256,256]{2,1,0:T(8,128)}, s32[]{:T(128)}) while((s32[]{:T(128)}, f32[4,256,256]{2,1,0:T(8,128)S(1)}, f32[1,256,256]{2,1,0:T(8,128)}, ...), condition=%wide.region_10.11_spmd, body=%wide.region_9.10_spmd.sunk | while | flops 6767258 | bytes 41261200 | solution.py:129
  98.5 2.0 collective-permute-start.1
  102.6 21.8 %collective-permute-done = f32[4,256,4]{2,1,0:T(8,128)S(1)} collective-permute-done((f32[4,256,4]{2,1,0:T(8,128)S(1)}, f32[4,256,4]{2,1,0:T(8,128)S(1)}, u32[]{:S(2)}, u32[]{:S(2)}) %collective-permute-start) | collective-permute-done | bytes 16416 | tf_op jit(solution)/shard_map/while/body/eval_jaxpr/ppermute | solution.py:34
  128.0 1.8 collective-permute-done.3
  129.8 1.9 pad_maximum_fusion.15
  131.7 2.0 fusion.51
  133.7 1.8 fusion.52
  135.6 1.8 fusion.53
  138.6 2.0 collective-permute-start.1
  142.6 21.1 %collective-permute-done = f32[4,256,4]{2,1,0:T(8,128)S(1)} collective-permute-done((f32[4,256,4]{2,1,0:T(8,128)S(1)}, f32[4,256,4]{2,1,0:T(8,128)S(1)}, u32[]{:S(2)}, u32[]{:S(2)}) %collective-permute-start) | collective-permute-done | bytes 16416 | tf_op jit(solution)/shard_map/while/body/eval_jaxpr/ppermute | solution.py:34
  167.1 1.6 collective-permute-done.3
  168.7 1.9 pad_maximum_fusion.15
  170.6 2.0 fusion.51
  172.6 1.8 fusion.52
  174.4 1.8 fusion.53
  177.4 2.0 collective-permute-start.1
  181.5 20.3 %collective-permute-done = f32[4,256,4]{2,1,0:T(8,128)S(1)} collective-permute-done((f32[4,256,4]{2,1,0:T(8,128)S(1)}, f32[4,256,4]{2,1,0:T(8,128)S(1)}, u32[]{:S(2)}, u32[]{:S(2)}) %collective-permute-start) | collective-permute-done | bytes 16416 | tf_op jit(solution)/shard_map/while/body/eval_jaxpr/ppermute | solution.py:34
  205.7 1.9 collective-permute-done.3
  207.5 1.9 pad_maximum_fusion.15
  209.4 2.0 fusion.51
  211.4 1.8 fusion.52
  213.3 1.8 fusion.53
  216.3 2.0 collective-permute-start.1
  220.4 21.1 %collective-permute-done = f32[4,256,4]{2,1,0:T(8,128)S(1)} collective-permute-done((f32[4,256,4]{2,1,0:T(8,128)S(1)}, f32[4,256,4]{2,1,0:T(8,128)S(1)}, u32[]{:S(2)}, u32[]{:S(2)}) %collective-permute-start) | collective-permute-done | bytes 16416 | tf_op jit(solution)/shard_map/while/body/eval_jaxpr/ppermute | solution.py:34
  244.8 1.6 collective-permute-done.3
  246.4 1.9 pad_maximum_fusion.15
  248.3 2.0 fusion.51
  250.3 1.8 fusion.52
  252.2 1.8 fusion.53
  255.6 9.1 %gather_fusion.1 = f32[1024]{0:T(1024)S(1)} fusion(f32[4,65536]{1,0:T(4,128)S(1)} %bitcast.111, s32[1024]{0:T(1024)S(1)} %bitcast.114), kind=kCustom, calls=%fused_computation.1 | custom fusion | bytes 16384 | tf_op jit(solution)/shard_map/gather | solution.py:131
  265.0 4.5 %collective-permute-start.27 = (f32[1,128]{1,0:T(1,128)S(1)}, f32[1,128]{1,0:T(1,128)S(1)}, u32[]{:S(2)}, u32[]{:S(2)}) collective-permute-start(f32[1,128]{1,0:T(1,128)S(1)} %get-tuple-element.116), channel_id=1, source_target_pairs={{0,28},{4,0},{8,4},{12,8},{16,12},{20,16},{24,20},{28,24},{1,29},{... | collective-permute-start | bytes 1544 | tf_op jit(solution)/shard_map/ppermute | solution.py:22
  269.6 4.7 %collective-permute-start.34 = (f32[1,128]{1,0:T(1,128)S(1)}, f32[1,128]{1,0:T(1,128)S(1)}, u32[]{:S(2)}, u32[]{:S(2)}) collective-permute-start(f32[1,128]{1,0:T(1,128)S(1)} %get-tuple-element.111), channel_id=1, source_target_pairs={{0,28},{4,0},{8,4},{12,8},{16,12},{20,16},{24,20},{28,24},{1,29},{... | collective-permute-start | bytes 1544 | tf_op jit(solution)/shard_map/ppermute | solution.py:22
  274.3 4.7 %collective-permute-start.30 = (f32[1,128]{1,0:T(1,128)S(1)}, f32[1,128]{1,0:T(1,128)S(1)}, u32[]{:S(2)}, u32[]{:S(2)}) collective-permute-start(f32[1,128]{1,0:T(1,128)S(1)} %get-tuple-element.114), channel_id=1, source_target_pairs={{0,28},{4,0},{8,4},{12,8},{16,12},{20,16},{24,20},{28,24},{1,29},{... | collective-permute-start | bytes 1544 | tf_op jit(solution)/shard_map/ppermute | solution.py:22
  282.5 17.7 %gather_fusion = f32[2048]{0:T(1024)S(1)} fusion(f32[4,65536]{1,0:T(4,128)S(1)} %bitcast.112, s32[2048]{0:T(1024)S(1)} %get-tuple-element.80), kind=kCustom, calls=%fused_computation | custom fusion | bytes 32768 | tf_op jit(solution)/shard_map/gather | solution.py:147
  300.3 13.1 %gather_fusion.2 = f32[2048]{0:T(1024)S(1)} fusion(f32[9,128]{1,0:T(8,128)S(1)} %stack.51, s32[2048]{0:T(1024)S(1)} %bitcast.113), kind=kCustom, calls=%fused_computation.2 | custom fusion | bytes 32768 | tf_op jit(solution)/shard_map/gather | solution.py:146
  (231 shorter events, 52.9 us)
Async XLA Ops:
  15.2 17.6 %collective-permute-start.4 = (f32[2,128]{1,0:T(2,128)S(1)}, f32[2,128]{1,0:T(2,128)S(1)}, u32[]{:S(2)}, u32[]{:S(2)}) collective-permute-start(f32[2,128]{1,0:T(2,128)S(1)} %get-tuple-element.104), channel_id=1, source_target_pairs={{0,28},{4,0},{8,4},{12,8},{16,12},{20,16},{24,20},{28,24},{1,29},{... | collective-permute-start | bytes 3080 | tf_op jit(solution)/shard_map/ppermute | solution.py:22
  21.2 16.2 %collective-permute-start.7 = (f32[2,128]{1,0:T(2,128)S(1)}, f32[2,128]{1,0:T(2,128)S(1)}, u32[]{:S(2)}, u32[]{:S(2)}) collective-permute-start(f32[2,128]{1,0:T(2,128)S(1)} %get-tuple-element.102), channel_id=1, source_target_pairs={{0,4},{4,8},{8,12},{12,16},{16,20},{20,24},{24,28},{28,0},{1,5},{5... | collective-permute-start | bytes 3080 | tf_op jit(solution)/shard_map/ppermute | solution.py:22
  21.2 16.3 %collective-permute-start.11 = (f32[2,128]{1,0:T(2,128)S(1)}, f32[2,128]{1,0:T(2,128)S(1)}, u32[]{:S(2)}, u32[]{:S(2)}) collective-permute-start(f32[2,128]{1,0:T(2,128)S(1)} %get-tuple-element.99), channel_id=1, source_target_pairs={{0,28},{4,0},{8,4},{12,8},{16,12},{20,16},{24,20},{28,24},{1,29},{... | collective-permute-start | bytes 3080 | tf_op jit(solution)/shard_map/ppermute | solution.py:22
  25.9 11.8 %collective-permute-start.14 = (f32[2,128]{1,0:T(2,128)S(1)}, f32[2,128]{1,0:T(2,128)S(1)}, u32[]{:S(2)}, u32[]{:S(2)}) collective-permute-start(f32[2,128]{1,0:T(2,128)S(1)} %get-tuple-element.97), channel_id=1, source_target_pairs={{0,4},{4,8},{8,12},{12,16},{16,20},{20,24},{24,28},{28,0},{1,5},{5... | collective-permute-start | bytes 3080 | tf_op jit(solution)/shard_map/ppermute | solution.py:22
  32.6 6.7 %collective-permute-start.6 = (f32[2,128]{1,0:T(2,128)S(1)}, f32[2,128]{1,0:T(2,128)S(1)}, u32[]{:S(2)}, u32[]{:S(2)}) collective-permute-start(f32[2,128]{1,0:T(2,128)S(1)} %get-tuple-element.103), channel_id=1, source_target_pairs={{0,3},{1,0},{2,1},{3,2},{4,7},{5,4},{6,5},{7,6},{8,11},{9,8},{10,9... | collective-permute-start | bytes 3080 | tf_op jit(solution)/shard_map/ppermute | solution.py:22
  32.8 6.6 %collective-permute-start.9 = (f32[2,128]{1,0:T(2,128)S(1)}, f32[2,128]{1,0:T(2,128)S(1)}, u32[]{:S(2)}, u32[]{:S(2)}) collective-permute-start(f32[2,128]{1,0:T(2,128)S(1)} %get-tuple-element.101), channel_id=1, source_target_pairs={{0,28},{4,0},{8,4},{12,8},{16,12},{20,16},{24,20},{28,24},{1,29},{... | collective-permute-start | bytes 3080 | tf_op jit(solution)/shard_map/ppermute | solution.py:22
  37.4 6.3 %collective-permute-start.10 = (f32[2,128]{1,0:T(2,128)S(1)}, f32[2,128]{1,0:T(2,128)S(1)}, u32[]{:S(2)}, u32[]{:S(2)}) collective-permute-start(f32[2,128]{1,0:T(2,128)S(1)} %get-tuple-element.100), channel_id=1, source_target_pairs={{0,4},{4,8},{8,12},{12,16},{16,20},{20,24},{24,28},{28,0},{1,5},{5... | collective-permute-start | bytes 3080 | tf_op jit(solution)/shard_map/ppermute | solution.py:22
  37.5 7.1 %collective-permute-start.13 = (f32[2,128]{1,0:T(2,128)S(1)}, f32[2,128]{1,0:T(2,128)S(1)}, u32[]{:S(2)}, u32[]{:S(2)}) collective-permute-start(f32[2,128]{1,0:T(2,128)S(1)} %get-tuple-element.98), channel_id=1, source_target_pairs={{0,1},{1,2},{2,3},{3,0},{4,5},{5,6},{6,7},{7,4},{8,9},{9,10},{10,1... | collective-permute-start | bytes 3080 | tf_op jit(solution)/shard_map/ppermute | solution.py:22
  37.7 7.0 %collective-permute-start.5 = (f32[2,128]{1,0:T(2,128)S(1)}, f32[2,128]{1,0:T(2,128)S(1)}, u32[]{:S(2)}, u32[]{:S(2)}) collective-permute-start(f32[2,128]{1,0:T(2,128)S(1)} %collective-permute-done.4), channel_id=1, source_target_pairs={{0,3},{1,0},{2,1},{3,2},{4,7},{5,4},{6,5},{7,6},{8,11},{9,8},{10,9... | collective-permute-start | bytes 3080 | tf_op jit(solution)/shard_map/ppermute | solution.py:22
  39.3 10.1 %collective-permute-start.8 = (f32[2,128]{1,0:T(2,128)S(1)}, f32[2,128]{1,0:T(2,128)S(1)}, u32[]{:S(2)}, u32[]{:S(2)}) collective-permute-start(f32[2,128]{1,0:T(2,128)S(1)} %collective-permute-done.7), channel_id=1, source_target_pairs={{0,3},{1,0},{2,1},{3,2},{4,7},{5,4},{6,5},{7,6},{8,11},{9,8},{10,9... | collective-permute-start | bytes 3080 | tf_op jit(solution)/shard_map/ppermute | solution.py:22
  39.4 10.0 %collective-permute-start.12 = (f32[2,128]{1,0:T(2,128)S(1)}, f32[2,128]{1,0:T(2,128)S(1)}, u32[]{:S(2)}, u32[]{:S(2)}) collective-permute-start(f32[2,128]{1,0:T(2,128)S(1)} %collective-permute-done.11), channel_id=1, source_target_pairs={{0,1},{1,2},{2,3},{3,0},{4,5},{5,6},{6,7},{7,4},{8,9},{9,10},{10,1... | collective-permute-start | bytes 3080 | tf_op jit(solution)/shard_map/ppermute | solution.py:22
  43.7 5.7 %collective-permute-start.15 = (f32[2,128]{1,0:T(2,128)S(1)}, f32[2,128]{1,0:T(2,128)S(1)}, u32[]{:S(2)}, u32[]{:S(2)}) collective-permute-start(f32[2,128]{1,0:T(2,128)S(1)} %collective-permute-done.14), channel_id=1, source_target_pairs={{0,1},{1,2},{2,3},{3,0},{4,5},{5,6},{6,7},{7,4},{8,9},{9,10},{10,1... | collective-permute-start | bytes 3080 | tf_op jit(solution)/shard_map/ppermute | solution.py:22
  44.6 28.3 %collective-permute-start.20 = (f32[1,256,4]{2,1,0:T(8,128)S(1)}, f32[1,256,4]{2,1,0:T(8,128)S(1)}, u32[]{:S(2)}, u32[]{:S(2)}) collective-permute-start(f32[1,256,4]{2,1,0:T(8,128)S(1)} %get-tuple-element.95), channel_id=1, source_target_pairs={{0,4},{4,8},{8,12},{12,16},{16,20},{20,24},{24,28},{28,0},{1,5},{5... | collective-permute-start | bytes 12296 | tf_op jit(solution)/shard_map/ppermute | solution.py:31
  44.7 28.2 %collective-permute-start.21 = (f32[1,256,4]{2,1,0:T(8,128)S(1)}, f32[1,256,4]{2,1,0:T(8,128)S(1)}, u32[]{:S(2)}, u32[]{:S(2)}) collective-permute-start(f32[1,256,4]{2,1,0:T(8,128)S(1)} %get-tuple-element.96), channel_id=1, source_target_pairs={{4,0},{8,4},{12,8},{16,12},{20,16},{24,20},{28,24},{0,28},{5,1},{9... | collective-permute-start | bytes 12296 | tf_op jit(solution)/shard_map/ppermute | solution.py:34
  68.0 22.0 %collective-permute-start.16 = (f32[4,256,4]{2,1,0:T(8,128)S(1)}, f32[4,256,4]{2,1,0:T(8,128)S(1)}, u32[]{:S(2)}, u32[]{:S(2)}) collective-permute-start(f32[4,256,4]{2,1,0:T(8,128)S(1)} %get-tuple-element.91), channel_id=1, source_target_pairs={{0,4},{4,8},{8,12},{12,16},{16,20},{20,24},{24,28},{28,0},{1,5},{5... | collective-permute-start | bytes 49160 | tf_op jit(solution)/shard_map/ppermute | solution.py:31
  68.2 26.0 %collective-permute-start.17 = (f32[4,256,4]{2,1,0:T(8,128)S(1)}, f32[4,256,4]{2,1,0:T(8,128)S(1)}, u32[]{:S(2)}, u32[]{:S(2)}) collective-permute-start(f32[4,256,4]{2,1,0:T(8,128)S(1)} %get-tuple-element.92), channel_id=1, source_target_pairs={{4,0},{8,4},{12,8},{16,12},{20,16},{24,20},{28,24},{0,28},{5,1},{9... | collective-permute-start | bytes 49160 | tf_op jit(solution)/shard_map/ppermute | solution.py:34
  73.0 23.0 %collective-permute-start.22 = (f32[1,4,264]{2,1,0:T(4,128)S(1)}, f32[1,4,264]{2,1,0:T(4,128)S(1)}, u32[]{:S(2)}, u32[]{:S(2)}) collective-permute-start(f32[1,4,264]{2,1,0:T(4,128)S(1)} %get-tuple-element.93), channel_id=1, source_target_pairs={{0,1},{1,2},{2,3},{3,0},{4,5},{5,6},{6,7},{7,4},{8,9},{9,10},{10,1... | collective-permute-start | bytes 12680 | tf_op jit(solution)/shard_map/ppermute | solution.py:31
  73.5 22.5 %collective-permute-start.23 = (f32[1,4,264]{2,1,0:T(4,128)S(1)}, f32[1,4,264]{2,1,0:T(4,128)S(1)}, u32[]{:S(2)}, u32[]{:S(2)}) collective-permute-start(f32[1,4,264]{2,1,0:T(4,128)S(1)} %get-tuple-element.94), channel_id=1, source_target_pairs={{1,0},{2,1},{3,2},{0,3},{5,4},{6,5},{7,6},{4,7},{9,8},{10,9},{11,1... | collective-permute-start | bytes 12680 | tf_op jit(solution)/shard_map/ppermute | solution.py:34
  94.2 3.3 %collective-permute-start.18 = (f32[4,4,264]{2,1,0:T(4,128)S(1)}, f32[4,4,264]{2,1,0:T(4,128)S(1)}, u32[]{:S(2)}, u32[]{:S(2)}) collective-permute-start(f32[4,4,264]{2,1,0:T(4,128)S(1)} %get-tuple-element.89), channel_id=1, source_target_pairs={{0,1},{1,2},{2,3},{3,0},{4,5},{5,6},{6,7},{7,4},{8,9},{9,10},{10,1... | collective-permute-start | bytes 50696 | tf_op jit(solution)/shard_map/ppermute | solution.py:31
  94.4 3.2 %collective-permute-start.19 = (f32[4,4,264]{2,1,0:T(4,128)S(1)}, f32[4,4,264]{2,1,0:T(4,128)S(1)}, u32[]{:S(2)}, u32[]{:S(2)}) collective-permute-start(f32[4,4,264]{2,1,0:T(4,128)S(1)} %get-tuple-element.90), channel_id=1, source_target_pairs={{1,0},{2,1},{3,2},{0,3},{5,4},{6,5},{7,6},{4,7},{9,8},{10,9},{11,1... | collective-permute-start | bytes 50696 | tf_op jit(solution)/shard_map/ppermute | solution.py:34
  98.4 26.0 %collective-permute-start = (f32[4,256,4]{2,1,0:T(8,128)S(1)}, f32[4,256,4]{2,1,0:T(8,128)S(1)}, u32[]{:S(2)}, u32[]{:S(2)}) collective-permute-start(f32[4,256,4]{2,1,0:T(8,128)S(1)} %get-tuple-element.185), channel_id=1, source_target_pairs={{4,0},{8,4},{12,8},{16,12},{20,16},{24,20},{28,24},{0,28},{5,1},{9... | collective-permute-start | bytes 49160 | tf_op jit(solution)/shard_map/while/body/eval_jaxpr/ppermute | solution.py:34
  98.5 25.9 %collective-permute-start.1 = (f32[4,256,4]{2,1,0:T(8,128)S(1)}, f32[4,256,4]{2,1,0:T(8,128)S(1)}, u32[]{:S(2)}, u32[]{:S(2)}) collective-permute-start(f32[4,256,4]{2,1,0:T(8,128)S(1)} %get-tuple-element.186), channel_id=1, source_target_pairs={{0,4},{4,8},{8,12},{12,16},{16,20},{20,24},{24,28},{28,0},{1,5},{5... | collective-permute-start | bytes 49160 | tf_op jit(solution)/shard_map/while/body/eval_jaxpr/ppermute | solution.py:31
  126.0 2.0 collective-permute-start.2
  126.3 3.5 %collective-permute-start.3 = (f32[4,4,264]{2,1,0:T(4,128)S(1)}, f32[4,4,264]{2,1,0:T(4,128)}, u32[]{:S(2)}, u32[]{:S(2)}) collective-permute-start(f32[4,4,264]{2,1,0:T(4,128)S(1)} %get-tuple-element.188), channel_id=1, source_target_pairs={{0,1},{1,2},{2,3},{3,0},{4,5},{5,6},{6,7},{7,4},{8,9},{9,10},{10,1... | collective-permute-start | bytes 50696 | tf_op jit(solution)/shard_map/while/body/eval_jaxpr/ppermute | solution.py:31
  138.5 25.2 %collective-permute-start = (f32[4,256,4]{2,1,0:T(8,128)S(1)}, f32[4,256,4]{2,1,0:T(8,128)S(1)}, u32[]{:S(2)}, u32[]{:S(2)}) collective-permute-start(f32[4,256,4]{2,1,0:T(8,128)S(1)} %get-tuple-element.185), channel_id=1, source_target_pairs={{4,0},{8,4},{12,8},{16,12},{20,16},{24,20},{28,24},{0,28},{5,1},{9... | collective-permute-start | bytes 49160 | tf_op jit(solution)/shard_map/while/body/eval_jaxpr/ppermute | solution.py:34
  138.6 25.2 %collective-permute-start.1 = (f32[4,256,4]{2,1,0:T(8,128)S(1)}, f32[4,256,4]{2,1,0:T(8,128)S(1)}, u32[]{:S(2)}, u32[]{:S(2)}) collective-permute-start(f32[4,256,4]{2,1,0:T(8,128)S(1)} %get-tuple-element.186), channel_id=1, source_target_pairs={{0,4},{4,8},{8,12},{12,16},{16,20},{20,24},{24,28},{28,0},{1,5},{5... | collective-permute-start | bytes 49160 | tf_op jit(solution)/shard_map/while/body/eval_jaxpr/ppermute | solution.py:31
  165.3 1.7 collective-permute-start.2
  165.4 3.4 %collective-permute-start.3 = (f32[4,4,264]{2,1,0:T(4,128)S(1)}, f32[4,4,264]{2,1,0:T(4,128)}, u32[]{:S(2)}, u32[]{:S(2)}) collective-permute-start(f32[4,4,264]{2,1,0:T(4,128)S(1)} %get-tuple-element.188), channel_id=1, source_target_pairs={{0,1},{1,2},{2,3},{3,0},{4,5},{5,6},{6,7},{7,4},{8,9},{9,10},{10,1... | collective-permute-start | bytes 50696 | tf_op jit(solution)/shard_map/while/body/eval_jaxpr/ppermute | solution.py:31
  177.4 24.5 %collective-permute-start = (f32[4,256,4]{2,1,0:T(8,128)S(1)}, f32[4,256,4]{2,1,0:T(8,128)S(1)}, u32[]{:S(2)}, u32[]{:S(2)}) collective-permute-start(f32[4,256,4]{2,1,0:T(8,128)S(1)} %get-tuple-element.185), channel_id=1, source_target_pairs={{4,0},{8,4},{12,8},{16,12},{20,16},{24,20},{28,24},{0,28},{5,1},{9... | collective-permute-start | bytes 49160 | tf_op jit(solution)/shard_map/while/body/eval_jaxpr/ppermute | solution.py:34
  177.4 24.4 %collective-permute-start.1 = (f32[4,256,4]{2,1,0:T(8,128)S(1)}, f32[4,256,4]{2,1,0:T(8,128)S(1)}, u32[]{:S(2)}, u32[]{:S(2)}) collective-permute-start(f32[4,256,4]{2,1,0:T(8,128)S(1)} %get-tuple-element.186), channel_id=1, source_target_pairs={{0,4},{4,8},{8,12},{12,16},{16,20},{20,24},{24,28},{28,0},{1,5},{5... | collective-permute-start | bytes 49160 | tf_op jit(solution)/shard_map/while/body/eval_jaxpr/ppermute | solution.py:31
  203.5 2.2 collective-permute-start.2
  203.9 3.6 %collective-permute-start.3 = (f32[4,4,264]{2,1,0:T(4,128)S(1)}, f32[4,4,264]{2,1,0:T(4,128)}, u32[]{:S(2)}, u32[]{:S(2)}) collective-permute-start(f32[4,4,264]{2,1,0:T(4,128)S(1)} %get-tuple-element.188), channel_id=1, source_target_pairs={{0,1},{1,2},{2,3},{3,0},{4,5},{5,6},{6,7},{7,4},{8,9},{9,10},{10,1... | collective-permute-start | bytes 50696 | tf_op jit(solution)/shard_map/while/body/eval_jaxpr/ppermute | solution.py:31
  216.2 25.2 %collective-permute-start = (f32[4,256,4]{2,1,0:T(8,128)S(1)}, f32[4,256,4]{2,1,0:T(8,128)S(1)}, u32[]{:S(2)}, u32[]{:S(2)}) collective-permute-start(f32[4,256,4]{2,1,0:T(8,128)S(1)} %get-tuple-element.185), channel_id=1, source_target_pairs={{4,0},{8,4},{12,8},{16,12},{20,16},{24,20},{28,24},{0,28},{5,1},{9... | collective-permute-start | bytes 49160 | tf_op jit(solution)/shard_map/while/body/eval_jaxpr/ppermute | solution.py:34
  216.3 25.2 %collective-permute-start.1 = (f32[4,256,4]{2,1,0:T(8,128)S(1)}, f32[4,256,4]{2,1,0:T(8,128)S(1)}, u32[]{:S(2)}, u32[]{:S(2)}) collective-permute-start(f32[4,256,4]{2,1,0:T(8,128)S(1)} %get-tuple-element.186), channel_id=1, source_target_pairs={{0,4},{4,8},{8,12},{12,16},{16,20},{20,24},{24,28},{28,0},{1,5},{5... | collective-permute-start | bytes 49160 | tf_op jit(solution)/shard_map/while/body/eval_jaxpr/ppermute | solution.py:31
  243.1 1.7 collective-permute-start.2
  243.1 3.4 %collective-permute-start.3 = (f32[4,4,264]{2,1,0:T(4,128)S(1)}, f32[4,4,264]{2,1,0:T(4,128)}, u32[]{:S(2)}, u32[]{:S(2)}) collective-permute-start(f32[4,4,264]{2,1,0:T(4,128)S(1)} %get-tuple-element.188), channel_id=1, source_target_pairs={{0,1},{1,2},{2,3},{3,0},{4,5},{5,6},{6,7},{7,4},{8,9},{9,10},{10,1... | collective-permute-start | bytes 50696 | tf_op jit(solution)/shard_map/while/body/eval_jaxpr/ppermute | solution.py:31
  264.8 9.5 %collective-permute-start.24 = (f32[1,128]{1,0:T(1,128)S(1)}, f32[1,128]{1,0:T(1,128)S(1)}, u32[]{:S(2)}, u32[]{:S(2)}) collective-permute-start(f32[1,128]{1,0:T(1,128)S(1)} %get-tuple-element.118), channel_id=1, source_target_pairs={{0,4},{4,8},{8,12},{12,16},{16,20},{20,24},{24,28},{28,0},{1,5},{5... | collective-permute-start | bytes 1544 | tf_op jit(solution)/shard_map/ppermute | solution.py:22
  265.0 9.3 %collective-permute-start.27 = (f32[1,128]{1,0:T(1,128)S(1)}, f32[1,128]{1,0:T(1,128)S(1)}, u32[]{:S(2)}, u32[]{:S(2)}) collective-permute-start(f32[1,128]{1,0:T(1,128)S(1)} %get-tuple-element.116), channel_id=1, source_target_pairs={{0,28},{4,0},{8,4},{12,8},{16,12},{20,16},{24,20},{28,24},{1,29},{... | collective-permute-start | bytes 1544 | tf_op jit(solution)/shard_map/ppermute | solution.py:22
  269.6 9.5 %collective-permute-start.31 = (f32[1,128]{1,0:T(1,128)S(1)}, f32[1,128]{1,0:T(1,128)S(1)}, u32[]{:S(2)}, u32[]{:S(2)}) collective-permute-start(f32[1,128]{1,0:T(1,128)S(1)} %get-tuple-element.113), channel_id=1, source_target_pairs={{0,4},{4,8},{8,12},{12,16},{16,20},{20,24},{24,28},{28,0},{1,5},{5... | collective-permute-start | bytes 1544 | tf_op jit(solution)/shard_map/ppermute | solution.py:22
  269.6 10.6 %collective-permute-start.34 = (f32[1,128]{1,0:T(1,128)S(1)}, f32[1,128]{1,0:T(1,128)S(1)}, u32[]{:S(2)}, u32[]{:S(2)}) collective-permute-start(f32[1,128]{1,0:T(1,128)S(1)} %get-tuple-element.111), channel_id=1, source_target_pairs={{0,28},{4,0},{8,4},{12,8},{16,12},{20,16},{24,20},{28,24},{1,29},{... | collective-permute-start | bytes 1544 | tf_op jit(solution)/shard_map/ppermute | solution.py:22
  274.3 5.9 %collective-permute-start.26 = (f32[1,128]{1,0:T(1,128)S(1)}, f32[1,128]{1,0:T(1,128)S(1)}, u32[]{:S(2)}, u32[]{:S(2)}) collective-permute-start(f32[1,128]{1,0:T(1,128)S(1)} %get-tuple-element.117), channel_id=1, source_target_pairs={{0,1},{1,2},{2,3},{3,0},{4,5},{5,6},{6,7},{7,4},{8,9},{9,10},{10,1... | collective-permute-start | bytes 1544 | tf_op jit(solution)/shard_map/ppermute | solution.py:22
  274.3 7.1 %collective-permute-start.29 = (f32[1,128]{1,0:T(1,128)S(1)}, f32[1,128]{1,0:T(1,128)S(1)}, u32[]{:S(2)}, u32[]{:S(2)}) collective-permute-start(f32[1,128]{1,0:T(1,128)S(1)} %get-tuple-element.115), channel_id=1, source_target_pairs={{0,4},{4,8},{8,12},{12,16},{16,20},{20,24},{24,28},{28,0},{1,5},{5... | collective-permute-start | bytes 1544 | tf_op jit(solution)/shard_map/ppermute | solution.py:22
  274.3 7.7 %collective-permute-start.30 = (f32[1,128]{1,0:T(1,128)S(1)}, f32[1,128]{1,0:T(1,128)S(1)}, u32[]{:S(2)}, u32[]{:S(2)}) collective-permute-start(f32[1,128]{1,0:T(1,128)S(1)} %get-tuple-element.114), channel_id=1, source_target_pairs={{0,28},{4,0},{8,4},{12,8},{16,12},{20,16},{24,20},{28,24},{1,29},{... | collective-permute-start | bytes 1544 | tf_op jit(solution)/shard_map/ppermute | solution.py:22
  279.0 21.2 %collective-permute-start.33 = (f32[1,128]{1,0:T(1,128)S(1)}, f32[1,128]{1,0:T(1,128)S(1)}, u32[]{:S(2)}, u32[]{:S(2)}) collective-permute-start(f32[1,128]{1,0:T(1,128)S(1)} %get-tuple-element.112), channel_id=1, source_target_pairs={{0,3},{1,0},{2,1},{3,2},{4,7},{5,4},{6,5},{7,6},{8,11},{9,8},{10,9... | collective-permute-start | bytes 1544 | tf_op jit(solution)/shard_map/ppermute | solution.py:22
  280.2 20.0 %collective-permute-start.25 = (f32[1,128]{1,0:T(1,128)S(1)}, f32[1,128]{1,0:T(1,128)S(1)}, u32[]{:S(2)}, u32[]{:S(2)}) collective-permute-start(f32[1,128]{1,0:T(1,128)S(1)} %collective-permute-done.24), channel_id=1, source_target_pairs={{0,1},{1,2},{2,3},{3,0},{4,5},{5,6},{6,7},{7,4},{8,9},{9,10},{10,1... | collective-permute-start | bytes 1544 | tf_op jit(solution)/shard_map/ppermute | solution.py:22
  280.2 20.0 %collective-permute-start.28 = (f32[1,128]{1,0:T(1,128)S(1)}, f32[1,128]{1,0:T(1,128)S(1)}, u32[]{:S(2)}, u32[]{:S(2)}) collective-permute-start(f32[1,128]{1,0:T(1,128)S(1)} %collective-permute-done.27), channel_id=1, source_target_pairs={{0,1},{1,2},{2,3},{3,0},{4,5},{5,6},{6,7},{7,4},{8,9},{9,10},{10,1... | collective-permute-start | bytes 1544 | tf_op jit(solution)/shard_map/ppermute | solution.py:22
  281.4 18.9 %collective-permute-start.32 = (f32[1,128]{1,0:T(1,128)S(1)}, f32[1,128]{1,0:T(1,128)S(1)}, u32[]{:S(2)}, u32[]{:S(2)}) collective-permute-start(f32[1,128]{1,0:T(1,128)S(1)} %collective-permute-done.31), channel_id=1, source_target_pairs={{0,3},{1,0},{2,1},{3,2},{4,7},{5,4},{6,5},{7,6},{8,11},{9,8},{10,9... | collective-permute-start | bytes 1544 | tf_op jit(solution)/shard_map/ppermute | solution.py:22
  282.0 18.2 %collective-permute-start.35 = (f32[1,128]{1,0:T(1,128)S(1)}, f32[1,128]{1,0:T(1,128)S(1)}, u32[]{:S(2)}, u32[]{:S(2)}) collective-permute-start(f32[1,128]{1,0:T(1,128)S(1)} %collective-permute-done.34), channel_id=1, source_target_pairs={{0,3},{1,0},{2,1},{3,2},{4,7},{5,4},{6,5},{7,6},{8,11},{9,8},{10,9... | collective-permute-start | bytes 1544 | tf_op jit(solution)/shard_map/ppermute | solution.py:22
  (36 other events, 310.1 us)
where the time goes:
time: 314 us
  waiting for transfers between devices  119 us (38%)
  other arithmetic  75.3 us (24%)
  starting transfers between devices  59 us (19%)
  local copies, waits for them, and re-layouts  53 us (17%)
  matrix products  6.2 us (2%)
    ppermute x12, waiting for transfers between devices, with_halo(): lax.ppermute(lax.slice_in_dim(block, 0, width, axis=dim), axis, backward)  91.2 us
    ppermute x24, starting transfers between devices, from_behind(): return lax.ppermute(value, axis, pairs)  35.6 us
    add x16, other arithmetic, sweep_cells(): return reward + GAMMA * living * highest  26 us
    ppermute x12, waiting for transfers between devices, with_halo(): lax.ppermute(lax.slice_in_dim(block, block.shape[dim] - width, None, axis...  23.5 us
    scatter-add x1, other arithmetic, on_device(): jnp.zeros((cell_count + 1,), jnp.float32).at[landing].add(1.0)[:cell_count]  18 us
    gather x1, local copies, waits for them, and re-layouts, on_device(): own_value = flat_values[agent_task, jnp.clip(owner_cell, 0, cell_count - 1)]  17.7 us
    ppermute x12, starting transfers between devices, with_halo(): lax.ppermute(lax.slice_in_dim(block, 0, width, axis=dim), axis, backward)  13.3 us
    gather x1, local copies, waits for them, and re-layouts, on_device(): far_value = back_table[heading, jnp.minimum(ranking, CAP - 1)]  13.1 us
  transfers between devices with their start and end apart: 48, of which 16 were waited for; matrix products, arithmetic and copies ran while one was open for 18% of the time, Pallas kernels for 0%

commit v1 on v0

v1 whole, which is shorter than its diff:
```python
import jax
import jax.numpy as jnp
from jax import lax
from jax.experimental import pallas as pl
from jax.experimental.pallas import tpu as pltpu
from jax.sharding import PartitionSpec as P


SWEEPS = 16
TERMINAL = 2
GAMMA = 0.95
PENALTY = 0.5
LANES = 128
SUB = 8


class Plan:
    def __init__(self, rows, cols, agents, steps, tasks, codes):
        self.rows, self.cols, self.agents = rows, cols, agents
        self.steps, self.tasks, self.codes = steps, tasks, codes
        self.near = steps
        self.wide = steps + SWEEPS
        self.ring = rows + 2 * self.wide
        self.tiles = cols // LANES + 1
        self.span = self.ring // SUB
        self.step = LANES - 2 * SWEEPS
        self.sweep_tiles = -(-(cols + 2 * self.near) // self.step)
        self.code_bits = (codes - 1).bit_length()
        self.across_rows = rows + 2 * self.near
        self.band = self.wide + self.near
        self.down_rows = self.tiles * self.band + (self.tiles - 1) * self.wide
        assert cols % LANES == 0 and rows % SUB == 0 and agents % LANES == 0
        assert 4 * self.wide <= LANES and self.near % SUB == 0 and self.wide % SUB == 0
        assert self.ring % SUB == 0 and codes <= LANES
        self.magic = -(-(1 << 16) // self.span)
        assert all((r * self.magic) >> 16 == r // self.span for r in range(self.ring))

    def start(self, j):
        return j * self.step - self.wide


def lane_of(shape):
    return lax.broadcasted_iota(jnp.int32, shape, len(shape) - 1)


def split_cell(cell, cols):
    if cols & (cols - 1) == 0:
        return cell >> (cols.bit_length() - 1), cell & (cols - 1)
    return lax.div(cell, cols), lax.rem(cell, cols)


def count_kernel(plan, act, start, task, code, hist, right, left, address, lane_out, row_hot, col_hot):
    p = plan
    ring_cols = p.tiles * LANES
    row_id = lax.broadcasted_iota(jnp.int32, (p.ring, LANES), 0)
    col_id = lax.broadcasted_iota(jnp.int32, (ring_cols, LANES), 0)
    for i in range(p.agents // LANES):
        here = slice(i * LANES, (i + 1) * LANES)
        a = act[:, here]
        one = lambda c: jnp.where(a == c, 1, 0)
        row_moves = jnp.sum(one(2) - one(1), axis=0, keepdims=True)
        col_moves = jnp.sum(one(4) - one(3), axis=0, keepdims=True)
        row, col = split_cell(start[i : i + 1, :], p.cols)
        row = row + row_moves
        col = col + col_moves
        ring_row = jnp.where(row < 0, row + p.ring, row)
        ring_col = jnp.where(col < 0, col + ring_cols, col)
        row_hot[:, here] = jnp.where(row_id == ring_row, 1.0, 0.0).astype(jnp.bfloat16)
        col_hot[:, here] = jnp.where(col_id == ring_col, 1.0, 0.0).astype(jnp.bfloat16)
        inner = col + p.near
        j = jnp.zeros_like(inner)
        for edge in range(1, p.sweep_tiles):
            j = j + jnp.where(inner >= edge * p.step, 1, 0)
        lane_out[i : i + 1, :] = inner - j * p.step + (p.wide - p.near)
        sub = (ring_row * p.magic) >> 16
        address[i : i + 1, :] = (
            (j * p.tasks + task[i : i + 1, :]) * p.ring + (ring_row - sub * p.span) * SUB + sub
        )
    counts = lax.dot_general(
        row_hot[...], col_hot[...], (((1,), (1,)), ((), ())), preferred_element_type=jnp.float32
    )
    for t in range(p.tiles):
        hist[t] = counts[:, t * LANES : (t + 1) * LANES]
    last = p.tiles - 1
    for dst, src, n in ((0, 0, p.rows), (p.rows, p.rows, p.near), (p.rows + p.near, p.ring - p.near, p.near)):
        lane = lane_of((n, LANES))
        at = pl.ds(src, n)
        to_right = jnp.where(lane < p.near, hist[last, at, :], hist[last - 1, at, :])
        to_left = jnp.where(lane < p.wide, hist[0, at, :], hist[last, at, :])
        if src == 0:
            low = code[:, :LANES].astype(jnp.float32)
            high = code[:, (last - 1) * LANES :].astype(jnp.float32)
            inside = (lane >= LANES - 2 * p.wide) & (lane < LANES - p.wide)
            to_right = jnp.where(inside, pltpu.roll(high, LANES - p.wide, 1), to_right)
            inside = (lane >= p.wide) & (lane < 2 * p.wide)
            to_left = jnp.where(inside, pltpu.roll(low, p.wide, 1), to_left)
        right[pl.ds(dst, n), :] = to_right
        left[pl.ds(dst, n), :] = to_left


def across_kernel(plan, hist, code, from_left, from_right, key, first, second, cnt, cds):
    p = plan
    last = p.tiles - 1
    for dst, src, n in ((0, 0, p.rows + p.near), (p.ring - p.near, p.rows + p.near, p.near)):
        lane = lane_of((n, LANES))
        at = pl.ds(dst, n)
        l = from_left[pl.ds(src, n), :]
        r = from_right[pl.ds(src, n), :]
        for t in range(p.tiles):
            h = hist[t, at, :]
            if t == 0:
                h = h + jnp.where(lane < p.near, l, 0.0)
            if t == last - 1:
                h = h + jnp.where(lane >= LANES - p.near, r, 0.0)
            if t == last:
                h = h + jnp.where(lane >= LANES - p.wide, l, jnp.where(lane < p.wide, r, 0.0))
            cnt[t, at, :] = h
    own = pl.ds(0, p.rows)
    lane = lane_of((p.rows, LANES))
    l = pltpu.roll(from_left[own, :], p.wide, 1)
    r = pltpu.roll(from_right[own, :], LANES - p.wide, 1)
    for t in range(last):
        cds[t] = code[:, t * LANES : (t + 1) * LANES].astype(jnp.float32)
    cds[last] = jnp.where(lane >= LANES - p.wide, l, jnp.where(lane < p.wide, r, 0.0))
    for t in range(p.tiles):
        key[t, own, :] = (cnt[t, own, :].astype(jnp.int32) << p.code_bits) + cds[t].astype(jnp.int32)
        for lo, n in ((p.rows, p.near), (p.ring - p.near, p.near)):
            at = pl.ds(lo, n)
            key[t, at, :] = cnt[t, at, :].astype(jnp.int32) << p.code_bits

    def write(down, up):
        lane = lane_of((p.wide, LANES))
        inside = (lane >= p.wide) & (lane < LANES - p.wide)
        for t in range(p.tiles):
            base = t * p.band
            down[pl.ds(base, p.band), :] = cnt[t, pl.ds(p.rows - p.wide, p.band), :]
            up[pl.ds(base, p.near), :] = cnt[t, pl.ds(p.ring - p.near, p.near), :]
            up[pl.ds(base + p.near, p.wide), :] = cnt[t, pl.ds(0, p.wide), :]
            low = cds[t, pl.ds(0, p.wide), :]
            high = cds[t, pl.ds(p.rows - p.wide, p.wide), :]
            if t < last:
                base = p.tiles * p.band + t * p.wide
                down[pl.ds(base, p.wide), :] = high
                up[pl.ds(base, p.wide), :] = low
            else:
                half = LANES // 2
                at = pl.ds(base, p.wide)
                down[at, :] = jnp.where(inside, pltpu.roll(high, half, 1), down[at, :])
                at = pl.ds(base + p.near, p.wide)
                up[at, :] = jnp.where(inside, pltpu.roll(low, half, 1), up[at, :])

    odd = lax.axis_index("gy") % 2 == 1

    @pl.when(odd)
    def _():
        write(second, first)

    @pl.when(jnp.logical_not(odd))
    def _():
        write(first, second)


def sweep_kernel(plan, table, key, first, second, address, lane_in, values, answers,
                 ring, tiles, reward, gain, value, natural, rows_of, sems):
    p = plan
    last = p.tiles - 1
    odd = lax.axis_index("gy") % 2 == 1
    half = LANES // 2

    def above(at, n):
        at = pl.ds(at, n)
        return jnp.where(odd, first[at, :], second[at, :]).astype(jnp.int32)

    def below(at, n):
        at = pl.ds(at, n)
        return jnp.where(odd, second[at, :], first[at, :]).astype(jnp.int32)

    w, s, bits = p.wide, p.near, p.code_bits
    for t in range(p.tiles):
        base = t * p.band
        code_base = p.tiles * p.band + t * w
        up_cnt = above(base, p.band) << bits
        low_cnt = below(base, p.band) << bits
        if t < last:
            up_code = above(code_base, w)
            low_code = below(code_base, w)
        else:
            up_code = pltpu.roll(above(base, w), half, 1)
            low_code = pltpu.roll(below(base + s, w), half, 1)
        own = lambda lo, n: key[t, pl.ds(lo, n), :]

        def put(lo, n, x):
            ring[t, pl.ds(lo, n), :] = x

        put(0, s, own(0, s) + up_cnt[w:])
        put(s, p.rows - 2 * s, own(s, p.rows - 2 * s))
        put(p.rows - s, s, own(p.rows - s, s) + low_cnt[:s])
        put(p.rows, s, own(p.rows, s) + low_cnt[s : 2 * s] + low_code[:s])
        put(p.rows + s, w - s, low_cnt[2 * s :] + low_code[s:])
        put(p.ring - w, w - s, up_cnt[: w - s] + up_code[: w - s])
        put(p.ring - s, s, own(p.ring - s, s) + up_cnt[w - s : w] + up_code[w - s :])

    lane = lane_of((p.ring, LANES))
    for j in range(p.sweep_tiles):
        at = p.start(j) % (p.tiles * LANES)
        a, off = at // LANES, at % LANES
        x = ring[a]
        if off:
            x = pltpu.roll(jnp.where(lane >= off, x, ring[(a + 1) % p.tiles]), LANES - off, 1)
        tiles[j] = x

    looks = [jnp.broadcast_to(table[t : t + 1, :], (SUB, LANES)) for t in range(p.tasks)]
    for j in range(p.sweep_tiles):
        for k in range(p.span):
            x = tiles[j, pl.ds(k, SUB, stride=p.span), :]
            code = x & ((1 << bits) - 1)
            crowd = PENALTY * (x >> bits).astype(jnp.float32)
            at = pl.ds(k * SUB, SUB)
            gain[j, at, :] = jnp.where(code < p.codes - TERMINAL, GAMMA, 0.0)
            for t in range(p.tasks):
                r = jnp.take_along_axis(looks[t], code, axis=1, mode="promise_in_bounds") - crowd
                reward[j * p.tasks + t, at, :] = r
                value[pl.ds((j * p.tasks + t) * p.ring + k * SUB, SUB), :] = r

    def sweep(_, carry):
        for j in range(p.sweep_tiles):
            base = [(j * p.tasks + t) * p.ring for t in range(p.tasks)]
            load = lambda t, k: value[pl.ds(base[t] + k * SUB, SUB), :]
            first_row = [load(t, 0) for t in range(p.tasks)]
            before = [pltpu.roll(load(t, p.span - 1), 1, 0) for t in range(p.tasks)]
            now = list(first_row)
            for k in range(p.span):
                g = gain[j, pl.ds(k * SUB, SUB), :]
                for t in range(p.tasks):
                    after = load(t, k + 1) if k + 1 < p.span else pltpu.roll(first_row[t], SUB - 1, 0)
                    side = jnp.maximum(pltpu.roll(now[t], 1, 1), pltpu.roll(now[t], LANES - 1, 1))
                    best = jnp.maximum(jnp.maximum(before[t], after), side)
                    new = reward[j * p.tasks + t, pl.ds(k * SUB, SUB), :] + g * best
                    value[pl.ds(base[t] + k * SUB, SUB), :] = new
                    before[t], now[t] = now[t], after
        return carry

    lax.fori_loop(0, SWEEPS, sweep, 0)

    lane = lane_of((SUB, LANES))
    copies = []
    for t in range(p.tasks):
        for c in range(last):
            for k in range(p.span):
                out = None
                for j in range(p.sweep_tiles):
                    lo = p.start(j) + SWEEPS - c * LANES
                    hi = lo + p.step
                    if hi <= 0 or lo >= LANES:
                        continue
                    x = value[pl.ds((j * p.tasks + t) * p.ring + k * SUB, SUB), :]
                    x = pltpu.roll(x, (p.start(j) - c * LANES) % LANES, 1)
                    out = x if out is None else jnp.where(lane >= lo, x, out)
                natural[t * last + c, pl.ds(k, SUB, stride=p.span), :] = out
            copy = pltpu.make_async_copy(
                natural.at[t * last + c, pl.ds(0, p.rows), :],
                values.at[t, :, pl.ds(c * LANES, LANES)],
                sems.at[t * last + c],
            )
            copy.start()
            copies.append(copy)

    def fetch(i, carry):
        for l in range(LANES):
            rows_of[pl.ds(i * LANES + l, 1), :] = value[pl.ds(address[i, l], 1), :]
        return carry

    lax.fori_loop(0, p.agents // LANES, fetch, 0)
    lane_id = lax.broadcasted_iota(jnp.int32, (LANES, LANES), 0)
    for i in range(p.agents // LANES):
        turned = jnp.transpose(rows_of[pl.ds(i * LANES, LANES), :])
        picked = jnp.where(lane_id == lane_in[i : i + 1, :], turned, 0.0)
        answers[i : i + 1, :] = jnp.sum(picked, axis=0, keepdims=True)
    for copy in copies:
        copy.wait()


def shift(value, axis, steps):
    count = lax.axis_size(axis)
    return lax.ppermute(value, axis, [(i, (i + steps) % count) for i in range(count)])


def swap(value, axis, parity):
    count = lax.axis_size(axis)
    assert count % 2 == 0
    return lax.ppermute(
        value, axis, [(i, (i + (1 if i % 2 == parity else -1)) % count) for i in range(count)]
    )


def on_device(map_codes, reward_table, start_cell, agent_task, actions):
    rows, cols = map_codes.shape
    tasks, codes = reward_table.shape
    steps, agents = actions.shape
    p = Plan(rows, cols, agents, steps, tasks, codes)
    vmem = pl.BlockSpec(memory_space=pltpu.VMEM)
    smem = pl.BlockSpec(memory_space=pltpu.SMEM)
    f32, i32 = jnp.float32, jnp.int32
    shape = jax.ShapeDtypeStruct
    by_lane = (agents // LANES, LANES)

    def bind(kernel):
        def body(*refs):
            kernel(p, *refs)

        return body

    table = jnp.pad(reward_table, ((0, 0), (0, LANES - codes)))
    hist, to_right, to_left, address, lane = pl.pallas_call(
        bind(count_kernel),
        in_specs=[vmem] * 4,
        out_specs=[vmem] * 5,
        out_shape=[
            shape((p.tiles, p.ring, LANES), f32),
            shape((p.across_rows, LANES), f32),
            shape((p.across_rows, LANES), f32),
            shape(by_lane, i32),
            shape(by_lane, i32),
        ],
        scratch_shapes=[
            pltpu.VMEM((p.ring, agents), jnp.bfloat16),
            pltpu.VMEM((p.tiles * LANES, agents), jnp.bfloat16),
        ],
        name="count",
    )(actions, start_cell.reshape(by_lane), agent_task.reshape(by_lane), map_codes)
    from_left = shift(to_right, "gx", 1)
    from_right = shift(to_left, "gx", -1)
    key, first, second = pl.pallas_call(
        bind(across_kernel),
        in_specs=[vmem] * 4,
        out_specs=[vmem] * 3,
        out_shape=[
            shape((p.tiles, p.ring, LANES), i32),
            shape((p.down_rows, LANES), f32),
            shape((p.down_rows, LANES), f32),
        ],
        scratch_shapes=[
            pltpu.VMEM((p.tiles, p.ring, LANES), f32),
            pltpu.VMEM((p.tiles, p.rows, LANES), f32),
        ],
        name="across",
    )(hist, map_codes, from_left, from_right)
    first = swap(first, "gy", 0)
    second = swap(second, "gy", 1)
    blocks = p.sweep_tiles * tasks
    outs = tasks * (p.tiles - 1)
    values, answers = pl.pallas_call(
        bind(sweep_kernel),
        in_specs=[vmem, vmem, vmem, vmem, smem, vmem],
        out_specs=[pl.BlockSpec(memory_space=pl.ANY), vmem],
        out_shape=[shape((tasks, rows, cols), f32), shape(by_lane, f32)],
        scratch_shapes=[
            pltpu.VMEM((p.tiles, p.ring, LANES), i32),
            pltpu.VMEM((p.sweep_tiles, p.ring, LANES), i32),
            pltpu.VMEM((blocks, p.ring, LANES), f32),
            pltpu.VMEM((p.sweep_tiles, p.ring, LANES), f32),
            pltpu.VMEM((blocks * p.ring, LANES), f32),
            pltpu.VMEM((outs, p.ring, LANES), f32),
            pltpu.VMEM((agents, LANES), f32),
            pltpu.SemaphoreType.DMA((outs,)),
        ],
        name="sweep",
    )(table, key, first, second, address, lane)
    return values, answers.reshape(agents)


def solution(mesh):
    placed = (P("gy", "gx"), P(), P(("gx", "gy")), P(("gx", "gy")), P(None, ("gx", "gy")))
    return jax.shard_map(
        on_device,
        mesh=mesh,
        in_specs=placed,
        out_specs=(P(None, "gy", "gx"), P(("gx", "gy"))),
        check_vma=False,
    )
```

time: 314 us -> 47.3 us (0.15)
  waiting for transfers between devices: 119 us -> 8.3 us
  other arithmetic: 75.3 us -> 0 us
  starting transfers between devices: 59 us -> 7.64 us
  local copies, waits for them, and re-layouts: 53 us -> 1.91 us
  Pallas kernels: 0 us -> 28.6 us
  matrix products: 6.2 us -> 0 us
    ppermute x48 -> x4, waiting for transfers between devices: 119 us -> 8.3 us  [the longest x2 5.63 us: shift(): lax.ppermute(value, axis, [(i, (i + steps) % count) for i in range(count)])]
    ppermute x48 -> x4, starting transfers between devices: 59 us -> 7.64 us  [the longest x2 6 us: shift(): lax.ppermute(value, axis, [(i, (i + steps) % count) for i in range(count)])]
    gather x3 -> x0, local copies, waits for them, and re-layouts: 39.9 us -> none  [the longest x1 17.7 us: on_device(): own_value = flat_values[agent_task, jnp.clip(owner_cell, 0, cell_count - 1)]]
    pallas_call x0 -> x3, Pallas kernels: none -> 28.6 us  [the longest x1 23 us: on_device(): pl.pallas_call(bind(sweep_kernel), in_specs=[vmem, vmem, vmem, vmem, smem...]
    add x16 -> x0, other arithmetic: 26 us -> none  [sweep_cells(): return reward + GAMMA * living * highest]
    scatter-add x1 -> x0, other arithmetic: 18 us -> none  [on_device(): jnp.zeros((cell_count + 1,), jnp.float32).at[landing].add(1.0)[:cell_count]]
    mul x17 -> x0, other arithmetic: 11.1 us -> none  [the longest x16 11.1 us: sweep_cells(): return reward + GAMMA * living * highest]
    concatenate x9 -> x0, other arithmetic: 9.1 us -> none  [the longest x6 8.28 us: with_halo(): block = jnp.concatenate([low, block, high], axis=dim)]
  transfers between devices with their start and end apart: 48 -> 4, of which waited for: 16 -> 3; matrix products, arithmetic and copies ran while one was open for 18% -> 1% of each run, Pallas kernels for 0% -> 0%
where the time goes in v1:
time: 47.3 us; the launch traced here: 47.1 us
  Pallas kernels  28.6 us (60%)
  waiting for transfers between devices  8.3 us (18%)
  starting transfers between devices  7.64 us (16%)
  local copies, waits for them, and re-layouts  1.91 us (4%)
  between operations  0.64 us (1%)
    pallas_call x1, Pallas kernels, on_device(): pl.pallas_call(bind(sweep_kernel), in_specs=[vmem, vmem, vmem, vmem, smem...  23 us
    ppermute x2, starting transfers between devices, shift(): lax.ppermute(value, axis, [(i, (i + steps) % count) for i in range(count)])  6 us
    ppermute x2, waiting for transfers between devices, shift(): lax.ppermute(value, axis, [(i, (i + steps) % count) for i in range(count)])  5.63 us
    pallas_call x1, Pallas kernels, on_device(): pl.pallas_call(bind(count_kernel), in_specs=[vmem] * 4, out_specs=[vmem]...  3.33 us
    ppermute x2, waiting for transfers between devices, swap(): lax.ppermute(value, axis, [(i, (i + (1 if i % 2 == parity else -1)) % cou...  2.67 us
    pallas_call x1, Pallas kernels, on_device(): pl.pallas_call(bind(across_kernel), in_specs=[vmem] * 4, out_specs=[vmem]...  2.28 us
    ppermute x2, starting transfers between devices, swap(): lax.ppermute(value, axis, [(i, (i + (1 if i % 2 == parity else -1)) % cou...  1.63 us
    unnamed x10, local copies, waits for them, and re-layouts  1.32 us
  transfers between devices with their start and end apart: 4, of which 3 were waited for; matrix products, arithmetic and copies ran while one was open for 1% of the time, Pallas kernels for 0%

profile of v1, /device:TPU:0, one launch (start us, length us, event | category | flops | bytes accessed | tf_op | source)
XLA Modules:
  0.0 47.1 jit_solution(8315158373464779090)
XLA Ops:
  0.6 3.3 %count.1 = (f32[3,320,128]{2,1,0:T(8,128)}, f32[288,128]{1,0:T(8,128)}, f32[288,128]{1,0:T(8,128)}, s32[16,128]{1,0:T(8,128)}, s32[16,128]{1,0:T(8,128)}) custom-call(s32[16,2048]{1,0:T(8,128)} %refs_0_.1, s32[16,128]{1,0:T(8,128)} %bitcast.3, s32[16,128]{1,0:T(8,128)} %bitcast.4, s32[256,256]{1,0:T(8,128)} %refs_1_.1), custom_call_target="tpu_custom_call" | custom-call | tf_op jit(solution)/shard_map/count/pallas_call | solution.py:314
  4.0 3.0 %collective-permute-start = (f32[288,128]{1,0:T(8,128)}, f32[288,128]{1,0:T(8,128)S(1)}, u32[]{:S(2)}, u32[]{:S(2)}) collective-permute-start(f32[288,128]{1,0:T(8,128)} %get-tuple-element.13), channel_id=1, source_target_pairs={{0,4},{4,8},{8,12},{12,16},{16,20},{20,24},{24,28},{28,0},{1,5},{5... | collective-permute-start | bytes 442376 | tf_op jit(solution)/shard_map/ppermute | solution.py:285
  6.9 3.0 %collective-permute-start.1 = (f32[288,128]{1,0:T(8,128)}, f32[288,128]{1,0:T(8,128)S(1)}, u32[]{:S(2)}, u32[]{:S(2)}) collective-permute-start(f32[288,128]{1,0:T(8,128)} %get-tuple-element.14), channel_id=1, source_target_pairs={{0,28},{4,0},{8,4},{12,8},{16,12},{20,16},{24,20},{28,24},{1,29},{... | collective-permute-start | bytes 442376 | tf_op jit(solution)/shard_map/ppermute | solution.py:285
  10.0 4.2 %collective-permute-done.refs_2_ = f32[288,128]{1,0:T(8,128)S(1)} collective-permute-done((f32[288,128]{1,0:T(8,128)}, f32[288,128]{1,0:T(8,128)S(1)}, u32[]{:S(2)}, u32[]{:S(2)}) %collective-permute-start) | collective-permute-done | bytes 147488 | tf_op jit(solution)/shard_map/ppermute | solution.py:285
  14.1 0.0 copy-start
  14.1 1.5 %collective-permute-done.1.refs_3_ = f32[288,128]{1,0:T(8,128)S(1)} collective-permute-done((f32[288,128]{1,0:T(8,128)}, f32[288,128]{1,0:T(8,128)S(1)}, u32[]{:S(2)}, u32[]{:S(2)}) %collective-permute-start.1) | collective-permute-done | bytes 147488 | tf_op jit(solution)/shard_map/ppermute | solution.py:285
  15.6 0.0 copy-start.1
  15.6 0.0 copy-done
  15.6 0.7 %copy-done.1 = f32[288,128]{1,0:T(8,128)} copy-done((f32[288,128]{1,0:T(8,128)}, f32[288,128]{1,0:T(8,128)S(1)}, u32[]{:S(2)}) %copy-start.1) | copy-done | bytes 147480
  16.3 2.3 %across.1 = (s32[3,320,128]{2,1,0:T(8,128)}, f32[208,128]{1,0:T(8,128)}, f32[208,128]{1,0:T(8,128)}) custom-call(f32[3,320,128]{2,1,0:T(8,128)} %get-tuple-element.12.refs_0_, s32[256,256]{1,0:T(8,128)} %refs_1_.1, f32[288,128]{1,0:T(8,128)} %copy-done, f32[288,128]{1,0:T(8,128)} %copy-done.1), custom_call_target="tpu_custom_call" | custom-call | tf_op jit(solution)/shard_map/across/pallas_call | solution.py:333
  18.5 0.0 copy-start.4
  18.5 0.0 collective-permute-start.2
  18.6 1.6 %collective-permute-start.3 = (f32[208,128]{1,0:T(8,128)}, f32[208,128]{1,0:T(8,128)S(1)}, u32[]{:S(2)}, u32[]{:S(2)}) collective-permute-start(f32[208,128]{1,0:T(8,128)} %get-tuple-element.17), channel_id=1, source_target_pairs={{0,3},{1,2},{2,1},{3,0},{4,7},{5,6},{6,5},{7,4},{8,11},{9,10},{10,... | collective-permute-start | bytes 319496 | tf_op jit(solution)/shard_map/ppermute | solution.py:291
  20.2 0.0 copy-done.4
  20.2 0.6 %pad.4.refs_0_ = f32[4,128]{1,0:T(4,128)} pad(f32[4,64]{1,0:T(4,128)S(1)} %copy-done.4, f32[]{:T(128)} %constant.2.clone.1), padding=0_0x0_64 | pad | bytes 3076 | tf_op jit(solution)/shard_map/jit(_pad)/pad | solution.py:313
  20.8 0.0 collective-permute-done.2.refs_2_
  20.8 0.0 copy-start.2
  20.8 2.7 %collective-permute-done.3.refs_3_ = f32[208,128]{1,0:T(8,128)S(1)} collective-permute-done((f32[208,128]{1,0:T(8,128)}, f32[208,128]{1,0:T(8,128)S(1)}, u32[]{:S(2)}, u32[]{:S(2)}) %collective-permute-start.3) | collective-permute-done | bytes 106528 | tf_op jit(solution)/shard_map/ppermute | solution.py:291
  23.4 0.0 copy-start.3
  23.4 0.0 copy-done.2
  23.5 0.6 %copy-done.3 = f32[208,128]{1,0:T(8,128)} copy-done((f32[208,128]{1,0:T(8,128)}, f32[208,128]{1,0:T(8,128)S(1)}, u32[]{:S(2)}) %copy-start.3) | copy-done | bytes 106520
  24.1 23.0 %sweep.1 = (f32[4,256,256]{2,1,0:T(8,128)}, f32[16,128]{1,0:T(8,128)}) custom-call(f32[4,128]{1,0:T(4,128)} %pad.4.refs_0_, s32[3,320,128]{2,1,0:T(8,128)} %get-tuple-element.15.refs_1_, f32[208,128]{1,0:T(8,128)} %copy-done.2, f32[208,128]{1,0:T(8,128)} %copy-done.3, s32[16,128]{1,0:T(8,128)} %get-tuple-element.18.refs_4_, s32[16,128]{1,0:T(8,128)} %get-tuple-element.19.refs_5_), custom_call_target="tpu_custom_call" | custom-call | tf_op jit(solution)/shard_map/sweep/pallas_call | solution.py:352
Async XLA Ops:
  4.0 10.2 %collective-permute-start = (f32[288,128]{1,0:T(8,128)}, f32[288,128]{1,0:T(8,128)S(1)}, u32[]{:S(2)}, u32[]{:S(2)}) collective-permute-start(f32[288,128]{1,0:T(8,128)} %get-tuple-element.13), channel_id=1, source_target_pairs={{0,4},{4,8},{8,12},{12,16},{16,20},{20,24},{24,28},{28,0},{1,5},{5... | collective-permute-start | bytes 442376 | tf_op jit(solution)/shard_map/ppermute | solution.py:285
  6.9 8.7 %collective-permute-start.1 = (f32[288,128]{1,0:T(8,128)}, f32[288,128]{1,0:T(8,128)S(1)}, u32[]{:S(2)}, u32[]{:S(2)}) collective-permute-start(f32[288,128]{1,0:T(8,128)} %get-tuple-element.14), channel_id=1, source_target_pairs={{0,28},{4,0},{8,4},{12,8},{16,12},{20,16},{24,20},{28,24},{1,29},{... | collective-permute-start | bytes 442376 | tf_op jit(solution)/shard_map/ppermute | solution.py:285
  14.1 1.5 %copy-start = (f32[288,128]{1,0:T(8,128)}, f32[288,128]{1,0:T(8,128)S(1)}, u32[]{:S(2)}) copy-start(f32[288,128]{1,0:T(8,128)S(1)} %collective-permute-done.refs_2_) | copy-start | bytes 442372
  15.6 0.7 %copy-start.1 = (f32[288,128]{1,0:T(8,128)}, f32[288,128]{1,0:T(8,128)S(1)}, u32[]{:S(2)}) copy-start(f32[288,128]{1,0:T(8,128)S(1)} %collective-permute-done.1.refs_3_) | copy-start | bytes 442372
  18.5 1.6 %copy-start.4 = (f32[4,64]{1,0:T(4,128)S(1)}, f32[4,64]{1,0:T(4,128)}, u32[]{:S(2)}) copy-start(f32[4,64]{1,0:T(4,128)} %param.6) | copy-start | bytes 3076
  18.5 2.2 %collective-permute-start.2 = (f32[208,128]{1,0:T(8,128)}, f32[208,128]{1,0:T(8,128)S(1)}, u32[]{:S(2)}, u32[]{:S(2)}) collective-permute-start(f32[208,128]{1,0:T(8,128)} %get-tuple-element.16), channel_id=1, source_target_pairs={{0,1},{1,0},{2,3},{3,2},{4,5},{5,4},{6,7},{7,6},{8,9},{9,8},{10,11... | collective-permute-start | bytes 319496 | tf_op jit(solution)/shard_map/ppermute | solution.py:291
  18.6 4.9 %collective-permute-start.3 = (f32[208,128]{1,0:T(8,128)}, f32[208,128]{1,0:T(8,128)S(1)}, u32[]{:S(2)}, u32[]{:S(2)}) collective-permute-start(f32[208,128]{1,0:T(8,128)} %get-tuple-element.17), channel_id=1, source_target_pairs={{0,3},{1,2},{2,1},{3,0},{4,7},{5,6},{6,5},{7,4},{8,11},{9,10},{10,... | collective-permute-start | bytes 319496 | tf_op jit(solution)/shard_map/ppermute | solution.py:291
  20.8 2.7 %copy-start.2 = (f32[208,128]{1,0:T(8,128)}, f32[208,128]{1,0:T(8,128)S(1)}, u32[]{:S(2)}) copy-start(f32[208,128]{1,0:T(8,128)S(1)} %collective-permute-done.2.refs_2_) | copy-start | bytes 319492
  23.4 0.6 %copy-start.3 = (f32[208,128]{1,0:T(8,128)}, f32[208,128]{1,0:T(8,128)S(1)}, u32[]{:S(2)}) copy-start(f32[208,128]{1,0:T(8,128)S(1)} %collective-permute-done.3.refs_3_) | copy-start | bytes 319492

commit v2 on v1

--- a/solution.py
+++ b/solution.py
@@ -161,7 +161,7 @@
 
 
 def sweep_kernel(plan, table, key, first, second, address, lane_in, values, answers,
-                 ring, tiles, reward, gain, value, natural, rows_of, sems):
+                 looked, ring, tiles, reward, gain, value, natural, rows_of, sems):
     p = plan
     last = p.tiles - 1
     odd = lax.axis_index("gy") % 2 == 1
@@ -209,7 +209,8 @@
             x = pltpu.roll(jnp.where(lane >= off, x, ring[(a + 1) % p.tiles]), LANES - off, 1)
         tiles[j] = x
 
-    looks = [jnp.broadcast_to(table[t : t + 1, :], (SUB, LANES)) for t in range(p.tasks)]
+    looked[pl.ds(0, p.tasks), pl.ds(0, p.codes)] = table[...]
+    looks = [jnp.broadcast_to(looked[t : t + 1, :], (SUB, LANES)) for t in range(p.tasks)]
     for j in range(p.sweep_tiles):
         for k in range(p.span):
             x = tiles[j, pl.ds(k, SUB, stride=p.span), :]
@@ -302,6 +303,8 @@
     smem = pl.BlockSpec(memory_space=pltpu.SMEM)
     f32, i32 = jnp.float32, jnp.int32
     shape = jax.ShapeDtypeStruct
+    fast = lambda dims, dtype: pltpu.VMEM(dims, dtype)
+    near = lambda x: pltpu.with_memory_space_constraint(x, pltpu.VMEM)
     by_lane = (agents // LANES, LANES)
 
     def bind(kernel):
@@ -310,17 +313,16 @@
 
         return body
 
-    table = jnp.pad(reward_table, ((0, 0), (0, LANES - codes)))
     hist, to_right, to_left, address, lane = pl.pallas_call(
         bind(count_kernel),
         in_specs=[vmem] * 4,
         out_specs=[vmem] * 5,
         out_shape=[
-            shape((p.tiles, p.ring, LANES), f32),
-            shape((p.across_rows, LANES), f32),
-            shape((p.across_rows, LANES), f32),
+            fast((p.tiles, p.ring, LANES), f32),
+            fast((p.across_rows, LANES), f32),
+            fast((p.across_rows, LANES), f32),
             shape(by_lane, i32),
-            shape(by_lane, i32),
+            fast(by_lane, i32),
         ],
         scratch_shapes=[
             pltpu.VMEM((p.ring, agents), jnp.bfloat16),
@@ -335,16 +337,16 @@
         in_specs=[vmem] * 4,
         out_specs=[vmem] * 3,
         out_shape=[
-            shape((p.tiles, p.ring, LANES), i32),
-            shape((p.down_rows, LANES), f32),
-            shape((p.down_rows, LANES), f32),
+            fast((p.tiles, p.ring, LANES), i32),
+            fast((p.down_rows, LANES), f32),
+            fast((p.down_rows, LANES), f32),
         ],
         scratch_shapes=[
             pltpu.VMEM((p.tiles, p.ring, LANES), f32),
             pltpu.VMEM((p.tiles, p.rows, LANES), f32),
         ],
         name="across",
-    )(hist, map_codes, from_left, from_right)
+    )(near(hist), map_codes, near(from_left), near(from_right))
     first = swap(first, "gy", 0)
     second = swap(second, "gy", 1)
     blocks = p.sweep_tiles * tasks
@@ -355,6 +357,7 @@
         out_specs=[pl.BlockSpec(memory_space=pl.ANY), vmem],
         out_shape=[shape((tasks, rows, cols), f32), shape(by_lane, f32)],
         scratch_shapes=[
+            pltpu.VMEM((tasks, LANES), f32),
             pltpu.VMEM((p.tiles, p.ring, LANES), i32),
             pltpu.VMEM((p.sweep_tiles, p.ring, LANES), i32),
             pltpu.VMEM((blocks, p.ring, LANES), f32),
@@ -365,7 +368,7 @@
             pltpu.SemaphoreType.DMA((outs,)),
         ],
         name="sweep",
-    )(table, key, first, second, address, lane)
+    )(reward_table, near(key), near(first), near(second), address, near(lane))
     return values, answers.reshape(agents)
 
 

time: 47.3 us -> 44.1 us (0.932)
  local copies, waits for them, and re-layouts: 1.91 us -> 0 us
  Pallas kernels: 28.6 us -> 27 us
    unnamed x10 -> x0, local copies, waits for them, and re-layouts: 1.32 us -> none
    pallas_call x1, Pallas kernels: 2.28 us -> 1.18 us  [on_device(): pl.pallas_call(bind(across_kernel), in_specs=[vmem] * 4, out_specs=[vmem]...]
    pad x1 -> x0, local copies, waits for them, and re-layouts: 0.59 us -> none  [on_device(): table = jnp.pad(reward_table, ((0, 0), (0, LANES - codes)))]
  transfers between devices with their start and end apart: 4 -> 4, of which waited for: 3 -> 3; matrix products, arithmetic and copies ran while one was open for 1% -> 0% of each run, Pallas kernels for 0% -> 0%
where the time goes in v2:
time: 44.1 us; the launch traced here: 43.8 us
  Pallas kernels  27 us (61%)
  waiting for transfers between devices  8.52 us (19%)
  starting transfers between devices  7.66 us (17%)
  between operations  0.64 us (1%)
    pallas_call x1, Pallas kernels, on_device(): pl.pallas_call(bind(sweep_kernel), in_specs=[vmem, vmem, vmem, vmem, smem...  22.8 us
    ppermute x2, starting transfers between devices, shift(): lax.ppermute(value, axis, [(i, (i + steps) % count) for i in range(count)])  6.01 us
    ppermute x2, waiting for transfers between devices, shift(): lax.ppermute(value, axis, [(i, (i + steps) % count) for i in range(count)])  5.42 us
    ppermute x2, waiting for transfers between devices, swap(): lax.ppermute(value, axis, [(i, (i + (1 if i % 2 == parity else -1)) % cou...  3.1 us
    pallas_call x1, Pallas kernels, on_device(): pl.pallas_call(bind(count_kernel), in_specs=[vmem] * 4, out_specs=[vmem]...  3.05 us
    ppermute x2, starting transfers between devices, swap(): lax.ppermute(value, axis, [(i, (i + (1 if i % 2 == parity else -1)) % cou...  1.64 us
    pallas_call x1, Pallas kernels, on_device(): pl.pallas_call(bind(across_kernel), in_specs=[vmem] * 4, out_specs=[vmem]...  1.18 us
  transfers between devices with their start and end apart: 4, of which 3 were waited for; matrix products, arithmetic and copies ran while one was open for 0% of the time, Pallas kernels for 0%

profile of v2, /device:TPU:0, one launch (start us, length us, event | category | flops | bytes accessed | tf_op | source)
XLA Modules:
  0.0 43.8 jit_solution(6949939384323610042)
XLA Ops:
  0.6 3.1 %count.1 = (f32[3,320,128]{2,1,0:T(8,128)S(1)}, f32[288,128]{1,0:T(8,128)S(1)}, f32[288,128]{1,0:T(8,128)S(1)}, s32[16,128]{1,0:T(8,128)}, s32[16,128]{1,0:T(8,128)S(1)}) custom-call(s32[16,2048]{1,0:T(8,128)} %refs_0_.2, s32[16,128]{1,0:T(8,128)} %bitcast.3, s32[16,128]{1,0:T(8,128)} %bitcast.4, s32[256,256]{1,0:T(8,128)} %refs_1_.1), custom_call_target="tpu_custom_call" | custom-call | tf_op jit(solution)/shard_map/count/pallas_call | solution.py:316
  3.7 3.0 %collective-permute-start = (f32[288,128]{1,0:T(8,128)S(1)}, f32[288,128]{1,0:T(8,128)S(1)}, u32[]{:S(2)}, u32[]{:S(2)}) collective-permute-start(f32[288,128]{1,0:T(8,128)S(1)} %get-tuple-element.13), channel_id=1, source_target_pairs={{0,4},{4,8},{8,12},{12,16},{16,20},{20,24},{24,28},{28,0},{1,5},{5... | collective-permute-start | bytes 442376 | tf_op jit(solution)/shard_map/ppermute | solution.py:286
  6.7 3.0 %collective-permute-start.1 = (f32[288,128]{1,0:T(8,128)S(1)}, f32[288,128]{1,0:T(8,128)S(1)}, u32[]{:S(2)}, u32[]{:S(2)}) collective-permute-start(f32[288,128]{1,0:T(8,128)S(1)} %get-tuple-element.14), channel_id=1, source_target_pairs={{0,28},{4,0},{8,4},{12,8},{16,12},{20,16},{24,20},{28,24},{1,29},{... | collective-permute-start | bytes 442376 | tf_op jit(solution)/shard_map/ppermute | solution.py:286
  9.7 3.9 %collective-permute-done.refs_2_ = f32[288,128]{1,0:T(8,128)S(1)} collective-permute-done((f32[288,128]{1,0:T(8,128)S(1)}, f32[288,128]{1,0:T(8,128)S(1)}, u32[]{:S(2)}, u32[]{:S(2)}) %collective-permute-start) | collective-permute-done | bytes 147488 | tf_op jit(solution)/shard_map/ppermute | solution.py:286
  13.6 1.5 %collective-permute-done.1.refs_3_ = f32[288,128]{1,0:T(8,128)S(1)} collective-permute-done((f32[288,128]{1,0:T(8,128)S(1)}, f32[288,128]{1,0:T(8,128)S(1)}, u32[]{:S(2)}, u32[]{:S(2)}) %collective-permute-start.1) | collective-permute-done | bytes 147488 | tf_op jit(solution)/shard_map/ppermute | solution.py:286
  15.1 1.2 %across.1 = (s32[3,320,128]{2,1,0:T(8,128)S(1)}, f32[208,128]{1,0:T(8,128)S(1)}, f32[208,128]{1,0:T(8,128)S(1)}) custom-call(f32[3,320,128]{2,1,0:T(8,128)S(1)} %get-tuple-element.12.refs_0_, s32[256,256]{1,0:T(8,128)} %refs_1_.1, f32[288,128]{1,0:T(8,128)S(1)} %collective-permute-done.refs_2_, f32[288,128]{1,0:T(8,128)S(1)} %collective-permute-done.1.refs_3_), custom_call_target="tpu_custom_call" | custom-call | tf_op jit(solution)/shard_map/across/pallas_call | solution.py:335
  16.3 0.0 collective-permute-start.2
  16.3 1.6 %collective-permute-start.3 = (f32[208,128]{1,0:T(8,128)S(1)}, f32[208,128]{1,0:T(8,128)S(1)}, u32[]{:S(2)}, u32[]{:S(2)}) collective-permute-start(f32[208,128]{1,0:T(8,128)S(1)} %get-tuple-element.17), channel_id=1, source_target_pairs={{0,3},{1,2},{2,1},{3,0},{4,7},{5,6},{6,5},{7,4},{8,11},{9,10},{10,... | collective-permute-start | bytes 319496 | tf_op jit(solution)/shard_map/ppermute | solution.py:292
  18.0 0.0 collective-permute-done.2.refs_2_
  18.0 3.1 %collective-permute-done.3.refs_3_ = f32[208,128]{1,0:T(8,128)S(1)} collective-permute-done((f32[208,128]{1,0:T(8,128)S(1)}, f32[208,128]{1,0:T(8,128)S(1)}, u32[]{:S(2)}, u32[]{:S(2)}) %collective-permute-start.3) | collective-permute-done | bytes 106528 | tf_op jit(solution)/shard_map/ppermute | solution.py:292
  21.1 22.8 %sweep.1 = (f32[4,256,256]{2,1,0:T(8,128)}, f32[16,128]{1,0:T(8,128)}) custom-call(f32[4,64]{1,0:T(4,128)} %refs_0_.3, s32[3,320,128]{2,1,0:T(8,128)S(1)} %get-tuple-element.15.refs_1_, f32[208,128]{1,0:T(8,128)S(1)} %collective-permute-done.2.refs_2_, f32[208,128]{1,0:T(8,128)S(1)} %collective-permute-done.3.refs_3_, s32[16,128]{1,0:T(8,128)} %get-tuple-element.18.refs_4_, ...), custom_call_target="tpu_custom_call" | custom-call | tf_op jit(solution)/shard_map/sweep/pallas_call | solution.py:354
Async XLA Ops:
  3.7 10.0 %collective-permute-start = (f32[288,128]{1,0:T(8,128)S(1)}, f32[288,128]{1,0:T(8,128)S(1)}, u32[]{:S(2)}, u32[]{:S(2)}) collective-permute-start(f32[288,128]{1,0:T(8,128)S(1)} %get-tuple-element.13), channel_id=1, source_target_pairs={{0,4},{4,8},{8,12},{12,16},{16,20},{20,24},{24,28},{28,0},{1,5},{5... | collective-permute-start | bytes 442376 | tf_op jit(solution)/shard_map/ppermute | solution.py:286
  6.7 8.5 %collective-permute-start.1 = (f32[288,128]{1,0:T(8,128)S(1)}, f32[288,128]{1,0:T(8,128)S(1)}, u32[]{:S(2)}, u32[]{:S(2)}) collective-permute-start(f32[288,128]{1,0:T(8,128)S(1)} %get-tuple-element.14), channel_id=1, source_target_pairs={{0,28},{4,0},{8,4},{12,8},{16,12},{20,16},{24,20},{28,24},{1,29},{... | collective-permute-start | bytes 442376 | tf_op jit(solution)/shard_map/ppermute | solution.py:286
  16.3 1.7 %collective-permute-start.2 = (f32[208,128]{1,0:T(8,128)S(1)}, f32[208,128]{1,0:T(8,128)S(1)}, u32[]{:S(2)}, u32[]{:S(2)}) collective-permute-start(f32[208,128]{1,0:T(8,128)S(1)} %get-tuple-element.16), channel_id=1, source_target_pairs={{0,1},{1,0},{2,3},{3,2},{4,5},{5,4},{6,7},{7,6},{8,9},{9,8},{10,11... | collective-permute-start | bytes 319496 | tf_op jit(solution)/shard_map/ppermute | solution.py:292
  16.3 4.7 %collective-permute-start.3 = (f32[208,128]{1,0:T(8,128)S(1)}, f32[208,128]{1,0:T(8,128)S(1)}, u32[]{:S(2)}, u32[]{:S(2)}) collective-permute-start(f32[208,128]{1,0:T(8,128)S(1)} %get-tuple-element.17), channel_id=1, source_target_pairs={{0,3},{1,2},{2,1},{3,0},{4,7},{5,6},{6,5},{7,4},{8,11},{9,10},{10,... | collective-permute-start | bytes 319496 | tf_op jit(solution)/shard_map/ppermute | solution.py:292

commit v3 on v2

--- a/solution.py
+++ b/solution.py
@@ -12,6 +12,8 @@
 PENALTY = 0.5
 LANES = 128
 SUB = 8
+PACK = 2
+UNROLL = 3
 
 
 class Plan:
@@ -22,21 +24,22 @@
         self.wide = steps + SWEEPS
         self.ring = rows + 2 * self.wide
         self.tiles = cols // LANES + 1
-        self.span = self.ring // SUB
-        self.step = LANES - 2 * SWEEPS
-        self.sweep_tiles = -(-(cols + 2 * self.near) // self.step)
+        self.lines = cols + 2 * self.wide
+        self.span = self.lines // SUB
+        self.blocks = LANES // PACK
+        self.deep = self.ring // self.blocks
+        self.groups = tasks // PACK
+        self.planes = self.groups * self.deep
         self.code_bits = (codes - 1).bit_length()
         self.across_rows = rows + 2 * self.near
         self.band = self.wide + self.near
         self.down_rows = self.tiles * self.band + (self.tiles - 1) * self.wide
         assert cols % LANES == 0 and rows % SUB == 0 and agents % LANES == 0
         assert 4 * self.wide <= LANES and self.near % SUB == 0 and self.wide % SUB == 0
-        assert self.ring % SUB == 0 and codes <= LANES
-        self.magic = -(-(1 << 16) // self.span)
-        assert all((r * self.magic) >> 16 == r // self.span for r in range(self.ring))
-
-    def start(self, j):
-        return j * self.step - self.wide
+        assert self.ring % self.blocks == 0 and self.lines % SUB == 0
+        assert tasks % PACK == 0 and codes <= LANES
+        self.magic = -(-(1 << 16) // self.deep)
+        assert all((r * self.magic) >> 16 == r // self.deep for r in range(self.ring))
 
 
 def lane_of(shape):
@@ -67,15 +70,12 @@
         ring_col = jnp.where(col < 0, col + ring_cols, col)
         row_hot[:, here] = jnp.where(row_id == ring_row, 1.0, 0.0).astype(jnp.bfloat16)
         col_hot[:, here] = jnp.where(col_id == ring_col, 1.0, 0.0).astype(jnp.bfloat16)
-        inner = col + p.near
-        j = jnp.zeros_like(inner)
-        for edge in range(1, p.sweep_tiles):
-            j = j + jnp.where(inner >= edge * p.step, 1, 0)
-        lane_out[i : i + 1, :] = inner - j * p.step + (p.wide - p.near)
-        sub = (ring_row * p.magic) >> 16
-        address[i : i + 1, :] = (
-            (j * p.tasks + task[i : i + 1, :]) * p.ring + (ring_row - sub * p.span) * SUB + sub
-        )
+        t = task[i : i + 1, :]
+        u = t // PACK
+        block = ((row + p.wide) * p.magic) >> 16
+        lane_out[i : i + 1, :] = (t - u * PACK) * p.blocks + block
+        plane = u * p.deep + row + p.wide - block * p.deep
+        address[i : i + 1, :] = plane * p.lines + col + p.wide
     counts = lax.dot_general(
         row_hot[...], col_hot[...], (((1,), (1,)), ((), ())), preferred_element_type=jnp.float32
     )
@@ -161,7 +161,7 @@
 
 
 def sweep_kernel(plan, table, key, first, second, address, lane_in, values, answers,
-                 looked, ring, tiles, reward, gain, value, natural, rows_of, sems):
+                 looked, ring, flat, turned, reward, gain, value, edge, final, natural, rows_of, sems):
     p = plan
     last = p.tiles - 1
     odd = lax.axis_index("gy") % 2 == 1
@@ -190,92 +190,118 @@
         own = lambda lo, n: key[t, pl.ds(lo, n), :]
 
         def put(lo, n, x):
-            ring[t, pl.ds(lo, n), :] = x
+            ring[t, pl.ds(lo + w, n), :] = x
 
         put(0, s, own(0, s) + up_cnt[w:])
         put(s, p.rows - 2 * s, own(s, p.rows - 2 * s))
         put(p.rows - s, s, own(p.rows - s, s) + low_cnt[:s])
         put(p.rows, s, own(p.rows, s) + low_cnt[s : 2 * s] + low_code[:s])
         put(p.rows + s, w - s, low_cnt[2 * s :] + low_code[s:])
-        put(p.ring - w, w - s, up_cnt[: w - s] + up_code[: w - s])
-        put(p.ring - s, s, own(p.ring - s, s) + up_cnt[w - s : w] + up_code[w - s :])
-
-    lane = lane_of((p.ring, LANES))
-    for j in range(p.sweep_tiles):
-        at = p.start(j) % (p.tiles * LANES)
-        a, off = at // LANES, at % LANES
-        x = ring[a]
-        if off:
-            x = pltpu.roll(jnp.where(lane >= off, x, ring[(a + 1) % p.tiles]), LANES - off, 1)
-        tiles[j] = x
+        put(-w, w - s, up_cnt[: w - s] + up_code[: w - s])
+        put(-s, s, own(p.ring - s, s) + up_cnt[w - s : w] + up_code[w - s :])
 
     looked[pl.ds(0, p.tasks), pl.ds(0, p.codes)] = table[...]
     looks = [jnp.broadcast_to(looked[t : t + 1, :], (SUB, LANES)) for t in range(p.tasks)]
-    for j in range(p.sweep_tiles):
-        for k in range(p.span):
-            x = tiles[j, pl.ds(k, SUB, stride=p.span), :]
+    for c in range(p.tiles):
+        for k in range(p.ring // SUB):
+            at = pl.ds(k * SUB, SUB)
+            x = ring[c, at, :]
             code = x & ((1 << bits) - 1)
             crowd = PENALTY * (x >> bits).astype(jnp.float32)
-            at = pl.ds(k * SUB, SUB)
-            gain[j, at, :] = jnp.where(code < p.codes - TERMINAL, GAMMA, 0.0)
+            flat[p.tasks * p.tiles + c, at, :] = jnp.where(code < p.codes - TERMINAL, GAMMA, 0.0)
             for t in range(p.tasks):
-                r = jnp.take_along_axis(looks[t], code, axis=1, mode="promise_in_bounds") - crowd
-                reward[j * p.tasks + t, at, :] = r
-                value[pl.ds((j * p.tasks + t) * p.ring + k * SUB, SUB), :] = r
-
-    def sweep(_, carry):
-        for j in range(p.sweep_tiles):
-            base = [(j * p.tasks + t) * p.ring for t in range(p.tasks)]
-            load = lambda t, k: value[pl.ds(base[t] + k * SUB, SUB), :]
-            first_row = [load(t, 0) for t in range(p.tasks)]
-            before = [pltpu.roll(load(t, p.span - 1), 1, 0) for t in range(p.tasks)]
-            now = list(first_row)
-            for k in range(p.span):
-                g = gain[j, pl.ds(k * SUB, SUB), :]
-                for t in range(p.tasks):
-                    after = load(t, k + 1) if k + 1 < p.span else pltpu.roll(first_row[t], SUB - 1, 0)
-                    side = jnp.maximum(pltpu.roll(now[t], 1, 1), pltpu.roll(now[t], LANES - 1, 1))
-                    best = jnp.maximum(jnp.maximum(before[t], after), side)
-                    new = reward[j * p.tasks + t, pl.ds(k * SUB, SUB), :] + g * best
-                    value[pl.ds(base[t] + k * SUB, SUB), :] = new
-                    before[t], now[t] = now[t], after
+                found = jnp.take_along_axis(looks[t], code, axis=1, mode="promise_in_bounds")
+                flat[t * p.tiles + c, at, :] = found - crowd
+
+    for u in range(p.groups + 1):
+        for i in range(p.deep):
+            for c in range(p.tiles):
+                parts = []
+                for h in range(PACK):
+                    t = u * PACK + h if u < p.groups else p.tasks
+                    parts.append(flat[t * p.tiles + c, pl.ds(i, p.blocks, stride=p.deep), :])
+                x = jnp.transpose(jnp.concatenate(parts, axis=0))
+                if c < last:
+                    turned[u * p.deep + i, pl.ds(w + c * LANES, LANES), :] = x
+                else:
+                    turned[u * p.deep + i, pl.ds(w + p.cols, w), :] = x[:w]
+                    turned[u * p.deep + i, pl.ds(0, w), :] = x[LANES - w :]
+
+    for q in range(p.span):
+        for n in range(p.planes + p.deep):
+            x = turned[n, pl.ds(q, SUB, stride=p.span), :]
+            if n < p.planes:
+                at = pl.ds((q * p.planes + n) * SUB, SUB)
+                reward[at, :] = x
+                value[at, :] = x
+            else:
+                gain[pl.ds((q * p.deep + n - p.planes) * SUB, SUB), :] = x
+
+    def sweep(put):
+        load = lambda q: [value[pl.ds((q * p.planes + n) * SUB, SUB), :] for n in range(p.planes)]
+        now = load(0)
+        before = [pltpu.roll(x, 1, 0) for x in load(p.span - 1)]
+        for n in range(p.planes):
+            edge[pl.ds(n * SUB, SUB), :] = pltpu.roll(now[n], SUB - 1, 0)
+        for q in range(p.span):
+            if q + 1 < p.span:
+                after = load(q + 1)
+            else:
+                after = [edge[pl.ds(n * SUB, SUB), :] for n in range(p.planes)]
+            for i in range(p.deep):
+                g = gain[pl.ds((q * p.deep + i) * SUB, SUB), :]
+                for u in range(p.groups):
+                    n = u * p.deep + i
+                    up = now[n - 1] if i > 0 else pltpu.roll(now[n + p.deep - 1], 1, 1)
+                    down = now[n + 1] if i + 1 < p.deep else pltpu.roll(now[n + 1 - p.deep], LANES - 1, 1)
+                    best = jnp.maximum(jnp.maximum(up, down), jnp.maximum(before[n], after[n]))
+                    put(q, n, reward[pl.ds((q * p.planes + n) * SUB, SUB), :] + g * best)
+            before, now = now, after
+
+    def put_value(q, n, x):
+        value[pl.ds((q * p.planes + n) * SUB, SUB), :] = x
+
+    def put_final(q, n, x):
+        final[pl.ds(n * p.lines + q, SUB, stride=p.span), :] = x
+
+    def sweeps(_, carry):
+        for _ in range(UNROLL):
+            sweep(put_value)
         return carry
 
-    lax.fori_loop(0, SWEEPS, sweep, 0)
-
-    lane = lane_of((SUB, LANES))
+    assert (SWEEPS - 1) % UNROLL == 0
+    lax.fori_loop(0, (SWEEPS - 1) // UNROLL, sweeps, 0)
+    sweep(put_final)
+
     copies = []
-    for t in range(p.tasks):
+    for u in range(p.groups):
         for c in range(last):
-            for k in range(p.span):
-                out = None
-                for j in range(p.sweep_tiles):
-                    lo = p.start(j) + SWEEPS - c * LANES
-                    hi = lo + p.step
-                    if hi <= 0 or lo >= LANES:
-                        continue
-                    x = value[pl.ds((j * p.tasks + t) * p.ring + k * SUB, SUB), :]
-                    x = pltpu.roll(x, (p.start(j) - c * LANES) % LANES, 1)
-                    out = x if out is None else jnp.where(lane >= lo, x, out)
-                natural[t * last + c, pl.ds(k, SUB, stride=p.span), :] = out
-            copy = pltpu.make_async_copy(
-                natural.at[t * last + c, pl.ds(0, p.rows), :],
-                values.at[t, :, pl.ds(c * LANES, LANES)],
-                sems.at[t * last + c],
-            )
-            copy.start()
-            copies.append(copy)
+            for i in range(p.deep):
+                lines = pl.ds((u * p.deep + i) * p.lines + w + c * LANES, LANES)
+                x = jnp.transpose(final[lines, :])
+                for h in range(PACK):
+                    at = pl.ds(i, p.blocks, stride=p.deep)
+                    natural[(u * PACK + h) * last + c, at, :] = x[h * p.blocks : (h + 1) * p.blocks]
+            for h in range(PACK):
+                t = u * PACK + h
+                copy = pltpu.make_async_copy(
+                    natural.at[t * last + c, pl.ds(w, p.rows), :],
+                    values.at[t, :, pl.ds(c * LANES, LANES)],
+                    sems.at[t * last + c],
+                )
+                copy.start()
+                copies.append(copy)
 
     def fetch(i, carry):
         for l in range(LANES):
-            rows_of[pl.ds(i * LANES + l, 1), :] = value[pl.ds(address[i, l], 1), :]
+            rows_of[pl.ds(i * LANES + l, 1), :] = final[pl.ds(address[i, l], 1), :]
         return carry
 
     lax.fori_loop(0, p.agents // LANES, fetch, 0)
     lane_id = lax.broadcasted_iota(jnp.int32, (LANES, LANES), 0)
     for i in range(p.agents // LANES):
-        turned = jnp.transpose(rows_of[pl.ds(i * LANES, LANES), :])
-        picked = jnp.where(lane_id == lane_in[i : i + 1, :], turned, 0.0)
+        x = jnp.transpose(rows_of[pl.ds(i * LANES, LANES), :])
+        picked = jnp.where(lane_id == lane_in[i : i + 1, :], x, 0.0)
         answers[i : i + 1, :] = jnp.sum(picked, axis=0, keepdims=True)
     for copy in copies:
         copy.wait()
@@ -349,7 +375,6 @@
     )(near(hist), map_codes, near(from_left), near(from_right))
     first = swap(first, "gy", 0)
     second = swap(second, "gy", 1)
-    blocks = p.sweep_tiles * tasks
     outs = tasks * (p.tiles - 1)
     values, answers = pl.pallas_call(
         bind(sweep_kernel),
@@ -359,10 +384,13 @@
         scratch_shapes=[
             pltpu.VMEM((tasks, LANES), f32),
             pltpu.VMEM((p.tiles, p.ring, LANES), i32),
-            pltpu.VMEM((p.sweep_tiles, p.ring, LANES), i32),
-            pltpu.VMEM((blocks, p.ring, LANES), f32),
-            pltpu.VMEM((p.sweep_tiles, p.ring, LANES), f32),
-            pltpu.VMEM((blocks * p.ring, LANES), f32),
+            pltpu.VMEM(((tasks + 1) * p.tiles, p.ring, LANES), f32),
+            pltpu.VMEM((p.planes + p.deep, p.lines, LANES), f32),
+            pltpu.VMEM((p.planes * p.lines, LANES), f32),
+            pltpu.VMEM((p.deep * p.lines, LANES), f32),
+            pltpu.VMEM((p.planes * p.lines, LANES), f32),
+            pltpu.VMEM((p.planes * SUB, LANES), f32),
+            pltpu.VMEM((p.planes * p.lines, LANES), f32),
             pltpu.VMEM((outs, p.ring, LANES), f32),
             pltpu.VMEM((agents, LANES), f32),
             pltpu.SemaphoreType.DMA((outs,)),

time: 44.1 us -> 32.6 us (0.74)
  Pallas kernels: 27 us -> 15.6 us
    pallas_call x1, Pallas kernels: 22.8 us -> 11.3 us  [on_device(): pl.pallas_call(bind(sweep_kernel), in_specs=[vmem, vmem, vmem, vmem, smem...]
where the time goes in v3:
time: 32.6 us; the launch traced here: 32.4 us
  Pallas kernels  15.6 us (48%)
  waiting for transfers between devices  8.51 us (26%)
  starting transfers between devices  7.66 us (23%)
  between operations  0.64 us (2%)
    pallas_call x1, Pallas kernels, on_device(): pl.pallas_call(bind(sweep_kernel), in_specs=[vmem, vmem, vmem, vmem, smem...  11.3 us
    ppermute x2, starting transfers between devices, shift(): lax.ppermute(value, axis, [(i, (i + steps) % count) for i in range(count)])  6.01 us
    ppermute x2, waiting for transfers between devices, shift(): lax.ppermute(value, axis, [(i, (i + steps) % count) for i in range(count)])  5.42 us
    ppermute x2, waiting for transfers between devices, swap(): lax.ppermute(value, axis, [(i, (i + (1 if i % 2 == parity else -1)) % cou...  3.1 us
    pallas_call x1, Pallas kernels, on_device(): pl.pallas_call(bind(count_kernel), in_specs=[vmem] * 4, out_specs=[vmem]...  3.08 us
    ppermute x2, starting transfers between devices, swap(): lax.ppermute(value, axis, [(i, (i + (1 if i % 2 == parity else -1)) % cou...  1.65 us
    pallas_call x1, Pallas kernels, on_device(): pl.pallas_call(bind(across_kernel), in_specs=[vmem] * 4, out_specs=[vmem]...  1.18 us
  transfers between devices with their start and end apart: 4, of which 3 were waited for; matrix products, arithmetic and copies ran while one was open for 0% of the time, Pallas kernels for 0%

profile of v3, /device:TPU:0, one launch (start us, length us, event | category | flops | bytes accessed | tf_op | source)
XLA Modules:
  0.0 32.4 jit_solution(15427306720560740599)
XLA Ops:
  0.6 3.1 %count.1 = (f32[3,320,128]{2,1,0:T(8,128)S(1)}, f32[288,128]{1,0:T(8,128)S(1)}, f32[288,128]{1,0:T(8,128)S(1)}, s32[16,128]{1,0:T(8,128)}, s32[16,128]{1,0:T(8,128)S(1)}) custom-call(s32[16,2048]{1,0:T(8,128)} %refs_0_.2, s32[16,128]{1,0:T(8,128)} %bitcast.3, s32[16,128]{1,0:T(8,128)} %bitcast.4, s32[256,256]{1,0:T(8,128)} %refs_1_.1), custom_call_target="tpu_custom_call" | custom-call | tf_op jit(solution)/shard_map/count/pallas_call | solution.py:342
  3.7 3.0 %collective-permute-start = (f32[288,128]{1,0:T(8,128)S(1)}, f32[288,128]{1,0:T(8,128)S(1)}, u32[]{:S(2)}, u32[]{:S(2)}) collective-permute-start(f32[288,128]{1,0:T(8,128)S(1)} %get-tuple-element.13), channel_id=1, source_target_pairs={{0,4},{4,8},{8,12},{12,16},{16,20},{20,24},{24,28},{28,0},{1,5},{5... | collective-permute-start | bytes 442376 | tf_op jit(solution)/shard_map/ppermute | solution.py:312
  6.7 3.0 %collective-permute-start.1 = (f32[288,128]{1,0:T(8,128)S(1)}, f32[288,128]{1,0:T(8,128)S(1)}, u32[]{:S(2)}, u32[]{:S(2)}) collective-permute-start(f32[288,128]{1,0:T(8,128)S(1)} %get-tuple-element.14), channel_id=1, source_target_pairs={{0,28},{4,0},{8,4},{12,8},{16,12},{20,16},{24,20},{28,24},{1,29},{... | collective-permute-start | bytes 442376 | tf_op jit(solution)/shard_map/ppermute | solution.py:312
  9.7 3.9 %collective-permute-done.refs_2_ = f32[288,128]{1,0:T(8,128)S(1)} collective-permute-done((f32[288,128]{1,0:T(8,128)S(1)}, f32[288,128]{1,0:T(8,128)S(1)}, u32[]{:S(2)}, u32[]{:S(2)}) %collective-permute-start) | collective-permute-done | bytes 147488 | tf_op jit(solution)/shard_map/ppermute | solution.py:312
  13.7 1.5 %collective-permute-done.1.refs_3_ = f32[288,128]{1,0:T(8,128)S(1)} collective-permute-done((f32[288,128]{1,0:T(8,128)S(1)}, f32[288,128]{1,0:T(8,128)S(1)}, u32[]{:S(2)}, u32[]{:S(2)}) %collective-permute-start.1) | collective-permute-done | bytes 147488 | tf_op jit(solution)/shard_map/ppermute | solution.py:312
  15.1 1.2 %across.1 = (s32[3,320,128]{2,1,0:T(8,128)S(1)}, f32[208,128]{1,0:T(8,128)S(1)}, f32[208,128]{1,0:T(8,128)S(1)}) custom-call(f32[3,320,128]{2,1,0:T(8,128)S(1)} %get-tuple-element.12.refs_0_, s32[256,256]{1,0:T(8,128)} %refs_1_.1, f32[288,128]{1,0:T(8,128)S(1)} %collective-permute-done.refs_2_, f32[288,128]{1,0:T(8,128)S(1)} %collective-permute-done.1.refs_3_), custom_call_target="tpu_custom_call" | custom-call | tf_op jit(solution)/shard_map/across/pallas_call | solution.py:361
  16.3 0.0 collective-permute-start.2
  16.4 1.6 %collective-permute-start.3 = (f32[208,128]{1,0:T(8,128)S(1)}, f32[208,128]{1,0:T(8,128)S(1)}, u32[]{:S(2)}, u32[]{:S(2)}) collective-permute-start(f32[208,128]{1,0:T(8,128)S(1)} %get-tuple-element.17), channel_id=1, source_target_pairs={{0,3},{1,2},{2,1},{3,0},{4,7},{5,6},{6,5},{7,4},{8,11},{9,10},{10,... | collective-permute-start | bytes 319496 | tf_op jit(solution)/shard_map/ppermute | solution.py:318
  18.0 0.0 collective-permute-done.2.refs_2_
  18.0 3.1 %collective-permute-done.3.refs_3_ = f32[208,128]{1,0:T(8,128)S(1)} collective-permute-done((f32[208,128]{1,0:T(8,128)S(1)}, f32[208,128]{1,0:T(8,128)S(1)}, u32[]{:S(2)}, u32[]{:S(2)}) %collective-permute-start.3) | collective-permute-done | bytes 106528 | tf_op jit(solution)/shard_map/ppermute | solution.py:318
  21.1 11.3 %sweep.1 = (f32[4,256,256]{2,1,0:T(8,128)}, f32[16,128]{1,0:T(8,128)}) custom-call(f32[4,64]{1,0:T(4,128)} %refs_0_.3, s32[3,320,128]{2,1,0:T(8,128)S(1)} %get-tuple-element.15.refs_1_, f32[208,128]{1,0:T(8,128)S(1)} %collective-permute-done.2.refs_2_, f32[208,128]{1,0:T(8,128)S(1)} %collective-permute-done.3.refs_3_, s32[16,128]{1,0:T(8,128)} %get-tuple-element.18.refs_4_, ...), custom_call_target="tpu_custom_call" | custom-call | tf_op jit(solution)/shard_map/sweep/pallas_call | solution.py:379
Async XLA Ops:
  3.7 10.0 %collective-permute-start = (f32[288,128]{1,0:T(8,128)S(1)}, f32[288,128]{1,0:T(8,128)S(1)}, u32[]{:S(2)}, u32[]{:S(2)}) collective-permute-start(f32[288,128]{1,0:T(8,128)S(1)} %get-tuple-element.13), channel_id=1, source_target_pairs={{0,4},{4,8},{8,12},{12,16},{16,20},{20,24},{24,28},{28,0},{1,5},{5... | collective-permute-start | bytes 442376 | tf_op jit(solution)/shard_map/ppermute | solution.py:312
  6.7 8.5 %collective-permute-start.1 = (f32[288,128]{1,0:T(8,128)S(1)}, f32[288,128]{1,0:T(8,128)S(1)}, u32[]{:S(2)}, u32[]{:S(2)}) collective-permute-start(f32[288,128]{1,0:T(8,128)S(1)} %get-tuple-element.14), channel_id=1, source_target_pairs={{0,28},{4,0},{8,4},{12,8},{16,12},{20,16},{24,20},{28,24},{1,29},{... | collective-permute-start | bytes 442376 | tf_op jit(solution)/shard_map/ppermute | solution.py:312
  16.3 1.7 %collective-permute-start.2 = (f32[208,128]{1,0:T(8,128)S(1)}, f32[208,128]{1,0:T(8,128)S(1)}, u32[]{:S(2)}, u32[]{:S(2)}) collective-permute-start(f32[208,128]{1,0:T(8,128)S(1)} %get-tuple-element.16), channel_id=1, source_target_pairs={{0,1},{1,0},{2,3},{3,2},{4,5},{5,4},{6,7},{7,6},{8,9},{9,8},{10,11... | collective-permute-start | bytes 319496 | tf_op jit(solution)/shard_map/ppermute | solution.py:318
  16.4 4.7 %collective-permute-start.3 = (f32[208,128]{1,0:T(8,128)S(1)}, f32[208,128]{1,0:T(8,128)S(1)}, u32[]{:S(2)}, u32[]{:S(2)}) collective-permute-start(f32[208,128]{1,0:T(8,128)S(1)} %get-tuple-element.17), channel_id=1, source_target_pairs={{0,3},{1,2},{2,1},{3,0},{4,7},{5,6},{6,5},{7,4},{8,11},{9,10},{10,... | collective-permute-start | bytes 319496 | tf_op jit(solution)/shard_map/ppermute | solution.py:318

commit v4 on v3

v4 whole, which is shorter than its diff:
```python
import jax
import jax.numpy as jnp
from jax import lax
from jax.experimental import pallas as pl
from jax.experimental.pallas import tpu as pltpu
from jax.sharding import PartitionSpec as P


SWEEPS = 16
TERMINAL = 2
GAMMA = 0.95
PENALTY = 0.5
LANES = 128
SUB = 8
PACK = 2
UNROLL = 2


class Plan:
    def __init__(self, rows, cols, agents, steps, tasks, codes):
        self.rows, self.cols, self.agents = rows, cols, agents
        self.steps, self.tasks, self.codes = steps, tasks, codes
        self.near = steps
        self.wide = steps + SWEEPS
        self.ring = rows + 2 * self.wide
        self.tiles = cols // LANES + 1
        self.lines = cols + 2 * self.wide
        self.span = self.lines // SUB
        self.blocks = LANES // PACK
        self.deep = self.ring // self.blocks
        self.groups = tasks // PACK
        self.planes = self.groups * self.deep
        self.code_bits = (codes - 1).bit_length()
        self.message = rows + 2 * self.near
        self.half = self.message // 2
        self.band = self.wide + self.near
        self.pack = -(-(rows - self.half) // (LANES // self.wide * SUB)) * SUB
        self.across_rows = self.half + self.pack
        self.down_rows = self.tiles * self.band + (self.tiles - 1) * self.wide
        assert cols % LANES == 0 and rows % SUB == 0 and agents % LANES == 0
        assert 4 * self.wide <= LANES and self.near % SUB == 0 and self.wide % SUB == 0
        assert self.half % SUB == 0 and LANES % self.wide == 0 and self.near % 16 == 0
        assert self.band + self.wide + self.band <= LANES
        assert self.ring % self.blocks == 0 and self.lines % SUB == 0
        assert tasks % PACK == 0 and codes <= LANES
        self.magic = -(-(1 << 16) // self.deep)
        assert all((r * self.magic) >> 16 == r // self.deep for r in range(self.ring))


def lane_of(shape):
    return lax.broadcasted_iota(jnp.int32, shape, len(shape) - 1)


def split_cell(cell, cols):
    if cols & (cols - 1) == 0:
        return cell >> (cols.bit_length() - 1), cell & (cols - 1)
    return lax.div(cell, cols), lax.rem(cell, cols)


def one_hot(ids, positions):
    return jnp.where(ids == positions, 1.0, 0.0).astype(jnp.bfloat16)


def counted(row_hot, col_hot):
    return lax.dot_general(
        row_hot[...], col_hot[...], (((1,), (1,)), ((), ())), preferred_element_type=jnp.float32
    )


def right_roll(p, piece):
    return {"second": p.band, "code": LANES - p.wide}.get(piece, None if isinstance(piece, str) else (piece + 1) * p.wide % LANES)


def left_roll(p, piece):
    return {"second": LANES - p.band, "code": p.wide}.get(piece, None if isinstance(piece, str) else piece * p.wide)


def roll(x, amount):
    amount %= LANES
    return x if amount == 0 else pltpu.roll(x, amount, 1)


def bands_kernel(plan, act, start, code, right, left, ring_row, ring_col, row_hot, col_hot):
    p = plan
    last = p.tiles - 1
    ring_cols = p.tiles * LANES
    row_id = lax.broadcasted_iota(jnp.int32, (p.message, LANES), 0)
    row_id = jnp.where(row_id >= p.rows + p.near, row_id + p.ring - p.message, row_id)
    lines = (
        (0, p.near, last * LANES),
        (LANES - p.wide, p.wide, (last - 1) * LANES + LANES - p.wide),
        (LANES, p.wide, 0),
        (2 * LANES - p.near, p.near, ring_cols - p.near),
    )
    blank = 0
    for at, n, _ in lines + ((2 * LANES, 0, 0),):
        if at > blank:
            col_hot[blank:at, :] = jnp.zeros((at - blank, p.agents), jnp.bfloat16)
        blank = at + n
    for i in range(p.agents // LANES):
        here = slice(i * LANES, (i + 1) * LANES)
        a = act[:, here]
        one = lambda c: jnp.where(a == c, 1, 0)
        row, col = split_cell(start[i : i + 1, :], p.cols)
        row = row + jnp.sum(one(2) - one(1), axis=0, keepdims=True)
        col = col + jnp.sum(one(4) - one(3), axis=0, keepdims=True)
        row = jnp.where(row < 0, row + p.ring, row)
        col = jnp.where(col < 0, col + ring_cols, col)
        ring_row[i : i + 1, :] = row
        ring_col[i : i + 1, :] = col
        row_hot[:, here] = one_hot(row_id, row)
        for at, n, first in lines:
            ids = first + lax.broadcasted_iota(jnp.int32, (n, LANES), 0)
            col_hot[at : at + n, here] = one_hot(ids, col)
    counts = counted(row_hot, col_hot)
    lane = lane_of((p.half, LANES))
    for out, side, spare, shift, band in (
        (right, 0, p.near, right_roll, code[:, (last - 1) * LANES :]),
        (left, 1, LANES - p.near - p.band, left_roll, code[:, :LANES]),
    ):
        own = counts[:, side * LANES : (side + 1) * LANES]
        band = band.astype(jnp.float32)
        x = own[: p.half]
        x = jnp.where((lane >= spare) & (lane < spare + p.band), roll(own[p.half :], shift(p, "second")), x)
        lo = LANES - 2 * p.wide if side == 0 else p.wide
        x = jnp.where((lane >= lo) & (lane < lo + p.wide), roll(band[: p.half], shift(p, "code")), x)
        out[pl.ds(0, p.half), :] = x
        packed_lane = lane_of((p.pack, LANES))
        rest = jnp.zeros((p.pack, LANES), jnp.float32)
        for g in range(LANES // p.wide):
            lo = p.half + g * p.pack
            n = min(p.pack, p.rows - lo)
            if n <= 0:
                break
            y = roll(band[lo : lo + n], shift(p, g))
            if n < p.pack:
                y = jnp.concatenate([y, jnp.zeros((p.pack - n, LANES), jnp.float32)], axis=0)
            rest = jnp.where((packed_lane >= g * p.wide) & (packed_lane < (g + 1) * p.wide), y, rest)
        out[pl.ds(p.half, p.pack), :] = rest


def local_kernel(plan, ring_row, ring_col, task, table, hist, address, lane_out, looked, row_hot, col_hot):
    p = plan
    ring_cols = p.tiles * LANES
    row_id = lax.broadcasted_iota(jnp.int32, (p.ring, LANES), 0)
    col_id = lax.broadcasted_iota(jnp.int32, (ring_cols, LANES), 0)
    for i in range(p.agents // LANES):
        here = slice(i * LANES, (i + 1) * LANES)
        row = ring_row[i : i + 1, :]
        col = ring_col[i : i + 1, :]
        row_hot[:, here] = one_hot(row_id, row)
        col_hot[:, here] = one_hot(col_id, col)
        row = jnp.where(row >= p.rows + p.near, row - p.ring, row) + p.wide
        col = jnp.where(col >= p.cols + p.near, col - ring_cols, col) + p.wide
        t = task[i : i + 1, :]
        u = t // PACK
        block = (row * p.magic) >> 16
        lane_out[i : i + 1, :] = (t - u * PACK) * p.blocks + block
        plane = u * p.deep + row - block * p.deep
        address[i : i + 1, :] = plane * p.lines + col
    counts = counted(row_hot, col_hot)
    for t in range(p.tiles):
        hist[t] = counts[:, t * LANES : (t + 1) * LANES]
    looked[...] = jnp.zeros_like(looked)
    looked[pl.ds(0, p.tasks), pl.ds(0, p.codes)] = table[...]


def side_counts(p, message, shift, lo, n):
    parts = []
    for a, b in ((lo, min(lo + n, p.half)), (max(lo, p.half), lo + n)):
        if a < b and a < p.half:
            parts.append(message[pl.ds(a, b - a), :])
        elif a < b:
            parts.append(roll(message[pl.ds(a - p.half, b - a), :], -shift(p, "second")))
    return parts[0] if len(parts) == 1 else jnp.concatenate(parts, axis=0)


def side_codes(p, message, shift, lo, n):
    parts = []
    at = lo
    while at < lo + n:
        if at < p.half:
            end = min(lo + n, p.half)
            parts.append(roll(message[pl.ds(at, end - at), :], -shift(p, "code")))
        else:
            g, r = divmod(at - p.half, p.pack)
            end = min(lo + n, at - r + p.pack)
            parts.append(roll(message[pl.ds(p.half + r, end - at), :], -shift(p, g)))
        at = end
    return parts[0] if len(parts) == 1 else jnp.concatenate(parts, axis=0)


def merged_counts(p, hist, from_left, from_right, row, n):
    last = p.tiles - 1
    lo = row if row < p.rows + p.near else row - p.ring + p.message
    lane = lane_of((n, LANES))
    l = side_counts(p, from_left, right_roll, lo, n)
    r = side_counts(p, from_right, left_roll, lo, n)
    out = []
    for t in range(p.tiles):
        h = hist[t, pl.ds(row, n), :]
        if t == 0:
            h = h + jnp.where(lane < p.near, l, 0.0)
        if t == last - 1:
            h = h + jnp.where(lane >= LANES - p.near, r, 0.0)
        if t == last:
            h = h + jnp.where(lane >= LANES - p.wide, l, jnp.where(lane < p.wide, r, 0.0))
        out.append(h)
    return out


def merged_codes(p, code, from_left, from_right, row, n):
    last = p.tiles - 1
    lane = lane_of((n, LANES))
    out = [code[pl.ds(row, n), pl.ds(t * LANES, LANES)].astype(jnp.float32) for t in range(last)]
    l = side_codes(p, from_left, right_roll, row, n)
    r = side_codes(p, from_right, left_roll, row, n)
    out.append(jnp.where(lane >= LANES - p.wide, l, jnp.where(lane < p.wide, r, 0.0)))
    return out


def across_kernel(plan, hist, code, from_left, from_right, first, second):
    p = plan
    last = p.tiles - 1
    down_cnt = merged_counts(p, hist, from_left, from_right, p.rows - p.wide, p.band)
    up_near = merged_counts(p, hist, from_left, from_right, p.ring - p.near, p.near)
    up_wide = merged_counts(p, hist, from_left, from_right, 0, p.wide)
    down_code = merged_codes(p, code, from_left, from_right, p.rows - p.wide, p.wide)
    up_code = merged_codes(p, code, from_left, from_right, 0, p.wide)
    lane = lane_of((p.wide, LANES))
    inside = (lane >= p.wide) & (lane < LANES - p.wide)
    half = LANES // 2
    odd = lax.axis_index("gy") % 2 == 1

    def put(at, n, down, up):
        first[pl.ds(at, n), :] = jnp.where(odd, up, down)
        second[pl.ds(at, n), :] = jnp.where(odd, down, up)

    for t in range(p.tiles):
        down, up = down_cnt[t], jnp.concatenate([up_near[t], up_wide[t]], axis=0)
        if t < last:
            put(p.tiles * p.band + t * p.wide, p.wide, down_code[t], up_code[t])
        else:
            head = jnp.where(inside, roll(down_code[t], half), down[: p.wide])
            down = jnp.concatenate([head, down[p.wide :]], axis=0)
            tail = jnp.where(inside, roll(up_code[t], half), up[p.near :])
            up = jnp.concatenate([up[: p.near], tail], axis=0)
        put(t * p.band, p.band, down, up)


def look_up(p, looked):
    tables = [jnp.broadcast_to(looked[t : t + 1, :], (SUB, LANES)) for t in range(p.tasks)]

    def put(flat, c, at, code, count):
        crowd = PENALTY * count
        at = pl.ds(at, SUB)
        flat[p.tasks * p.tiles + c, at, :] = jnp.where(code < p.codes - TERMINAL, GAMMA, 0.0)
        for t in range(p.tasks):
            found = jnp.take_along_axis(tables[t], code, axis=1, mode="promise_in_bounds")
            flat[t * p.tiles + c, at, :] = found - crowd

    return put


def rewards_kernel(plan, hist, code, from_left, from_right, looked, flat, near):
    p = plan
    put = look_up(p, looked)
    for row in range(0, p.rows, SUB):
        counts = merged_counts(p, hist, from_left, from_right, row, SUB)
        codes = merged_codes(p, code, from_left, from_right, row, SUB)
        for c in range(p.tiles):
            put(flat, c, row + p.wide, codes[c].astype(jnp.int32), counts[c])
    for at, row in ((0, p.rows), (p.near, p.ring - p.near)):
        counts = merged_counts(p, hist, from_left, from_right, row, p.near)
        for c in range(p.tiles):
            near[c, pl.ds(at, p.near), :] = counts[c]


def sweep_kernel(plan, looked, flat_in, near, first, second, address_in, lane_in, values, answers, flat,
                 turned, reward, gain, value, edge, final, natural, rows_of, address, sems):
    p = plan
    del flat_in
    fetch_address = pltpu.make_async_copy(address_in, address, sems.at[p.tasks * (p.tiles - 1)])
    fetch_address.start()
    last = p.tiles - 1
    odd = lax.axis_index("gy") % 2 == 1
    half = LANES // 2
    w, s = p.wide, p.near

    def above(at, n):
        at = pl.ds(at, n)
        return jnp.where(odd, first[at, :], second[at, :])

    def below(at, n):
        at = pl.ds(at, n)
        return jnp.where(odd, second[at, :], first[at, :])

    put = look_up(p, looked)
    for c in range(p.tiles):
        base = c * p.band
        code_base = p.tiles * p.band + c * w
        for at, extra in ((0, above(base + w, s)), (p.rows - s, below(base, s))):
            at = pl.ds(w + at, s)
            for t in range(p.tasks):
                flat[t * p.tiles + c, at, :] = flat[t * p.tiles + c, at, :] - PENALTY * extra
        for row in range(0, w, SUB):
            count = above(base + row, SUB)
            code = above(code_base + row, SUB) if c < last else roll(count, half)
            if row >= w - s:
                count = count + near[c, pl.ds(s + row - (w - s), SUB), :]
            put(flat, c, row, code.astype(jnp.int32) & (LANES - 1), count)
            count = below(base + s + row, SUB)
            code = below(code_base + row, SUB) if c < last else roll(count, half)
            if row < s:
                count = count + near[c, pl.ds(row, SUB), :]
            put(flat, c, w + p.rows + row, code.astype(jnp.int32) & (LANES - 1), count)

    for u in range(p.groups + 1):
        for i in range(p.deep):
            for c in range(p.tiles):
                parts = []
                for h in range(PACK):
                    t = u * PACK + h if u < p.groups else p.tasks
                    parts.append(flat[t * p.tiles + c, pl.ds(i, p.blocks, stride=p.deep), :])
                x = jnp.transpose(jnp.concatenate(parts, axis=0))
                if c < last:
                    turned[u * p.deep + i, pl.ds(w + c * LANES, LANES), :] = x
                else:
                    turned[u * p.deep + i, pl.ds(w + p.cols, w), :] = x[:w]
                    turned[u * p.deep + i, pl.ds(0, w), :] = x[LANES - w :]

    for q in range(p.span):
        for n in range(p.planes + p.deep):
            x = turned[n, pl.ds(q, SUB, stride=p.span), :]
            if n < p.planes:
                at = pl.ds((q * p.planes + n) * SUB, SUB)
                reward[at, :] = x
            else:
                gain[pl.ds((q * p.deep + n - p.planes) * SUB, SUB), :] = x

    def sweep(held, put):
        load = lambda q: [held[pl.ds((q * p.planes + n) * SUB, SUB), :] for n in range(p.planes)]
        now = load(0)
        before = [pltpu.roll(x, 1, 0) for x in load(p.span - 1)]
        for n in range(p.planes):
            edge[pl.ds(n * SUB, SUB), :] = pltpu.roll(now[n], SUB - 1, 0)
        for q in range(p.span):
            if q + 1 < p.span:
                after = load(q + 1)
            else:
                after = [edge[pl.ds(n * SUB, SUB), :] for n in range(p.planes)]
            for i in range(p.deep):
                g = gain[pl.ds((q * p.deep + i) * SUB, SUB), :]
                for u in range(p.groups):
                    n = u * p.deep + i
                    up = now[n - 1] if i > 0 else pltpu.roll(now[n + p.deep - 1], 1, 1)
                    down = now[n + 1] if i + 1 < p.deep else pltpu.roll(now[n + 1 - p.deep], LANES - 1, 1)
                    best = jnp.maximum(jnp.maximum(up, down), jnp.maximum(before[n], after[n]))
                    put(q, n, reward[pl.ds((q * p.planes + n) * SUB, SUB), :] + g * best)
            before, now = now, after

    def put_value(q, n, x):
        value[pl.ds((q * p.planes + n) * SUB, SUB), :] = x

    def put_final(q, n, x):
        final[pl.ds(n * p.lines + q, SUB, stride=p.span), :] = x

    def sweeps(_, carry):
        for _ in range(UNROLL):
            sweep(value, put_value)
        return carry

    assert (SWEEPS - 2) % UNROLL == 0
    sweep(reward, put_value)
    lax.fori_loop(0, (SWEEPS - 2) // UNROLL, sweeps, 0)
    sweep(value, put_final)
    fetch_address.wait()

    copies = []
    for u in range(p.groups):
        for c in range(last):
            for i in range(p.deep):
                lines = pl.ds((u * p.deep + i) * p.lines + w + c * LANES, LANES)
                x = jnp.transpose(final[lines, :])
                for h in range(PACK):
                    at = pl.ds(i, p.blocks, stride=p.deep)
                    natural[(u * PACK + h) * last + c, at, :] = x[h * p.blocks : (h + 1) * p.blocks]
            for h in range(PACK):
                t = u * PACK + h
                copy = pltpu.make_async_copy(
                    natural.at[t * last + c, pl.ds(w, p.rows), :],
                    values.at[t, :, pl.ds(c * LANES, LANES)],
                    sems.at[t * last + c],
                )
                copy.start()
                copies.append(copy)

    def fetch(i, carry):
        for l in range(LANES):
            rows_of[pl.ds(i * LANES + l, 1), :] = final[pl.ds(address[i, l], 1), :]
        return carry

    lax.fori_loop(0, p.agents // LANES, fetch, 0)
    lane_id = lax.broadcasted_iota(jnp.int32, (LANES, LANES), 0)
    for i in range(p.agents // LANES):
        x = jnp.transpose(rows_of[pl.ds(i * LANES, LANES), :])
        picked = jnp.where(lane_id == lane_in[i : i + 1, :], x, 0.0)
        answers[i : i + 1, :] = jnp.sum(picked, axis=0, keepdims=True)
    for copy in copies:
        copy.wait()


def shift(value, axis, steps):
    count = lax.axis_size(axis)
    return lax.ppermute(value, axis, [(i, (i + steps) % count) for i in range(count)])


def swap(value, axis, parity):
    count = lax.axis_size(axis)
    assert count % 2 == 0
    return lax.ppermute(
        value, axis, [(i, (i + (1 if i % 2 == parity else -1)) % count) for i in range(count)]
    )


def on_device(map_codes, reward_table, start_cell, agent_task, actions):
    rows, cols = map_codes.shape
    tasks, codes = reward_table.shape
    steps, agents = actions.shape
    p = Plan(rows, cols, agents, steps, tasks, codes)
    vmem = pl.BlockSpec(memory_space=pltpu.VMEM)
    smem = pl.BlockSpec(memory_space=pltpu.SMEM)
    f32, i32 = jnp.float32, jnp.int32
    shape = jax.ShapeDtypeStruct
    fast = lambda dims, dtype: pltpu.VMEM(dims, dtype)
    near = lambda x: pltpu.with_memory_space_constraint(x, pltpu.VMEM)
    by_lane = (agents // LANES, LANES)

    def bind(kernel):
        def body(*refs):
            kernel(p, *refs)

        return body

    to_right, to_left, ring_row, ring_col = pl.pallas_call(
        bind(bands_kernel),
        in_specs=[vmem] * 3,
        out_specs=[vmem] * 4,
        out_shape=[
            fast((p.across_rows, LANES), f32),
            fast((p.across_rows, LANES), f32),
            fast(by_lane, i32),
            fast(by_lane, i32),
        ],
        scratch_shapes=[
            pltpu.VMEM((p.message, agents), jnp.bfloat16),
            pltpu.VMEM((2 * LANES, agents), jnp.bfloat16),
        ],
        name="bands",
    )(actions, start_cell.reshape(by_lane), map_codes)
    from_left = shift(to_right, "gx", 1)
    from_right = shift(to_left, "gx", -1)
    hist, address, lane, looked = pl.pallas_call(
        bind(local_kernel),
        in_specs=[vmem] * 4,
        out_specs=[vmem] * 4,
        out_shape=[
            fast((p.tiles, p.ring, LANES), f32),
            fast(by_lane, i32),
            fast(by_lane, i32),
            fast((SUB, LANES), f32),
        ],
        scratch_shapes=[
            pltpu.VMEM((p.ring, agents), jnp.bfloat16),
            pltpu.VMEM((p.tiles * LANES, agents), jnp.bfloat16),
        ],
        name="local",
    )(near(ring_row), near(ring_col), agent_task.reshape(by_lane), reward_table)
    sides = (near(hist), map_codes, near(from_left), near(from_right))
    first, second = pl.pallas_call(
        bind(across_kernel),
        in_specs=[vmem] * 4,
        out_specs=[vmem] * 2,
        out_shape=[fast((p.down_rows, LANES), f32), fast((p.down_rows, LANES), f32)],
        name="across",
    )(*sides)
    first = swap(first, "gy", 0)
    second = swap(second, "gy", 1)
    flats = ((tasks + 1) * p.tiles, p.ring, LANES)
    flat, edges = pl.pallas_call(
        bind(rewards_kernel),
        in_specs=[vmem] * 5,
        out_specs=[vmem] * 2,
        out_shape=[fast(flats, f32), fast((p.tiles, 2 * p.near, LANES), f32)],
        name="rewards",
    )(*sides, near(looked))
    outs = tasks * (p.tiles - 1)
    values, answers, _ = pl.pallas_call(
        bind(sweep_kernel),
        in_specs=[vmem] * 7,
        out_specs=[pl.BlockSpec(memory_space=pl.ANY), vmem, vmem],
        out_shape=[shape((tasks, rows, cols), f32), shape(by_lane, f32), fast(flats, f32)],
        scratch_shapes=[
            pltpu.VMEM((p.planes + p.deep, p.lines, LANES), f32),
            pltpu.VMEM((p.planes * p.lines, LANES), f32),
            pltpu.VMEM((p.deep * p.lines, LANES), f32),
            pltpu.VMEM((p.planes * p.lines, LANES), f32),
            pltpu.VMEM((p.planes * SUB, LANES), f32),
            pltpu.VMEM((p.planes * p.lines, LANES), f32),
            pltpu.VMEM((outs, p.ring, LANES), f32),
            pltpu.VMEM((agents, LANES), f32),
            pltpu.SMEM(by_lane, i32),
            pltpu.SemaphoreType.DMA((outs + 1,)),
        ],
        input_output_aliases={1: 2},
        name="sweep",
    )(near(looked), near(flat), near(edges), near(first), near(second), near(address), near(lane))
    return values, answers.reshape(agents)


def solution(mesh):
    placed = (P("gy", "gx"), P(), P(("gx", "gy")), P(("gx", "gy")), P(None, ("gx", "gy")))
    return jax.shard_map(
        on_device,
        mesh=mesh,
        in_specs=placed,
        out_specs=(P(None, "gy", "gx"), P(("gx", "gy"))),
        check_vma=False,
    )
```

time: 32.6 us -> 35.1 us (1.077)
  waiting for transfers between devices: 8.51 us -> 1.3 us
  local copies, waits for them, and re-layouts: 0 us -> 5.71 us
  Pallas kernels: 15.6 us -> 19.3 us
    unnamed x0 -> x12, local copies, waits for them, and re-layouts: none -> 5.71 us
    ppermute x2, waiting for transfers between devices: 5.42 us -> 1.3 us  [shift(): lax.ppermute(value, axis, [(i, (i + steps) % count) for i in range(count)])]
    pallas_call x2 -> x4, Pallas kernels: 14.4 us -> 17.5 us  [the longest x1 10.3 us: on_device(): pl.pallas_call(bind(sweep_kernel), in_specs=[vmem] * 7, out_specs=[pl.Blo...]
    ppermute x2, waiting for transfers between devices: 3.1 us -> 0.01 us  [swap(): lax.ppermute(value, axis, [(i, (i + (1 if i % 2 == parity else -1)) % cou...]
    pallas_call x1, Pallas kernels: 1.18 us -> 1.8 us  [on_device(): pl.pallas_call(bind(across_kernel), in_specs=[vmem] * 4, out_specs=[vmem]...]
  transfers between devices with their start and end apart: 4 -> 4, of which waited for: 3 -> 2; matrix products, arithmetic and copies ran while one was open for 0% -> 0% of each run, Pallas kernels for 0% -> 15%
where the time goes in v4:
time: 35.1 us; the launch traced here: 34.8 us
  Pallas kernels  19.3 us (55%)
  starting transfers between devices  7.76 us (22%)
  local copies, waits for them, and re-layouts  5.71 us (16%)
  waiting for transfers between devices  1.3 us (4%)
  between operations  0.67 us (2%)
    pallas_call x1, Pallas kernels, on_device(): pl.pallas_call(bind(sweep_kernel), in_specs=[vmem] * 7, out_specs=[pl.Blo...  10.3 us
    ppermute x2, starting transfers between devices, shift(): lax.ppermute(value, axis, [(i, (i + steps) % count) for i in range(count)])  6.12 us
    unnamed x12, local copies, waits for them, and re-layouts  5.71 us
    pallas_call x1, Pallas kernels, on_device(): pl.pallas_call(bind(rewards_kernel), in_specs=[vmem] * 5, out_specs=[vmem...  3.3 us
    pallas_call x1, Pallas kernels, on_device(): pl.pallas_call(bind(local_kernel), in_specs=[vmem] * 4, out_specs=[vmem]...  2.04 us
    pallas_call x1, Pallas kernels, on_device(): pl.pallas_call(bind(bands_kernel), in_specs=[vmem] * 3, out_specs=[vmem]...  1.91 us
    pallas_call x1, Pallas kernels, on_device(): pl.pallas_call(bind(across_kernel), in_specs=[vmem] * 4, out_specs=[vmem]...  1.8 us
    ppermute x2, starting transfers between devices, swap(): lax.ppermute(value, axis, [(i, (i + (1 if i % 2 == parity else -1)) % cou...  1.63 us
  transfers between devices with their start and end apart: 4, of which 2 were waited for; matrix products, arithmetic and copies ran while one was open for 0% of the time, Pallas kernels for 15%

profile of v4, /device:TPU:0, one launch (start us, length us, event | category | flops | bytes accessed | tf_op | source)
XLA Modules:
  0.0 34.8 jit_solution(13920900593108495864)
XLA Ops:
  0.6 1.9 %bands.1 = (f32[176,128]{1,0:T(8,128)S(1)}, f32[176,128]{1,0:T(8,128)S(1)}, s32[16,128]{1,0:T(8,128)S(1)}, s32[16,128]{1,0:T(8,128)S(1)}) custom-call(s32[16,2048]{1,0:T(8,128)} %refs_0_.1, s32[16,128]{1,0:T(8,128)} %bitcast.3, s32[256,256]{1,0:T(8,128)} %refs_1_.3), custom_call_target="tpu_custom_call" | custom-call | tf_op jit(solution)/shard_map/bands/pallas_call | solution.py:445
  2.5 3.0 %collective-permute-start = (f32[176,128]{1,0:T(8,128)S(1)}, f32[176,128]{1,0:T(8,128)S(1)}, u32[]{:S(2)}, u32[]{:S(2)}) collective-permute-start(f32[176,128]{1,0:T(8,128)S(1)} %get-tuple-element.20), channel_id=1, source_target_pairs={{0,4},{4,8},{8,12},{12,16},{16,20},{20,24},{24,28},{28,0},{1,5},{5... | collective-permute-start | bytes 270344 | tf_op jit(solution)/shard_map/ppermute | solution.py:415
  5.6 3.1 %collective-permute-start.1 = (f32[176,128]{1,0:T(8,128)S(1)}, f32[176,128]{1,0:T(8,128)S(1)}, u32[]{:S(2)}, u32[]{:S(2)}) collective-permute-start(f32[176,128]{1,0:T(8,128)S(1)} %get-tuple-element.21), channel_id=1, source_target_pairs={{0,28},{4,0},{8,4},{12,8},{16,12},{20,16},{24,20},{28,24},{1,29},{... | collective-permute-start | bytes 270344 | tf_op jit(solution)/shard_map/ppermute | solution.py:415
  8.7 2.0 %local.1 = (f32[3,320,128]{2,1,0:T(8,128)S(1)}, s32[16,128]{1,0:T(8,128)S(1)}, s32[16,128]{1,0:T(8,128)S(1)}, f32[8,128]{1,0:T(8,128)S(1)}) custom-call(s32[16,128]{1,0:T(8,128)S(1)} %get-tuple-element.16.refs_0_, s32[16,128]{1,0:T(8,128)S(1)} %get-tuple-element.17.refs_1_, s32[16,128]{1,0:T(8,128)} %bitcast.4, f32[4,64]{1,0:T(4,128)} %refs_3_.1), custom_call_target="tpu_custom_call" | custom-call | tf_op jit(solution)/shard_map/local/pallas_call | solution.py:463
  10.7 0.0 copy-start.2
  10.7 0.6 %collective-permute-done.refs_2_ = f32[176,128]{1,0:T(8,128)S(1)} collective-permute-done((f32[176,128]{1,0:T(8,128)S(1)}, f32[176,128]{1,0:T(8,128)S(1)}, u32[]{:S(2)}, u32[]{:S(2)}) %collective-permute-start) | collective-permute-done | bytes 90144 | tf_op jit(solution)/shard_map/ppermute | solution.py:415
  11.3 0.7 %collective-permute-done.1.refs_3_ = f32[176,128]{1,0:T(8,128)S(1)} collective-permute-done((f32[176,128]{1,0:T(8,128)S(1)}, f32[176,128]{1,0:T(8,128)S(1)}, u32[]{:S(2)}, u32[]{:S(2)}) %collective-permute-start.1) | collective-permute-done | bytes 90144 | tf_op jit(solution)/shard_map/ppermute | solution.py:415
  12.0 1.8 %across.1 = (f32[208,128]{1,0:T(8,128)}, f32[208,128]{1,0:T(8,128)}) custom-call(f32[3,320,128]{2,1,0:T(8,128)S(1)} %get-tuple-element.19.refs_0_, s32[256,256]{1,0:T(8,128)} %refs_1_.3, f32[176,128]{1,0:T(8,128)S(1)} %collective-permute-done.refs_2_, f32[176,128]{1,0:T(8,128)S(1)} %collective-permute-done.1.refs_3_), custom_call_target="tpu_custom_call" | custom-call | tf_op jit(solution)/shard_map/across/pallas_call | solution.py:480
  13.8 0.0 collective-permute-start.2
  13.8 1.6 %collective-permute-start.3 = (f32[208,128]{1,0:T(8,128)}, f32[208,128]{1,0:T(8,128)S(1)}, u32[]{:S(2)}, u32[]{:S(2)}) collective-permute-start(f32[208,128]{1,0:T(8,128)} %get-tuple-element.25), channel_id=1, source_target_pairs={{0,3},{1,2},{2,1},{3,0},{4,7},{5,6},{6,5},{7,4},{8,11},{9,10},{10,... | collective-permute-start | bytes 319496 | tf_op jit(solution)/shard_map/ppermute | solution.py:421
  15.5 0.0 copy-done.2
  15.5 0.0 copy-start.3
  15.5 1.0 %copy-done.3 = f32[3,320,128]{2,1,0:T(8,128)S(1)} copy-done((f32[3,320,128]{2,1,0:T(8,128)S(1)}, f32[3,320,128]{2,1,0:T(8,128)}, u32[]{:S(2)}) %copy-start.3) | copy-done | bytes 491544
  16.5 3.3 %rewards.1 = (f32[15,320,128]{2,1,0:T(8,128)S(1)}, f32[3,32,128]{2,1,0:T(8,128)S(1)}) custom-call(f32[3,320,128]{2,1,0:T(8,128)S(1)} %copy-done.3, s32[256,256]{1,0:T(8,128)} %refs_1_.3, f32[176,128]{1,0:T(8,128)S(1)} %collective-permute-done.refs_2_, f32[176,128]{1,0:T(8,128)S(1)} %collective-permute-done.1.refs_3_, ...), custom_call_target="tpu_custom_call" | custom-call | tf_op jit(solution)/shard_map/rewards/pallas_call | solution.py:490
  19.8 0.0 copy-start
  19.8 1.4 %copy-done = f32[15,320,128]{2,1,0:T(8,128)} copy-done((f32[15,320,128]{2,1,0:T(8,128)}, f32[15,320,128]{2,1,0:T(8,128)S(1)}, u32[]{:S(2)}) %copy-start) | copy-done | bytes 2457624
  21.2 0.0 collective-permute-done.2.refs_3_
  21.3 0.0 collective-permute-done.3.refs_4_
  21.3 0.0 copy-start.4
  21.3 0.6 %copy-done.4 = f32[208,128]{1,0:T(8,128)} copy-done((f32[208,128]{1,0:T(8,128)}, f32[208,128]{1,0:T(8,128)S(1)}, u32[]{:S(2)}) %copy-start.4) | copy-done | bytes 106520
  21.9 0.0 copy-start.1
  21.9 1.7 %copy-done.1 = f32[15,320,128]{2,1,0:T(8,128)S(1)} copy-done((f32[15,320,128]{2,1,0:T(8,128)S(1)}, f32[15,320,128]{2,1,0:T(8,128)}, u32[]{:S(2)}) %copy-start.1) | copy-done | bytes 2457624
  23.6 0.0 copy-start.5
  23.6 0.9 %copy-done.5 = f32[208,128]{1,0:T(8,128)S(1)} copy-done((f32[208,128]{1,0:T(8,128)S(1)}, f32[208,128]{1,0:T(8,128)}, u32[]{:S(2)}) %copy-start.5) | copy-done | bytes 106520
  24.5 10.3 %sweep.1 = (f32[4,256,256]{2,1,0:T(8,128)}, f32[16,128]{1,0:T(8,128)}, f32[15,320,128]{2,1,0:T(8,128)S(1)}) custom-call(f32[8,128]{1,0:T(8,128)S(1)} %get-tuple-element.18.refs_4_.refs_0_, f32[15,320,128]{2,1,0:T(8,128)S(1)} %copy-done.1, f32[3,32,128]{2,1,0:T(8,128)S(1)} %get-tuple-element.23.refs_2_, ...), custom_call_target="tpu_custom_call", output_to_operand_aliasing={{2}: (1, {})} | custom-call | tf_op jit(solution)/shard_map/sweep/pallas_call | solution.py:498
Async XLA Ops:
  2.5 8.8 %collective-permute-start = (f32[176,128]{1,0:T(8,128)S(1)}, f32[176,128]{1,0:T(8,128)S(1)}, u32[]{:S(2)}, u32[]{:S(2)}) collective-permute-start(f32[176,128]{1,0:T(8,128)S(1)} %get-tuple-element.20), channel_id=1, source_target_pairs={{0,4},{4,8},{8,12},{12,16},{16,20},{20,24},{24,28},{28,0},{1,5},{5... | collective-permute-start | bytes 270344 | tf_op jit(solution)/shard_map/ppermute | solution.py:415
  5.6 6.5 %collective-permute-start.1 = (f32[176,128]{1,0:T(8,128)S(1)}, f32[176,128]{1,0:T(8,128)S(1)}, u32[]{:S(2)}, u32[]{:S(2)}) collective-permute-start(f32[176,128]{1,0:T(8,128)S(1)} %get-tuple-element.21), channel_id=1, source_target_pairs={{0,28},{4,0},{8,4},{12,8},{16,12},{20,16},{24,20},{28,24},{1,29},{... | collective-permute-start | bytes 270344 | tf_op jit(solution)/shard_map/ppermute | solution.py:415
  10.7 4.7 %copy-start.2 = (f32[3,320,128]{2,1,0:T(8,128)}, f32[3,320,128]{2,1,0:T(8,128)S(1)}, u32[]{:S(2)}) copy-start(f32[3,320,128]{2,1,0:T(8,128)S(1)} %get-tuple-element.19.refs_0_) | copy-start | bytes 1474564
  13.8 7.4 %collective-permute-start.2 = (f32[208,128]{1,0:T(8,128)}, f32[208,128]{1,0:T(8,128)S(1)}, u32[]{:S(2)}, u32[]{:S(2)}) collective-permute-start(f32[208,128]{1,0:T(8,128)} %get-tuple-element.24), channel_id=1, source_target_pairs={{0,1},{1,0},{2,3},{3,2},{4,5},{5,4},{6,7},{7,6},{8,9},{9,8},{10,11... | collective-permute-start | bytes 319496 | tf_op jit(solution)/shard_map/ppermute | solution.py:421
  13.8 7.4 %collective-permute-start.3 = (f32[208,128]{1,0:T(8,128)}, f32[208,128]{1,0:T(8,128)S(1)}, u32[]{:S(2)}, u32[]{:S(2)}) collective-permute-start(f32[208,128]{1,0:T(8,128)} %get-tuple-element.25), channel_id=1, source_target_pairs={{0,3},{1,2},{2,1},{3,0},{4,7},{5,6},{6,5},{7,4},{8,11},{9,10},{10,... | collective-permute-start | bytes 319496 | tf_op jit(solution)/shard_map/ppermute | solution.py:421
  15.5 1.0 %copy-start.3 = (f32[3,320,128]{2,1,0:T(8,128)S(1)}, f32[3,320,128]{2,1,0:T(8,128)}, u32[]{:S(2)}) copy-start(f32[3,320,128]{2,1,0:T(8,128)} %copy-done.2) | copy-start | bytes 1474564
  19.8 1.5 %copy-start = (f32[15,320,128]{2,1,0:T(8,128)}, f32[15,320,128]{2,1,0:T(8,128)S(1)}, u32[]{:S(2)}) copy-start(f32[15,320,128]{2,1,0:T(8,128)S(1)} %get-tuple-element.22.refs_1_) | copy-start | bytes 7372804
  21.3 0.6 %copy-start.4 = (f32[208,128]{1,0:T(8,128)}, f32[208,128]{1,0:T(8,128)S(1)}, u32[]{:S(2)}) copy-start(f32[208,128]{1,0:T(8,128)S(1)} %collective-permute-done.3.refs_4_) | copy-start | bytes 319492
  21.9 1.7 %copy-start.1 = (f32[15,320,128]{2,1,0:T(8,128)S(1)}, f32[15,320,128]{2,1,0:T(8,128)}, u32[]{:S(2)}) copy-start(f32[15,320,128]{2,1,0:T(8,128)} %copy-done) | copy-start | bytes 7372804
  23.6 0.9 %copy-start.5 = (f32[208,128]{1,0:T(8,128)S(1)}, f32[208,128]{1,0:T(8,128)}, u32[]{:S(2)}) copy-start(f32[208,128]{1,0:T(8,128)} %copy-done.4) | copy-start | bytes 319492

commit v5 on v4

--- a/solution.py
+++ b/solution.py
@@ -139,7 +139,9 @@
         out[pl.ds(p.half, p.pack), :] = rest
 
 
-def local_kernel(plan, ring_row, ring_col, task, table, hist, address, lane_out, looked, row_hot, col_hot):
+def local_kernel(
+    plan, ring_row, ring_col, task, table, code, hist, address, lane_out, looked, code_out, row_hot, col_hot
+):
     p = plan
     ring_cols = p.tiles * LANES
     row_id = lax.broadcasted_iota(jnp.int32, (p.ring, LANES), 0)
@@ -161,6 +163,7 @@
     counts = counted(row_hot, col_hot)
     for t in range(p.tiles):
         hist[t] = counts[:, t * LANES : (t + 1) * LANES]
+    code_out[...] = code[...].astype(jnp.float32)
     looked[...] = jnp.zeros_like(looked)
     looked[pl.ds(0, p.tasks), pl.ds(0, p.codes)] = table[...]
 
@@ -212,7 +215,7 @@
 def merged_codes(p, code, from_left, from_right, row, n):
     last = p.tiles - 1
     lane = lane_of((n, LANES))
-    out = [code[pl.ds(row, n), pl.ds(t * LANES, LANES)].astype(jnp.float32) for t in range(last)]
+    out = [code[pl.ds(row, n), pl.ds(t * LANES, LANES)] for t in range(last)]
     l = side_codes(p, from_left, right_roll, row, n)
     r = side_codes(p, from_right, left_roll, row, n)
     out.append(jnp.where(lane >= LANES - p.wide, l, jnp.where(lane < p.wide, r, 0.0)))
@@ -456,32 +459,36 @@
             pltpu.VMEM((p.message, agents), jnp.bfloat16),
             pltpu.VMEM((2 * LANES, agents), jnp.bfloat16),
         ],
+        compiler_params=pltpu.CompilerParams(vmem_limit_bytes=12 << 20),
         name="bands",
     )(actions, start_cell.reshape(by_lane), map_codes)
     from_left = shift(to_right, "gx", 1)
     from_right = shift(to_left, "gx", -1)
-    hist, address, lane, looked = pl.pallas_call(
+    hist, address, lane, looked, kept = pl.pallas_call(
         bind(local_kernel),
-        in_specs=[vmem] * 4,
-        out_specs=[vmem] * 4,
+        in_specs=[vmem] * 5,
+        out_specs=[vmem] * 5,
         out_shape=[
             fast((p.tiles, p.ring, LANES), f32),
             fast(by_lane, i32),
             fast(by_lane, i32),
             fast((SUB, LANES), f32),
+            fast((rows, cols), f32),
         ],
         scratch_shapes=[
             pltpu.VMEM((p.ring, agents), jnp.bfloat16),
             pltpu.VMEM((p.tiles * LANES, agents), jnp.bfloat16),
         ],
+        compiler_params=pltpu.CompilerParams(vmem_limit_bytes=12 << 20),
         name="local",
-    )(near(ring_row), near(ring_col), agent_task.reshape(by_lane), reward_table)
-    sides = (near(hist), map_codes, near(from_left), near(from_right))
+    )(near(ring_row), near(ring_col), agent_task.reshape(by_lane), reward_table, map_codes)
+    sides = (near(hist), near(kept), near(from_left), near(from_right))
     first, second = pl.pallas_call(
         bind(across_kernel),
         in_specs=[vmem] * 4,
         out_specs=[vmem] * 2,
         out_shape=[fast((p.down_rows, LANES), f32), fast((p.down_rows, LANES), f32)],
+        compiler_params=pltpu.CompilerParams(vmem_limit_bytes=8 << 20),
         name="across",
     )(*sides)
     first = swap(first, "gy", 0)
@@ -492,6 +499,7 @@
         in_specs=[vmem] * 5,
         out_specs=[vmem] * 2,
         out_shape=[fast(flats, f32), fast((p.tiles, 2 * p.near, LANES), f32)],
+        compiler_params=pltpu.CompilerParams(vmem_limit_bytes=12 << 20),
         name="rewards",
     )(*sides, near(looked))
     outs = tasks * (p.tiles - 1)
@@ -513,6 +521,7 @@
             pltpu.SemaphoreType.DMA((outs + 1,)),
         ],
         input_output_aliases={1: 2},
+        compiler_params=pltpu.CompilerParams(vmem_limit_bytes=24 << 20),
         name="sweep",
     )(near(looked), near(flat), near(edges), near(first), near(second), near(address), near(lane))
     return values, answers.reshape(agents)

time: 35.1 us -> 29.4 us (0.84)
  Pallas kernels: 19.3 us -> 15.1 us
  local copies, waits for them, and re-layouts: 5.71 us -> 4.87 us
  waiting for transfers between devices: 1.3 us -> 0.61 us
    pallas_call x1, Pallas kernels: 1.8 us -> 0.15 us  [on_device(): pl.pallas_call(bind(across_kernel), in_specs=[vmem] * 4, out_specs=[vmem]...]
    ppermute x2, waiting for transfers between devices: 1.3 us -> 0.01 us  [shift(): lax.ppermute(value, axis, [(i, (i + steps) % count) for i in range(count)])]
    pallas_call x1, Pallas kernels: 1.91 us -> 0.89 us  [on_device(): pl.pallas_call(bind(bands_kernel), in_specs=[vmem] * 3, out_specs=[vmem]...]
    pallas_call x1, Pallas kernels: 3.3 us -> 2.36 us  [on_device(): pl.pallas_call(bind(rewards_kernel), in_specs=[vmem] * 5, out_specs=[vmem...]
    unnamed x12, local copies, waits for them, and re-layouts: 5.71 us -> 4.87 us
    pallas_call x1, Pallas kernels: 2.04 us -> 1.36 us  [on_device(): pl.pallas_call(bind(local_kernel), in_specs=[vmem] * 5, out_specs=[vmem]...]
    ppermute x2, waiting for transfers between devices: 0.01 us -> 0.6 us  [swap(): lax.ppermute(value, axis, [(i, (i + (1 if i % 2 == parity else -1)) % cou...]
  transfers between devices with their start and end apart: 4 -> 4, of which waited for: 2 -> 1; matrix products, arithmetic and copies ran while one was open for 0% -> 0% of each run, Pallas kernels for 15% -> 13%
where the time goes in v5:
time: 29.4 us; the launch traced here: 29.1 us
  Pallas kernels  15.1 us (51%)
  starting transfers between devices  7.92 us (27%)
  local copies, waits for them, and re-layouts  4.87 us (17%)
  between operations  0.69 us (2%)
  waiting for transfers between devices  0.61 us (2%)
    pallas_call x1, Pallas kernels, on_device(): pl.pallas_call(bind(sweep_kernel), in_specs=[vmem] * 7, out_specs=[pl.Blo...  10.3 us
    ppermute x2, starting transfers between devices, shift(): lax.ppermute(value, axis, [(i, (i + steps) % count) for i in range(count)])  6.12 us
    unnamed x12, local copies, waits for them, and re-layouts  4.87 us
    pallas_call x1, Pallas kernels, on_device(): pl.pallas_call(bind(rewards_kernel), in_specs=[vmem] * 5, out_specs=[vmem...  2.36 us
    ppermute x2, starting transfers between devices, swap(): lax.ppermute(value, axis, [(i, (i + (1 if i % 2 == parity else -1)) % cou...  1.79 us
    pallas_call x1, Pallas kernels, on_device(): pl.pallas_call(bind(local_kernel), in_specs=[vmem] * 5, out_specs=[vmem]...  1.36 us
    pallas_call x1, Pallas kernels, on_device(): pl.pallas_call(bind(bands_kernel), in_specs=[vmem] * 3, out_specs=[vmem]...  0.89 us
    ppermute x2, waiting for transfers between devices, swap(): lax.ppermute(value, axis, [(i, (i + (1 if i % 2 == parity else -1)) % cou...  0.6 us
  transfers between devices with their start and end apart: 4, of which 1 were waited for; matrix products, arithmetic and copies ran while one was open for 0% of the time, Pallas kernels for 13%

profile of v5, /device:TPU:0, one launch (start us, length us, event | category | flops | bytes accessed | tf_op | source)
XLA Modules:
  0.0 29.1 jit_solution(12873097085675935888)
XLA Ops:
  0.6 0.0 copy-start
  0.6 0.9 %copy-done = s32[256,256]{1,0:T(8,128)S(1)} copy-done((s32[256,256]{1,0:T(8,128)S(1)}, s32[256,256]{1,0:T(8,128)}, u32[]{:S(2)}) %copy-start) | copy-done | bytes 262168
  1.6 0.0 copy-start.2
  1.6 0.9 %copy-done.2 = s32[16,2048]{1,0:T(8,128)S(1)} copy-done((s32[16,2048]{1,0:T(8,128)S(1)}, s32[16,2048]{1,0:T(8,128)}, u32[]{:S(2)}) %copy-start.2) | copy-done | bytes 131096
  2.5 0.0 copy-start.3
  2.5 0.7 %copy-done.3 = s32[2048]{0:T(1024)S(1)} copy-done((s32[2048]{0:T(1024)S(1)}, s32[2048]{0:T(1024)}, u32[]{:S(2)}) %copy-start.3) | copy-done | bytes 8216
  3.2 0.9 %bands.1 = (f32[176,128]{1,0:T(8,128)S(1)}, f32[176,128]{1,0:T(8,128)S(1)}, s32[16,128]{1,0:T(8,128)S(1)}, s32[16,128]{1,0:T(8,128)S(1)}) custom-call(s32[16,2048]{1,0:T(8,128)S(1)} %copy-done.2, s32[16,128]{1,0:T(8,128)S(1)} %bitcast.3, s32[256,256]{1,0:T(8,128)S(1)} %copy-done), custom_call_target="tpu_custom_call" | custom-call | tf_op jit(solution)/shard_map/bands/pallas_call | solution.py:448
  4.1 3.0 %collective-permute-start = (f32[176,128]{1,0:T(8,128)S(1)}, f32[176,128]{1,0:T(8,128)S(1)}, u32[]{:S(2)}, u32[]{:S(2)}) collective-permute-start(f32[176,128]{1,0:T(8,128)S(1)} %get-tuple-element.22), channel_id=1, source_target_pairs={{0,4},{4,8},{8,12},{12,16},{16,20},{20,24},{24,28},{28,0},{1,5},{5... | collective-permute-start | bytes 270344 | tf_op jit(solution)/shard_map/ppermute | solution.py:418
  7.1 3.1 %collective-permute-start.1 = (f32[176,128]{1,0:T(8,128)S(1)}, f32[176,128]{1,0:T(8,128)S(1)}, u32[]{:S(2)}, u32[]{:S(2)}) collective-permute-start(f32[176,128]{1,0:T(8,128)S(1)} %get-tuple-element.23), channel_id=1, source_target_pairs={{0,28},{4,0},{8,4},{12,8},{16,12},{20,16},{24,20},{28,24},{1,29},{... | collective-permute-start | bytes 270344 | tf_op jit(solution)/shard_map/ppermute | solution.py:418
  10.2 0.0 copy-start.1
  10.2 0.9 %copy-done.1 = s32[256,256]{1,0:T(8,128)S(1)} copy-done((s32[256,256]{1,0:T(8,128)S(1)}, s32[256,256]{1,0:T(8,128)}, u32[]{:S(2)}) %copy-start.1) | copy-done | bytes 262168
  11.2 0.0 copy-start.4
  11.2 0.7 %copy-done.4 = s32[2048]{0:T(1024)S(1)} copy-done((s32[2048]{0:T(1024)S(1)}, s32[2048]{0:T(1024)}, u32[]{:S(2)}) %copy-start.4) | copy-done | bytes 8216
  11.9 0.0 copy-start.5
  11.9 0.7 %copy-done.5 = f32[4,64]{1,0:T(4,128)S(1)} copy-done((f32[4,64]{1,0:T(4,128)S(1)}, f32[4,64]{1,0:T(4,128)}, u32[]{:S(2)}) %copy-start.5) | copy-done | bytes 1048
  12.5 1.4 %local.1 = (f32[3,320,128]{2,1,0:T(8,128)S(1)}, s32[16,128]{1,0:T(8,128)S(1)}, s32[16,128]{1,0:T(8,128)S(1)}, f32[8,128]{1,0:T(8,128)S(1)}, f32[256,256]{1,0:T(8,128)S(1)}) custom-call(s32[16,128]{1,0:T(8,128)S(1)} %get-tuple-element.17.refs_0_, s32[16,128]{1,0:T(8,128)S(1)} %get-tuple-element.18.refs_1_, s32[16,128]{1,0:T(8,128)S(1)} %bitcast.4, ...), custom_call_target="tpu_custom_call" | custom-call | tf_op jit(solution)/shard_map/local/pallas_call | solution.py:467
  13.9 0.0 collective-permute-done.refs_2_
  13.9 0.0 collective-permute-done.1.refs_3_
  13.9 0.2 across.1
  14.1 0.0 collective-permute-start.2
  14.1 1.8 %collective-permute-start.3 = (f32[208,128]{1,0:T(8,128)S(1)}, f32[208,128]{1,0:T(8,128)S(1)}, u32[]{:S(2)}, u32[]{:S(2)}) collective-permute-start(f32[208,128]{1,0:T(8,128)S(1)} %get-tuple-element.27), channel_id=1, source_target_pairs={{0,3},{1,2},{2,1},{3,0},{4,7},{5,6},{6,5},{7,4},{8,11},{9,10},{10,... | collective-permute-start | bytes 319496 | tf_op jit(solution)/shard_map/ppermute | solution.py:424
  15.9 2.4 %rewards.1 = (f32[15,320,128]{2,1,0:T(8,128)S(1)}, f32[3,32,128]{2,1,0:T(8,128)S(1)}) custom-call(f32[3,320,128]{2,1,0:T(8,128)S(1)} %get-tuple-element.20.refs_0_, f32[256,256]{1,0:T(8,128)S(1)} %get-tuple-element.21.refs_1_, f32[176,128]{1,0:T(8,128)S(1)} %collective-permute-done.refs_2_, f32[176,128]{1,0:T(8,128)S(1)} %collective-permute-done.1.refs_3_, ...), custom_call_target="tpu_custom_call" | custom-call | tf_op jit(solution)/shard_map/rewards/pallas_call | solution.py:497
  18.2 0.0 collective-permute-done.2.refs_3_
  18.2 0.6 %collective-permute-done.3.refs_4_ = f32[208,128]{1,0:T(8,128)S(1)} collective-permute-done((f32[208,128]{1,0:T(8,128)S(1)}, f32[208,128]{1,0:T(8,128)S(1)}, u32[]{:S(2)}, u32[]{:S(2)}) %collective-permute-start.3) | collective-permute-done | bytes 106528 | tf_op jit(solution)/shard_map/ppermute | solution.py:424
  18.9 10.3 %sweep.1 = (f32[4,256,256]{2,1,0:T(8,128)}, f32[16,128]{1,0:T(8,128)}, f32[15,320,128]{2,1,0:T(8,128)S(1)}) custom-call(f32[8,128]{1,0:T(8,128)S(1)} %get-tuple-element.19.refs_4_.refs_0_, f32[15,320,128]{2,1,0:T(8,128)S(1)} %get-tuple-element.24.refs_1_, f32[3,32,128]{2,1,0:T(8,128)S(1)} %get-tuple-element.25.refs_2_, ...), custom_call_target="tpu_custom_call", output_to_operand_aliasing={{2}: (1, {})} | custom-call | tf_op jit(solution)/shard_map/sweep/pallas_call | solution.py:506
Async XLA Ops:
  0.6 1.0 %copy-start = (s32[256,256]{1,0:T(8,128)S(1)}, s32[256,256]{1,0:T(8,128)}, u32[]{:S(2)}) copy-start(s32[256,256]{1,0:T(8,128)} %refs_4_.1) | copy-start | bytes 786436
  1.6 0.9 %copy-start.2 = (s32[16,2048]{1,0:T(8,128)S(1)}, s32[16,2048]{1,0:T(8,128)}, u32[]{:S(2)}) copy-start(s32[16,2048]{1,0:T(8,128)} %refs_0_.1) | copy-start | bytes 393220
  2.5 0.7 %copy-start.3 = (s32[2048]{0:T(1024)S(1)}, s32[2048]{0:T(1024)}, u32[]{:S(2)}) copy-start(s32[2048]{0:T(1024)} %param.7) | copy-start | bytes 24580
  4.1 9.8 %collective-permute-start = (f32[176,128]{1,0:T(8,128)S(1)}, f32[176,128]{1,0:T(8,128)S(1)}, u32[]{:S(2)}, u32[]{:S(2)}) collective-permute-start(f32[176,128]{1,0:T(8,128)S(1)} %get-tuple-element.22), channel_id=1, source_target_pairs={{0,4},{4,8},{8,12},{12,16},{16,20},{20,24},{24,28},{28,0},{1,5},{5... | collective-permute-start | bytes 270344 | tf_op jit(solution)/shard_map/ppermute | solution.py:418
  7.1 6.8 %collective-permute-start.1 = (f32[176,128]{1,0:T(8,128)S(1)}, f32[176,128]{1,0:T(8,128)S(1)}, u32[]{:S(2)}, u32[]{:S(2)}) collective-permute-start(f32[176,128]{1,0:T(8,128)S(1)} %get-tuple-element.23), channel_id=1, source_target_pairs={{0,28},{4,0},{8,4},{12,8},{16,12},{20,16},{24,20},{28,24},{1,29},{... | collective-permute-start | bytes 270344 | tf_op jit(solution)/shard_map/ppermute | solution.py:418
  10.2 0.9 %copy-start.1 = (s32[256,256]{1,0:T(8,128)S(1)}, s32[256,256]{1,0:T(8,128)}, u32[]{:S(2)}) copy-start(s32[256,256]{1,0:T(8,128)} %refs_4_.1) | copy-start | bytes 786436
  11.2 0.7 %copy-start.4 = (s32[2048]{0:T(1024)S(1)}, s32[2048]{0:T(1024)}, u32[]{:S(2)}) copy-start(s32[2048]{0:T(1024)} %param.8) | copy-start | bytes 24580
  11.9 0.7 %copy-start.5 = (f32[4,64]{1,0:T(4,128)S(1)}, f32[4,64]{1,0:T(4,128)}, u32[]{:S(2)}) copy-start(f32[4,64]{1,0:T(4,128)} %refs_3_.1) | copy-start | bytes 3076
  14.1 4.2 %collective-permute-start.2 = (f32[208,128]{1,0:T(8,128)S(1)}, f32[208,128]{1,0:T(8,128)S(1)}, u32[]{:S(2)}, u32[]{:S(2)}) collective-permute-start(f32[208,128]{1,0:T(8,128)S(1)} %get-tuple-element.26), channel_id=1, source_target_pairs={{0,1},{1,0},{2,3},{3,2},{4,5},{5,4},{6,7},{7,6},{8,9},{9,8},{10,11... | collective-permute-start | bytes 319496 | tf_op jit(solution)/shard_map/ppermute | solution.py:424
  14.1 4.7 %collective-permute-start.3 = (f32[208,128]{1,0:T(8,128)S(1)}, f32[208,128]{1,0:T(8,128)S(1)}, u32[]{:S(2)}, u32[]{:S(2)}) collective-permute-start(f32[208,128]{1,0:T(8,128)S(1)} %get-tuple-element.27), channel_id=1, source_target_pairs={{0,3},{1,2},{2,1},{3,0},{4,7},{5,6},{6,5},{7,4},{8,11},{9,10},{10,... | collective-permute-start | bytes 319496 | tf_op jit(solution)/shard_map/ppermute | solution.py:424

commit v6 on v4

--- a/solution.py
+++ b/solution.py
@@ -80,8 +80,15 @@
     return x if amount == 0 else pltpu.roll(x, amount, 1)
 
 
-def bands_kernel(plan, act, start, code, right, left, ring_row, ring_col, row_hot, col_hot):
+def bands_kernel(
+    plan, act_in, start_in, code_in, task_in, table_in,
+    right, left, ring_row, ring_col, code, task, table, act, start, row_hot, col_hot, sems,
+):
     p = plan
+    pairs = ((act_in, act), (start_in, start), (code_in, code), (task_in, task), (table_in, table))
+    copies = [pltpu.make_async_copy(src, dst, sems.at[n]) for n, (src, dst) in enumerate(pairs)]
+    for copy in copies:
+        copy.start()
     last = p.tiles - 1
     ring_cols = p.tiles * LANES
     row_id = lax.broadcasted_iota(jnp.int32, (p.message, LANES), 0)
@@ -97,6 +104,8 @@
         if at > blank:
             col_hot[blank:at, :] = jnp.zeros((at - blank, p.agents), jnp.bfloat16)
         blank = at + n
+    copies[0].wait()
+    copies[1].wait()
     for i in range(p.agents // LANES):
         here = slice(i * LANES, (i + 1) * LANES)
         a = act[:, here]
@@ -113,6 +122,8 @@
             ids = first + lax.broadcasted_iota(jnp.int32, (n, LANES), 0)
             col_hot[at : at + n, here] = one_hot(ids, col)
     counts = counted(row_hot, col_hot)
+    for copy in copies[2:]:
+        copy.wait()
     lane = lane_of((p.half, LANES))
     for out, side, spare, shift, band in (
         (right, 0, p.near, right_roll, code[:, (last - 1) * LANES :]),
@@ -139,7 +150,9 @@
         out[pl.ds(p.half, p.pack), :] = rest
 
 
-def local_kernel(plan, ring_row, ring_col, task, table, hist, address, lane_out, looked, row_hot, col_hot):
+def local_kernel(
+    plan, ring_row, ring_col, task, table, hist, address, lane_out, looked, row_hot, col_hot
+):
     p = plan
     ring_cols = p.tiles * LANES
     row_id = lax.broadcasted_iota(jnp.int32, (p.ring, LANES), 0)
@@ -433,6 +446,7 @@
     f32, i32 = jnp.float32, jnp.int32
     shape = jax.ShapeDtypeStruct
     fast = lambda dims, dtype: pltpu.VMEM(dims, dtype)
+    far = lambda x: pltpu.with_memory_space_constraint(x, pltpu.HBM)
     near = lambda x: pltpu.with_memory_space_constraint(x, pltpu.VMEM)
     by_lane = (agents // LANES, LANES)
 
@@ -442,22 +456,29 @@
 
         return body
 
-    to_right, to_left, ring_row, ring_col = pl.pallas_call(
+    to_right, to_left, ring_row, ring_col, kept, task, table = pl.pallas_call(
         bind(bands_kernel),
-        in_specs=[vmem] * 3,
-        out_specs=[vmem] * 4,
+        in_specs=[pl.BlockSpec(memory_space=pl.ANY)] * 5,
+        out_specs=[vmem] * 7,
         out_shape=[
             fast((p.across_rows, LANES), f32),
             fast((p.across_rows, LANES), f32),
             fast(by_lane, i32),
             fast(by_lane, i32),
+            fast((rows, cols), i32),
+            fast(by_lane, i32),
+            fast((tasks, codes), f32),
         ],
         scratch_shapes=[
+            pltpu.VMEM((steps, agents), i32),
+            pltpu.VMEM(by_lane, i32),
             pltpu.VMEM((p.message, agents), jnp.bfloat16),
             pltpu.VMEM((2 * LANES, agents), jnp.bfloat16),
+            pltpu.SemaphoreType.DMA((5,)),
         ],
+        compiler_params=pltpu.CompilerParams(vmem_limit_bytes=12 << 20),
         name="bands",
-    )(actions, start_cell.reshape(by_lane), map_codes)
+    )(*map(far, (actions, start_cell.reshape(by_lane), map_codes, agent_task.reshape(by_lane), reward_table)))
     from_left = shift(to_right, "gx", 1)
     from_right = shift(to_left, "gx", -1)
     hist, address, lane, looked = pl.pallas_call(
@@ -474,14 +495,16 @@
             pltpu.VMEM((p.ring, agents), jnp.bfloat16),
             pltpu.VMEM((p.tiles * LANES, agents), jnp.bfloat16),
         ],
+        compiler_params=pltpu.CompilerParams(vmem_limit_bytes=12 << 20),
         name="local",
-    )(near(ring_row), near(ring_col), agent_task.reshape(by_lane), reward_table)
-    sides = (near(hist), map_codes, near(from_left), near(from_right))
+    )(near(ring_row), near(ring_col), near(task), near(table))
+    sides = (near(hist), near(kept), near(from_left), near(from_right))
     first, second = pl.pallas_call(
         bind(across_kernel),
         in_specs=[vmem] * 4,
         out_specs=[vmem] * 2,
         out_shape=[fast((p.down_rows, LANES), f32), fast((p.down_rows, LANES), f32)],
+        compiler_params=pltpu.CompilerParams(vmem_limit_bytes=8 << 20),
         name="across",
     )(*sides)
     first = swap(first, "gy", 0)
@@ -492,6 +515,7 @@
         in_specs=[vmem] * 5,
         out_specs=[vmem] * 2,
         out_shape=[fast(flats, f32), fast((p.tiles, 2 * p.near, LANES), f32)],
+        compiler_params=pltpu.CompilerParams(vmem_limit_bytes=12 << 20),
         name="rewards",
     )(*sides, near(looked))
     outs = tasks * (p.tiles - 1)
@@ -513,6 +537,7 @@
             pltpu.SemaphoreType.DMA((outs + 1,)),
         ],
         input_output_aliases={1: 2},
+        compiler_params=pltpu.CompilerParams(vmem_limit_bytes=24 << 20),
         name="sweep",
     )(near(looked), near(flat), near(edges), near(first), near(second), near(address), near(lane))
     return values, answers.reshape(agents)

time: 35.1 us -> 27.5 us (0.78)
  local copies, waits for them, and re-layouts: 5.71 us -> 0 us
  Pallas kernels: 19.3 us -> 16.1 us
  waiting for transfers between devices: 1.3 us -> 2.72 us
    unnamed x12 -> x0, local copies, waits for them, and re-layouts: 5.71 us -> none
    pallas_call x1, Pallas kernels: 1.8 us -> 0.15 us  [on_device(): pl.pallas_call(bind(across_kernel), in_specs=[vmem] * 4, out_specs=[vmem]...]
    pallas_call x1, Pallas kernels: 3.3 us -> 2.36 us  [on_device(): pl.pallas_call(bind(rewards_kernel), in_specs=[vmem] * 5, out_specs=[vmem...]
    ppermute x2, waiting for transfers between devices: 0.01 us -> 0.73 us  [swap(): lax.ppermute(value, axis, [(i, (i + (1 if i % 2 == parity else -1)) % cou...]
    ppermute x2, waiting for transfers between devices: 1.3 us -> 1.99 us  [shift(): lax.ppermute(value, axis, [(i, (i + steps) % count) for i in range(count)])]
    pallas_call x1, Pallas kernels: 2.04 us -> 1.36 us  [on_device(): pl.pallas_call(bind(local_kernel), in_specs=[vmem] * 4, out_specs=[vmem]...]
  transfers between devices with their start and end apart: 4 -> 4, of which waited for: 2 -> 3; matrix products, arithmetic and copies ran while one was open for 0% -> 0% of each run, Pallas kernels for 15% -> 14%
where the time goes in v6:
time: 27.5 us; the launch traced here: 27.3 us
  Pallas kernels  16.1 us (59%)
  starting transfers between devices  7.79 us (28%)
  waiting for transfers between devices  2.72 us (10%)
  between operations  0.66 us (2%)
    pallas_call x1, Pallas kernels, on_device(): pl.pallas_call(bind(sweep_kernel), in_specs=[vmem] * 7, out_specs=[pl.Blo...  10.3 us
    ppermute x2, starting transfers between devices, shift(): lax.ppermute(value, axis, [(i, (i + steps) % count) for i in range(count)])  6.12 us
    pallas_call x1, Pallas kernels, on_device(): pl.pallas_call(bind(rewards_kernel), in_specs=[vmem] * 5, out_specs=[vmem...  2.36 us
    ppermute x2, waiting for transfers between devices, shift(): lax.ppermute(value, axis, [(i, (i + steps) % count) for i in range(count)])  1.99 us
    pallas_call x1, Pallas kernels, on_device(): pl.pallas_call(bind(bands_kernel), in_specs=[pl.BlockSpec(memory_space=pl...  1.98 us
    ppermute x2, starting transfers between devices, swap(): lax.ppermute(value, axis, [(i, (i + (1 if i % 2 == parity else -1)) % cou...  1.66 us
    pallas_call x1, Pallas kernels, on_device(): pl.pallas_call(bind(local_kernel), in_specs=[vmem] * 4, out_specs=[vmem]...  1.36 us
    ppermute x2, waiting for transfers between devices, swap(): lax.ppermute(value, axis, [(i, (i + (1 if i % 2 == parity else -1)) % cou...  0.73 us
  transfers between devices with their start and end apart: 4, of which 3 were waited for; matrix products, arithmetic and copies ran while one was open for 0% of the time, Pallas kernels for 14%

profile of v6, /device:TPU:0, one launch (start us, length us, event | category | flops | bytes accessed | tf_op | source)
XLA Modules:
  0.0 27.3 jit_solution(15227514535479682230)
XLA Ops:
  0.6 2.0 %bands.1 = (f32[176,128]{1,0:T(8,128)S(1)}, f32[176,128]{1,0:T(8,128)S(1)}, s32[16,128]{1,0:T(8,128)S(1)}, s32[16,128]{1,0:T(8,128)S(1)}, s32[256,256]{1,0:T(8,1...) custom-call(s32[16,2048]{1,0:T(8,128)} %refs_0_.1, s32[16,128]{1,0:T(8,128)} %bitcast.3, s32[256,256]{1,0:T(8,128)} %refs_2_.1, ...), custom_call_target="tpu_custom_call" | custom-call | tf_op jit(solution)/shard_map/bands/pallas_call | solution.py:459
  2.6 3.0 %collective-permute-start = (f32[176,128]{1,0:T(8,128)S(1)}, f32[176,128]{1,0:T(8,128)S(1)}, u32[]{:S(2)}, u32[]{:S(2)}) collective-permute-start(f32[176,128]{1,0:T(8,128)S(1)} %get-tuple-element.26), channel_id=1, source_target_pairs={{0,4},{4,8},{8,12},{12,16},{16,20},{20,24},{24,28},{28,0},{1,5},{5... | collective-permute-start | bytes 270344 | tf_op jit(solution)/shard_map/ppermute | solution.py:428
  5.6 3.1 %collective-permute-start.1 = (f32[176,128]{1,0:T(8,128)S(1)}, f32[176,128]{1,0:T(8,128)S(1)}, u32[]{:S(2)}, u32[]{:S(2)}) collective-permute-start(f32[176,128]{1,0:T(8,128)S(1)} %get-tuple-element.27), channel_id=1, source_target_pairs={{0,28},{4,0},{8,4},{12,8},{16,12},{20,16},{24,20},{28,24},{1,29},{... | collective-permute-start | bytes 270344 | tf_op jit(solution)/shard_map/ppermute | solution.py:428
  8.7 1.4 %local.1 = (f32[3,320,128]{2,1,0:T(8,128)S(1)}, s32[16,128]{1,0:T(8,128)S(1)}, s32[16,128]{1,0:T(8,128)S(1)}, f32[8,128]{1,0:T(8,128)S(1)}) custom-call(s32[16,128]{1,0:T(8,128)S(1)} %get-tuple-element.19.refs_0_, s32[16,128]{1,0:T(8,128)S(1)} %get-tuple-element.20.refs_1_, s32[16,128]{1,0:T(8,128)S(1)} %get-tuple-element.21.refs_2_, ...), custom_call_target="tpu_custom_call" | custom-call | tf_op jit(solution)/shard_map/local/pallas_call | solution.py:484
  10.1 1.3 %collective-permute-done.refs_2_ = f32[176,128]{1,0:T(8,128)S(1)} collective-permute-done((f32[176,128]{1,0:T(8,128)S(1)}, f32[176,128]{1,0:T(8,128)S(1)}, u32[]{:S(2)}, u32[]{:S(2)}) %collective-permute-start) | collective-permute-done | bytes 90144 | tf_op jit(solution)/shard_map/ppermute | solution.py:428
  11.4 0.7 %collective-permute-done.1.refs_3_ = f32[176,128]{1,0:T(8,128)S(1)} collective-permute-done((f32[176,128]{1,0:T(8,128)S(1)}, f32[176,128]{1,0:T(8,128)S(1)}, u32[]{:S(2)}, u32[]{:S(2)}) %collective-permute-start.1) | collective-permute-done | bytes 90144 | tf_op jit(solution)/shard_map/ppermute | solution.py:428
  12.1 0.1 across.1
  12.3 0.0 collective-permute-start.2
  12.3 1.6 %collective-permute-start.3 = (f32[208,128]{1,0:T(8,128)S(1)}, f32[208,128]{1,0:T(8,128)S(1)}, u32[]{:S(2)}, u32[]{:S(2)}) collective-permute-start(f32[208,128]{1,0:T(8,128)S(1)} %get-tuple-element.31), channel_id=1, source_target_pairs={{0,3},{1,2},{2,1},{3,0},{4,7},{5,6},{6,5},{7,4},{8,11},{9,10},{10,... | collective-permute-start | bytes 319496 | tf_op jit(solution)/shard_map/ppermute | solution.py:434
  13.9 2.4 %rewards.1 = (f32[15,320,128]{2,1,0:T(8,128)S(1)}, f32[3,32,128]{2,1,0:T(8,128)S(1)}) custom-call(f32[3,320,128]{2,1,0:T(8,128)S(1)} %get-tuple-element.24.refs_0_, s32[256,256]{1,0:T(8,128)S(1)} %get-tuple-element.25.refs_1_, f32[176,128]{1,0:T(8,128)S(1)} %collective-permute-done.refs_2_, f32[176,128]{1,0:T(8,128)S(1)} %collective-permute-done.1.refs_3_, ...), custom_call_target="tpu_custom_call" | custom-call | tf_op jit(solution)/shard_map/rewards/pallas_call | solution.py:513
  16.3 0.0 collective-permute-done.2.refs_3_
  16.3 0.7 %collective-permute-done.3.refs_4_ = f32[208,128]{1,0:T(8,128)S(1)} collective-permute-done((f32[208,128]{1,0:T(8,128)S(1)}, f32[208,128]{1,0:T(8,128)S(1)}, u32[]{:S(2)}, u32[]{:S(2)}) %collective-permute-start.3) | collective-permute-done | bytes 106528 | tf_op jit(solution)/shard_map/ppermute | solution.py:434
  17.0 10.3 %sweep.1 = (f32[4,256,256]{2,1,0:T(8,128)}, f32[16,128]{1,0:T(8,128)}, f32[15,320,128]{2,1,0:T(8,128)S(1)}) custom-call(f32[8,128]{1,0:T(8,128)S(1)} %get-tuple-element.23.refs_4_.refs_0_, f32[15,320,128]{2,1,0:T(8,128)S(1)} %get-tuple-element.28.refs_1_, f32[3,32,128]{2,1,0:T(8,128)S(1)} %get-tuple-element.29.refs_2_, ...), custom_call_target="tpu_custom_call", output_to_operand_aliasing={{2}: (1, {})} | custom-call | tf_op jit(solution)/shard_map/sweep/pallas_call | solution.py:522
Async XLA Ops:
  2.6 8.8 %collective-permute-start = (f32[176,128]{1,0:T(8,128)S(1)}, f32[176,128]{1,0:T(8,128)S(1)}, u32[]{:S(2)}, u32[]{:S(2)}) collective-permute-start(f32[176,128]{1,0:T(8,128)S(1)} %get-tuple-element.26), channel_id=1, source_target_pairs={{0,4},{4,8},{8,12},{12,16},{16,20},{20,24},{24,28},{28,0},{1,5},{5... | collective-permute-start | bytes 270344 | tf_op jit(solution)/shard_map/ppermute | solution.py:428
  5.6 6.5 %collective-permute-start.1 = (f32[176,128]{1,0:T(8,128)S(1)}, f32[176,128]{1,0:T(8,128)S(1)}, u32[]{:S(2)}, u32[]{:S(2)}) collective-permute-start(f32[176,128]{1,0:T(8,128)S(1)} %get-tuple-element.27), channel_id=1, source_target_pairs={{0,28},{4,0},{8,4},{12,8},{16,12},{20,16},{24,20},{28,24},{1,29},{... | collective-permute-start | bytes 270344 | tf_op jit(solution)/shard_map/ppermute | solution.py:428
  12.3 4.0 %collective-permute-start.2 = (f32[208,128]{1,0:T(8,128)S(1)}, f32[208,128]{1,0:T(8,128)S(1)}, u32[]{:S(2)}, u32[]{:S(2)}) collective-permute-start(f32[208,128]{1,0:T(8,128)S(1)} %get-tuple-element.30), channel_id=1, source_target_pairs={{0,1},{1,0},{2,3},{3,2},{4,5},{5,4},{6,7},{7,6},{8,9},{9,8},{10,11... | collective-permute-start | bytes 319496 | tf_op jit(solution)/shard_map/ppermute | solution.py:434
  12.3 4.7 %collective-permute-start.3 = (f32[208,128]{1,0:T(8,128)S(1)}, f32[208,128]{1,0:T(8,128)S(1)}, u32[]{:S(2)}, u32[]{:S(2)}) collective-permute-start(f32[208,128]{1,0:T(8,128)S(1)} %get-tuple-element.31), channel_id=1, source_target_pairs={{0,3},{1,2},{2,1},{3,0},{4,7},{5,6},{6,5},{7,4},{8,11},{9,10},{10,... | collective-permute-start | bytes 319496 | tf_op jit(solution)/shard_map/ppermute | solution.py:434

commit v7 on v6

--- a/solution.py
+++ b/solution.py
@@ -14,6 +14,7 @@
 SUB = 8
 PACK = 2
 UNROLL = 2
+TAIL = 12
 
 
 class Plan:
@@ -290,7 +291,7 @@
 
 
 def sweep_kernel(plan, looked, flat_in, near, first, second, address_in, lane_in, values, answers, flat,
-                 turned, reward, gain, value, edge, final, natural, rows_of, address, sems):
+                 turned, reward, gain, value, edge, spin, raw, final, natural, rows_of, address, sems):
     p = plan
     del flat_in
     fetch_address = pltpu.make_async_copy(address_in, address, sems.at[p.tasks * (p.tiles - 1)])
@@ -342,35 +343,73 @@
                     turned[u * p.deep + i, pl.ds(w + p.cols, w), :] = x[:w]
                     turned[u * p.deep + i, pl.ds(0, w), :] = x[LANES - w :]
 
+    early = p.span - TAIL
+    ends = [(u, up) for u in range(p.groups) for up in (True, False)]
+
+    def end_of(line, u, up):
+        return line[u * p.deep + (p.deep - 1 if up else 0)]
+
+    def turn(x, up):
+        return pltpu.roll(x, 1 if up else LANES - 1, 1)
+
+    def spot(q, e):
+        return pl.ds((q * len(ends) + e) * SUB, SUB)
+
+    def put_ends(q, line):
+        for e, (u, up) in enumerate(ends):
+            x = end_of(line, u, up)
+            if q < early:
+                spin[spot(q, e), :] = turn(x, up)
+            else:
+                raw[spot(q - early, e), :] = x
+
     for q in range(p.span):
+        line = []
         for n in range(p.planes + p.deep):
             x = turned[n, pl.ds(q, SUB, stride=p.span), :]
             if n < p.planes:
-                at = pl.ds((q * p.planes + n) * SUB, SUB)
-                reward[at, :] = x
+                reward[pl.ds((q * p.planes + n) * SUB, SUB), :] = x
+                line.append(x)
             else:
                 gain[pl.ds((q * p.deep + n - p.planes) * SUB, SUB), :] = x
-
-    def sweep(held, put):
+        put_ends(q, line)
+
+    def sweep(held, put, more=True):
         load = lambda q: [held[pl.ds((q * p.planes + n) * SUB, SUB), :] for n in range(p.planes)]
+        for q in range(early, p.span):
+            for e, (u, up) in enumerate(ends):
+                spin[spot(q, e), :] = turn(raw[spot(q - early, e), :], up)
         now = load(0)
         before = [pltpu.roll(x, 1, 0) for x in load(p.span - 1)]
         for n in range(p.planes):
             edge[pl.ds(n * SUB, SUB), :] = pltpu.roll(now[n], SUB - 1, 0)
+        passed = [
+            jnp.maximum(before[n - 1], now[n]) if n % p.deep else None for n in range(p.planes)
+        ]
         for q in range(p.span):
             if q + 1 < p.span:
                 after = load(q + 1)
             else:
                 after = [edge[pl.ds(n * SUB, SUB), :] for n in range(p.planes)]
+            corner = [None] * p.planes
+            made = [None] * p.planes
+            for n in range(p.planes):
+                above_cell = now[n - 1] if n % p.deep else spin[spot(q, 2 * (n // p.deep)), :]
+                corner[n] = jnp.maximum(above_cell, after[n])
             for i in range(p.deep):
                 g = gain[pl.ds((q * p.deep + i) * SUB, SUB), :]
                 for u in range(p.groups):
                     n = u * p.deep + i
-                    up = now[n - 1] if i > 0 else pltpu.roll(now[n + p.deep - 1], 1, 1)
-                    down = now[n + 1] if i + 1 < p.deep else pltpu.roll(now[n + 1 - p.deep], LANES - 1, 1)
-                    best = jnp.maximum(jnp.maximum(up, down), jnp.maximum(before[n], after[n]))
-                    put(q, n, reward[pl.ds((q * p.planes + n) * SUB, SUB), :] + g * best)
-            before, now = now, after
+                    if i + 1 < p.deep:
+                        other = passed[n + 1]
+                    else:
+                        other = jnp.maximum(before[n], spin[spot(q, 2 * u + 1), :])
+                    best = jnp.maximum(corner[n], other)
+                    made[n] = reward[pl.ds((q * p.planes + n) * SUB, SUB), :] + g * best
+                    put(q, n, made[n])
+            if more:
+                put_ends(q, made)
+            before, now, passed = now, after, corner
 
     def put_value(q, n, x):
         value[pl.ds((q * p.planes + n) * SUB, SUB), :] = x
@@ -386,7 +425,7 @@
     assert (SWEEPS - 2) % UNROLL == 0
     sweep(reward, put_value)
     lax.fori_loop(0, (SWEEPS - 2) // UNROLL, sweeps, 0)
-    sweep(value, put_final)
+    sweep(value, put_final, more=False)
     fetch_address.wait()
 
     copies = []
@@ -530,6 +569,8 @@
             pltpu.VMEM((p.deep * p.lines, LANES), f32),
             pltpu.VMEM((p.planes * p.lines, LANES), f32),
             pltpu.VMEM((p.planes * SUB, LANES), f32),
+            pltpu.VMEM((2 * p.groups * p.span * SUB, LANES), f32),
+            pltpu.VMEM((2 * p.groups * TAIL * SUB, LANES), f32),
             pltpu.VMEM((p.planes * p.lines, LANES), f32),
             pltpu.VMEM((outs, p.ring, LANES), f32),
             pltpu.VMEM((agents, LANES), f32),

time: 27.5 us -> 27.4 us (level)
  no operation moved by 1% of the time
where the time goes in v7:
time: 27.4 us; the launch traced here: 27.2 us
  Pallas kernels  16 us (58%)
  starting transfers between devices  7.79 us (28%)
  waiting for transfers between devices  2.72 us (10%)
  between operations  0.66 us (2%)
    pallas_call x1, Pallas kernels, on_device(): pl.pallas_call(bind(sweep_kernel), in_specs=[vmem] * 7, out_specs=[pl.Blo...  10.2 us
    ppermute x2, starting transfers between devices, shift(): lax.ppermute(value, axis, [(i, (i + steps) % count) for i in range(count)])  6.12 us
    pallas_call x1, Pallas kernels, on_device(): pl.pallas_call(bind(rewards_kernel), in_specs=[vmem] * 5, out_specs=[vmem...  2.36 us
    ppermute x2, waiting for transfers between devices, shift(): lax.ppermute(value, axis, [(i, (i + steps) % count) for i in range(count)])  1.99 us
    pallas_call x1, Pallas kernels, on_device(): pl.pallas_call(bind(bands_kernel), in_specs=[pl.BlockSpec(memory_space=pl...  1.98 us
    ppermute x2, starting transfers between devices, swap(): lax.ppermute(value, axis, [(i, (i + (1 if i % 2 == parity else -1)) % cou...  1.66 us
    pallas_call x1, Pallas kernels, on_device(): pl.pallas_call(bind(local_kernel), in_specs=[vmem] * 4, out_specs=[vmem]...  1.36 us
    ppermute x2, waiting for transfers between devices, swap(): lax.ppermute(value, axis, [(i, (i + (1 if i % 2 == parity else -1)) % cou...  0.73 us
  transfers between devices with their start and end apart: 4, of which 3 were waited for; matrix products, arithmetic and copies ran while one was open for 0% of the time, Pallas kernels for 14%

profile of v7, /device:TPU:0, one launch (start us, length us, event | category | flops | bytes accessed | tf_op | source)
XLA Modules:
  0.0 27.2 jit_solution(10157766399253582502)
XLA Ops:
  0.6 2.0 %bands.1 = (f32[176,128]{1,0:T(8,128)S(1)}, f32[176,128]{1,0:T(8,128)S(1)}, s32[16,128]{1,0:T(8,128)S(1)}, s32[16,128]{1,0:T(8,128)S(1)}, s32[256,256]{1,0:T(8,1...) custom-call(s32[16,2048]{1,0:T(8,128)} %refs_0_.1, s32[16,128]{1,0:T(8,128)} %bitcast.3, s32[256,256]{1,0:T(8,128)} %refs_2_.1, ...), custom_call_target="tpu_custom_call" | custom-call | tf_op jit(solution)/shard_map/bands/pallas_call | solution.py:498
  2.6 3.0 %collective-permute-start = (f32[176,128]{1,0:T(8,128)S(1)}, f32[176,128]{1,0:T(8,128)S(1)}, u32[]{:S(2)}, u32[]{:S(2)}) collective-permute-start(f32[176,128]{1,0:T(8,128)S(1)} %get-tuple-element.26), channel_id=1, source_target_pairs={{0,4},{4,8},{8,12},{12,16},{16,20},{20,24},{24,28},{28,0},{1,5},{5... | collective-permute-start | bytes 270344 | tf_op jit(solution)/shard_map/ppermute | solution.py:467
  5.6 3.1 %collective-permute-start.1 = (f32[176,128]{1,0:T(8,128)S(1)}, f32[176,128]{1,0:T(8,128)S(1)}, u32[]{:S(2)}, u32[]{:S(2)}) collective-permute-start(f32[176,128]{1,0:T(8,128)S(1)} %get-tuple-element.27), channel_id=1, source_target_pairs={{0,28},{4,0},{8,4},{12,8},{16,12},{20,16},{24,20},{28,24},{1,29},{... | collective-permute-start | bytes 270344 | tf_op jit(solution)/shard_map/ppermute | solution.py:467
  8.7 1.4 %local.1 = (f32[3,320,128]{2,1,0:T(8,128)S(1)}, s32[16,128]{1,0:T(8,128)S(1)}, s32[16,128]{1,0:T(8,128)S(1)}, f32[8,128]{1,0:T(8,128)S(1)}) custom-call(s32[16,128]{1,0:T(8,128)S(1)} %get-tuple-element.19.refs_0_, s32[16,128]{1,0:T(8,128)S(1)} %get-tuple-element.20.refs_1_, s32[16,128]{1,0:T(8,128)S(1)} %get-tuple-element.21.refs_2_, ...), custom_call_target="tpu_custom_call" | custom-call | tf_op jit(solution)/shard_map/local/pallas_call | solution.py:523
  10.1 1.3 %collective-permute-done.refs_2_ = f32[176,128]{1,0:T(8,128)S(1)} collective-permute-done((f32[176,128]{1,0:T(8,128)S(1)}, f32[176,128]{1,0:T(8,128)S(1)}, u32[]{:S(2)}, u32[]{:S(2)}) %collective-permute-start) | collective-permute-done | bytes 90144 | tf_op jit(solution)/shard_map/ppermute | solution.py:467
  11.4 0.7 %collective-permute-done.1.refs_3_ = f32[176,128]{1,0:T(8,128)S(1)} collective-permute-done((f32[176,128]{1,0:T(8,128)S(1)}, f32[176,128]{1,0:T(8,128)S(1)}, u32[]{:S(2)}, u32[]{:S(2)}) %collective-permute-start.1) | collective-permute-done | bytes 90144 | tf_op jit(solution)/shard_map/ppermute | solution.py:467
  12.1 0.1 across.1
  12.3 0.0 collective-permute-start.2
  12.3 1.6 %collective-permute-start.3 = (f32[208,128]{1,0:T(8,128)S(1)}, f32[208,128]{1,0:T(8,128)S(1)}, u32[]{:S(2)}, u32[]{:S(2)}) collective-permute-start(f32[208,128]{1,0:T(8,128)S(1)} %get-tuple-element.31), channel_id=1, source_target_pairs={{0,3},{1,2},{2,1},{3,0},{4,7},{5,6},{6,5},{7,4},{8,11},{9,10},{10,... | collective-permute-start | bytes 319496 | tf_op jit(solution)/shard_map/ppermute | solution.py:473
  13.9 2.4 %rewards.1 = (f32[15,320,128]{2,1,0:T(8,128)S(1)}, f32[3,32,128]{2,1,0:T(8,128)S(1)}) custom-call(f32[3,320,128]{2,1,0:T(8,128)S(1)} %get-tuple-element.24.refs_0_, s32[256,256]{1,0:T(8,128)S(1)} %get-tuple-element.25.refs_1_, f32[176,128]{1,0:T(8,128)S(1)} %collective-permute-done.refs_2_, f32[176,128]{1,0:T(8,128)S(1)} %collective-permute-done.1.refs_3_, ...), custom_call_target="tpu_custom_call" | custom-call | tf_op jit(solution)/shard_map/rewards/pallas_call | solution.py:552
  16.3 0.0 collective-permute-done.2.refs_3_
  16.3 0.7 %collective-permute-done.3.refs_4_ = f32[208,128]{1,0:T(8,128)S(1)} collective-permute-done((f32[208,128]{1,0:T(8,128)S(1)}, f32[208,128]{1,0:T(8,128)S(1)}, u32[]{:S(2)}, u32[]{:S(2)}) %collective-permute-start.3) | collective-permute-done | bytes 106528 | tf_op jit(solution)/shard_map/ppermute | solution.py:473
  17.0 10.2 %sweep.1 = (f32[4,256,256]{2,1,0:T(8,128)}, f32[16,128]{1,0:T(8,128)}, f32[15,320,128]{2,1,0:T(8,128)S(1)}) custom-call(f32[8,128]{1,0:T(8,128)S(1)} %get-tuple-element.23.refs_4_.refs_0_, f32[15,320,128]{2,1,0:T(8,128)S(1)} %get-tuple-element.28.refs_1_, f32[3,32,128]{2,1,0:T(8,128)S(1)} %get-tuple-element.29.refs_2_, ...), custom_call_target="tpu_custom_call", output_to_operand_aliasing={{2}: (1, {})} | custom-call | tf_op jit(solution)/shard_map/sweep/pallas_call | solution.py:561
Async XLA Ops:
  2.6 8.8 %collective-permute-start = (f32[176,128]{1,0:T(8,128)S(1)}, f32[176,128]{1,0:T(8,128)S(1)}, u32[]{:S(2)}, u32[]{:S(2)}) collective-permute-start(f32[176,128]{1,0:T(8,128)S(1)} %get-tuple-element.26), channel_id=1, source_target_pairs={{0,4},{4,8},{8,12},{12,16},{16,20},{20,24},{24,28},{28,0},{1,5},{5... | collective-permute-start | bytes 270344 | tf_op jit(solution)/shard_map/ppermute | solution.py:467
  5.6 6.5 %collective-permute-start.1 = (f32[176,128]{1,0:T(8,128)S(1)}, f32[176,128]{1,0:T(8,128)S(1)}, u32[]{:S(2)}, u32[]{:S(2)}) collective-permute-start(f32[176,128]{1,0:T(8,128)S(1)} %get-tuple-element.27), channel_id=1, source_target_pairs={{0,28},{4,0},{8,4},{12,8},{16,12},{20,16},{24,20},{28,24},{1,29},{... | collective-permute-start | bytes 270344 | tf_op jit(solution)/shard_map/ppermute | solution.py:467
  12.3 4.0 %collective-permute-start.2 = (f32[208,128]{1,0:T(8,128)S(1)}, f32[208,128]{1,0:T(8,128)S(1)}, u32[]{:S(2)}, u32[]{:S(2)}) collective-permute-start(f32[208,128]{1,0:T(8,128)S(1)} %get-tuple-element.30), channel_id=1, source_target_pairs={{0,1},{1,0},{2,3},{3,2},{4,5},{5,4},{6,7},{7,6},{8,9},{9,8},{10,11... | collective-permute-start | bytes 319496 | tf_op jit(solution)/shard_map/ppermute | solution.py:473
  12.3 4.7 %collective-permute-start.3 = (f32[208,128]{1,0:T(8,128)S(1)}, f32[208,128]{1,0:T(8,128)S(1)}, u32[]{:S(2)}, u32[]{:S(2)}) collective-permute-start(f32[208,128]{1,0:T(8,128)S(1)} %get-tuple-element.31), channel_id=1, source_target_pairs={{0,3},{1,2},{2,1},{3,0},{4,7},{5,6},{6,5},{7,4},{8,11},{9,10},{10,... | collective-permute-start | bytes 319496 | tf_op jit(solution)/shard_map/ppermute | solution.py:473

commit v8 on v7

--- a/solution.py
+++ b/solution.py
@@ -31,7 +31,8 @@
         self.deep = self.ring // self.blocks
         self.groups = tasks // PACK
         self.planes = self.groups * self.deep
-        self.code_bits = (codes - 1).bit_length()
+        self.code_bits = max(3, (codes - 1).bit_length())
+        self.shelf = 1 << self.code_bits
         self.message = rows + 2 * self.near
         self.half = self.message // 2
         self.band = self.wide + self.near
@@ -43,7 +44,7 @@
         assert self.half % SUB == 0 and LANES % self.wide == 0 and self.near % 16 == 0
         assert self.band + self.wide + self.band <= LANES
         assert self.ring % self.blocks == 0 and self.lines % SUB == 0
-        assert tasks % PACK == 0 and codes <= LANES
+        assert tasks % PACK == 0 and self.shelf <= LANES and tasks <= LANES
         self.magic = -(-(1 << 16) // self.deep)
         assert all((r * self.magic) >> 16 == r // self.deep for r in range(self.ring))
 
@@ -152,7 +153,7 @@
 
 
 def local_kernel(
-    plan, ring_row, ring_col, task, table, hist, address, lane_out, looked, row_hot, col_hot
+    plan, ring_row, ring_col, task, table, hist, address, lane_out, looked, row_hot, col_hot, padded
 ):
     p = plan
     ring_cols = p.tiles * LANES
@@ -175,8 +176,11 @@
     counts = counted(row_hot, col_hot)
     for t in range(p.tiles):
         hist[t] = counts[:, t * LANES : (t + 1) * LANES]
-    looked[...] = jnp.zeros_like(looked)
-    looked[pl.ds(0, p.tasks), pl.ds(0, p.codes)] = table[...]
+    padded[...] = jnp.zeros_like(padded)
+    padded[pl.ds(0, p.tasks), pl.ds(0, p.codes)] = table[...]
+    upright = jnp.transpose(padded[...])
+    for t in range(p.tasks):
+        looked[t] = jnp.broadcast_to(upright[: p.shelf, t : t + 1], (p.shelf, LANES))
 
 
 def side_counts(p, message, shift, lo, n):
@@ -263,15 +267,23 @@
 
 
 def look_up(p, looked):
-    tables = [jnp.broadcast_to(looked[t : t + 1, :], (SUB, LANES)) for t in range(p.tasks)]
+    def pick(t, low, high):
+        found = [
+            jnp.take_along_axis(looked[t, pl.ds(g * SUB, SUB), :], low, axis=0, mode="promise_in_bounds")
+            for g in range(p.shelf // SUB)
+        ]
+        for bit in high:
+            found = [jnp.where(bit, found[g + 1], found[g]) for g in range(0, len(found), 2)]
+        return found[0]
 
     def put(flat, c, at, code, count):
         crowd = PENALTY * count
         at = pl.ds(at, SUB)
+        low = code & (SUB - 1)
+        high = [(code & (1 << b)) != 0 for b in range(3, p.code_bits)]
         flat[p.tasks * p.tiles + c, at, :] = jnp.where(code < p.codes - TERMINAL, GAMMA, 0.0)
         for t in range(p.tasks):
-            found = jnp.take_along_axis(tables[t], code, axis=1, mode="promise_in_bounds")
-            flat[t * p.tiles + c, at, :] = found - crowd
+            flat[t * p.tiles + c, at, :] = pick(t, low, high) - crowd
 
     return put
 
@@ -322,12 +334,12 @@
             code = above(code_base + row, SUB) if c < last else roll(count, half)
             if row >= w - s:
                 count = count + near[c, pl.ds(s + row - (w - s), SUB), :]
-            put(flat, c, row, code.astype(jnp.int32) & (LANES - 1), count)
+            put(flat, c, row, code.astype(jnp.int32) & (p.shelf - 1), count)
             count = below(base + s + row, SUB)
             code = below(code_base + row, SUB) if c < last else roll(count, half)
             if row < s:
                 count = count + near[c, pl.ds(row, SUB), :]
-            put(flat, c, w + p.rows + row, code.astype(jnp.int32) & (LANES - 1), count)
+            put(flat, c, w + p.rows + row, code.astype(jnp.int32) & (p.shelf - 1), count)
 
     for u in range(p.groups + 1):
         for i in range(p.deep):
@@ -428,7 +440,19 @@
     sweep(value, put_final, more=False)
     fetch_address.wait()
 
+    lane_id = lax.broadcasted_iota(jnp.int32, (LANES, LANES), 0)
+
+    def fetch(a):
+        rows_of[pl.ds(a, 1), :] = final[pl.ds(address[a // LANES, a % LANES], 1), :]
+
+    def answer(i):
+        x = jnp.transpose(rows_of[pl.ds(i * LANES, LANES), :])
+        picked = jnp.where(lane_id == lane_in[i : i + 1, :], x, 0.0)
+        answers[i : i + 1, :] = jnp.sum(picked, axis=0, keepdims=True)
+
     copies = []
+    fetched = answered = 0
+    turns = p.planes * last
     for u in range(p.groups):
         for c in range(last):
             for i in range(p.deep):
@@ -437,6 +461,13 @@
                 for h in range(PACK):
                     at = pl.ds(i, p.blocks, stride=p.deep)
                     natural[(u * PACK + h) * last + c, at, :] = x[h * p.blocks : (h + 1) * p.blocks]
+                until = -(-p.agents * ((u * last + c) * p.deep + i + 1) // turns)
+                for a in range(fetched, until):
+                    fetch(a)
+                fetched = until
+                while (answered + 1) * LANES <= fetched:
+                    answer(answered)
+                    answered += 1
             for h in range(PACK):
                 t = u * PACK + h
                 copy = pltpu.make_async_copy(
@@ -446,18 +477,6 @@
                 )
                 copy.start()
                 copies.append(copy)
-
-    def fetch(i, carry):
-        for l in range(LANES):
-            rows_of[pl.ds(i * LANES + l, 1), :] = final[pl.ds(address[i, l], 1), :]
-        return carry
-
-    lax.fori_loop(0, p.agents // LANES, fetch, 0)
-    lane_id = lax.broadcasted_iota(jnp.int32, (LANES, LANES), 0)
-    for i in range(p.agents // LANES):
-        x = jnp.transpose(rows_of[pl.ds(i * LANES, LANES), :])
-        picked = jnp.where(lane_id == lane_in[i : i + 1, :], x, 0.0)
-        answers[i : i + 1, :] = jnp.sum(picked, axis=0, keepdims=True)
     for copy in copies:
         copy.wait()
 
@@ -528,11 +547,12 @@
             fast((p.tiles, p.ring, LANES), f32),
             fast(by_lane, i32),
             fast(by_lane, i32),
-            fast((SUB, LANES), f32),
+            fast((tasks, p.shelf, LANES), f32),
         ],
         scratch_shapes=[
             pltpu.VMEM((p.ring, agents), jnp.bfloat16),
             pltpu.VMEM((p.tiles * LANES, agents), jnp.bfloat16),
+            pltpu.VMEM((LANES, LANES), f32),
         ],
         compiler_params=pltpu.CompilerParams(vmem_limit_bytes=12 << 20),
         name="local",

time: 27.4 us -> 26.7 us (0.974)
  Pallas kernels: 16 us -> 14.1 us
  waiting for transfers between devices: 2.72 us -> 3.98 us
    pallas_call x1, Pallas kernels: 2.36 us -> 1.17 us  [on_device(): pl.pallas_call(bind(rewards_kernel), in_specs=[vmem] * 5, out_specs=[vmem...]
    ppermute x2, waiting for transfers between devices: 0.73 us -> 1.92 us  [swap(): lax.ppermute(value, axis, [(i, (i + (1 if i % 2 == parity else -1)) % cou...]
    pallas_call x1, Pallas kernels: 10.2 us -> 9.5 us  [on_device(): pl.pallas_call(bind(sweep_kernel), in_specs=[vmem] * 7, out_specs=[pl.Blo...]
  transfers between devices with their start and end apart: 4 -> 4, of which waited for: 3 -> 3; matrix products, arithmetic and copies ran while one was open for 0% -> 0% of each run, Pallas kernels for 14% -> 9%
where the time goes in v8:
time: 26.7 us; the launch traced here: 26.5 us
  Pallas kernels  14.1 us (53%)
  starting transfers between devices  7.79 us (29%)
  waiting for transfers between devices  3.98 us (15%)
  between operations  0.67 us (3%)
    pallas_call x1, Pallas kernels, on_device(): pl.pallas_call(bind(sweep_kernel), in_specs=[vmem] * 7, out_specs=[pl.Blo...  9.5 us
    ppermute x2, starting transfers between devices, shift(): lax.ppermute(value, axis, [(i, (i + steps) % count) for i in range(count)])  6.12 us
    ppermute x2, waiting for transfers between devices, shift(): lax.ppermute(value, axis, [(i, (i + steps) % count) for i in range(count)])  2.06 us
    pallas_call x1, Pallas kernels, on_device(): pl.pallas_call(bind(bands_kernel), in_specs=[pl.BlockSpec(memory_space=pl...  1.98 us
    ppermute x2, waiting for transfers between devices, swap(): lax.ppermute(value, axis, [(i, (i + (1 if i % 2 == parity else -1)) % cou...  1.92 us
    ppermute x2, starting transfers between devices, swap(): lax.ppermute(value, axis, [(i, (i + (1 if i % 2 == parity else -1)) % cou...  1.66 us
    pallas_call x1, Pallas kernels, on_device(): pl.pallas_call(bind(local_kernel), in_specs=[vmem] * 4, out_specs=[vmem]...  1.29 us
    pallas_call x1, Pallas kernels, on_device(): pl.pallas_call(bind(rewards_kernel), in_specs=[vmem] * 5, out_specs=[vmem...  1.17 us
  transfers between devices with their start and end apart: 4, of which 3 were waited for; matrix products, arithmetic and copies ran while one was open for 0% of the time, Pallas kernels for 9%

profile of v8, /device:TPU:0, one launch (start us, length us, event | category | flops | bytes accessed | tf_op | source)
XLA Modules:
  0.0 26.5 jit_solution(17055558567646446483)
XLA Ops:
  0.6 2.0 %bands.1 = (f32[176,128]{1,0:T(8,128)S(1)}, f32[176,128]{1,0:T(8,128)S(1)}, s32[16,128]{1,0:T(8,128)S(1)}, s32[16,128]{1,0:T(8,128)S(1)}, s32[256,256]{1,0:T(8,1...) custom-call(s32[16,2048]{1,0:T(8,128)} %refs_0_.1, s32[16,128]{1,0:T(8,128)} %bitcast.3, s32[256,256]{1,0:T(8,128)} %refs_2_.1, ...), custom_call_target="tpu_custom_call" | custom-call | tf_op jit(solution)/shard_map/bands/pallas_call | solution.py:517
  2.6 3.0 %collective-permute-start = (f32[176,128]{1,0:T(8,128)S(1)}, f32[176,128]{1,0:T(8,128)S(1)}, u32[]{:S(2)}, u32[]{:S(2)}) collective-permute-start(f32[176,128]{1,0:T(8,128)S(1)} %get-tuple-element.26), channel_id=1, source_target_pairs={{0,4},{4,8},{8,12},{12,16},{16,20},{20,24},{24,28},{28,0},{1,5},{5... | collective-permute-start | bytes 270344 | tf_op jit(solution)/shard_map/ppermute | solution.py:486
  5.6 3.1 %collective-permute-start.1 = (f32[176,128]{1,0:T(8,128)S(1)}, f32[176,128]{1,0:T(8,128)S(1)}, u32[]{:S(2)}, u32[]{:S(2)}) collective-permute-start(f32[176,128]{1,0:T(8,128)S(1)} %get-tuple-element.27), channel_id=1, source_target_pairs={{0,28},{4,0},{8,4},{12,8},{16,12},{20,16},{24,20},{28,24},{1,29},{... | collective-permute-start | bytes 270344 | tf_op jit(solution)/shard_map/ppermute | solution.py:486
  8.7 1.3 %local.1 = (f32[3,320,128]{2,1,0:T(8,128)S(1)}, s32[16,128]{1,0:T(8,128)S(1)}, s32[16,128]{1,0:T(8,128)S(1)}, f32[4,64,128]{2,1,0:T(8,128)S(1)}) custom-call(s32[16,128]{1,0:T(8,128)S(1)} %get-tuple-element.19.refs_0_, s32[16,128]{1,0:T(8,128)S(1)} %get-tuple-element.20.refs_1_, s32[16,128]{1,0:T(8,128)S(1)} %get-tuple-element.21.refs_2_, ...), custom_call_target="tpu_custom_call" | custom-call | tf_op jit(solution)/shard_map/local/pallas_call | solution.py:542
  10.0 1.4 %collective-permute-done.refs_2_ = f32[176,128]{1,0:T(8,128)S(1)} collective-permute-done((f32[176,128]{1,0:T(8,128)S(1)}, f32[176,128]{1,0:T(8,128)S(1)}, u32[]{:S(2)}, u32[]{:S(2)}) %collective-permute-start) | collective-permute-done | bytes 90144 | tf_op jit(solution)/shard_map/ppermute | solution.py:486
  11.4 0.7 %collective-permute-done.1.refs_3_ = f32[176,128]{1,0:T(8,128)S(1)} collective-permute-done((f32[176,128]{1,0:T(8,128)S(1)}, f32[176,128]{1,0:T(8,128)S(1)}, u32[]{:S(2)}, u32[]{:S(2)}) %collective-permute-start.1) | collective-permute-done | bytes 90144 | tf_op jit(solution)/shard_map/ppermute | solution.py:486
  12.1 0.1 across.1
  12.3 0.0 collective-permute-start.2
  12.3 1.6 %collective-permute-start.3 = (f32[208,128]{1,0:T(8,128)S(1)}, f32[208,128]{1,0:T(8,128)S(1)}, u32[]{:S(2)}, u32[]{:S(2)}) collective-permute-start(f32[208,128]{1,0:T(8,128)S(1)} %get-tuple-element.31), channel_id=1, source_target_pairs={{0,3},{1,2},{2,1},{3,0},{4,7},{5,6},{6,5},{7,4},{8,11},{9,10},{10,... | collective-permute-start | bytes 319496 | tf_op jit(solution)/shard_map/ppermute | solution.py:492
  13.9 1.2 %rewards.1 = (f32[15,320,128]{2,1,0:T(8,128)S(1)}, f32[3,32,128]{2,1,0:T(8,128)S(1)}) custom-call(f32[3,320,128]{2,1,0:T(8,128)S(1)} %get-tuple-element.24.refs_0_, s32[256,256]{1,0:T(8,128)S(1)} %get-tuple-element.25.refs_1_, f32[176,128]{1,0:T(8,128)S(1)} %collective-permute-done.refs_2_, f32[176,128]{1,0:T(8,128)S(1)} %collective-permute-done.1.refs_3_, ...), custom_call_target="tpu_custom_call" | custom-call | tf_op jit(solution)/shard_map/rewards/pallas_call | solution.py:572
  15.1 0.0 collective-permute-done.2.refs_3_
  15.1 1.9 %collective-permute-done.3.refs_4_ = f32[208,128]{1,0:T(8,128)S(1)} collective-permute-done((f32[208,128]{1,0:T(8,128)S(1)}, f32[208,128]{1,0:T(8,128)S(1)}, u32[]{:S(2)}, u32[]{:S(2)}) %collective-permute-start.3) | collective-permute-done | bytes 106528 | tf_op jit(solution)/shard_map/ppermute | solution.py:492
  17.0 9.5 %sweep.1 = (f32[4,256,256]{2,1,0:T(8,128)}, f32[16,128]{1,0:T(8,128)}, f32[15,320,128]{2,1,0:T(8,128)S(1)}) custom-call(f32[4,64,128]{2,1,0:T(8,128)S(1)} %get-tuple-element.23.refs_4_.refs_0_, f32[15,320,128]{2,1,0:T(8,128)S(1)} %get-tuple-element.28.refs_1_, f32[3,32,128]{2,1,0:T(8,128)S(1)} %get-tuple-element.29.refs_2_, ...), custom_call_target="tpu_custom_call", output_to_operand_aliasing={{2}: (1, {})} | custom-call | tf_op jit(solution)/shard_map/sweep/pallas_call | solution.py:581
Async XLA Ops:
  2.6 8.8 %collective-permute-start = (f32[176,128]{1,0:T(8,128)S(1)}, f32[176,128]{1,0:T(8,128)S(1)}, u32[]{:S(2)}, u32[]{:S(2)}) collective-permute-start(f32[176,128]{1,0:T(8,128)S(1)} %get-tuple-element.26), channel_id=1, source_target_pairs={{0,4},{4,8},{8,12},{12,16},{16,20},{20,24},{24,28},{28,0},{1,5},{5... | collective-permute-start | bytes 270344 | tf_op jit(solution)/shard_map/ppermute | solution.py:486
  5.6 6.5 %collective-permute-start.1 = (f32[176,128]{1,0:T(8,128)S(1)}, f32[176,128]{1,0:T(8,128)S(1)}, u32[]{:S(2)}, u32[]{:S(2)}) collective-permute-start(f32[176,128]{1,0:T(8,128)S(1)} %get-tuple-element.27), channel_id=1, source_target_pairs={{0,28},{4,0},{8,4},{12,8},{16,12},{20,16},{24,20},{28,24},{1,29},{... | collective-permute-start | bytes 270344 | tf_op jit(solution)/shard_map/ppermute | solution.py:486
  12.3 2.9 %collective-permute-start.2 = (f32[208,128]{1,0:T(8,128)S(1)}, f32[208,128]{1,0:T(8,128)S(1)}, u32[]{:S(2)}, u32[]{:S(2)}) collective-permute-start(f32[208,128]{1,0:T(8,128)S(1)} %get-tuple-element.30), channel_id=1, source_target_pairs={{0,1},{1,0},{2,3},{3,2},{4,5},{5,4},{6,7},{7,6},{8,9},{9,8},{10,11... | collective-permute-start | bytes 319496 | tf_op jit(solution)/shard_map/ppermute | solution.py:492
  12.3 4.7 %collective-permute-start.3 = (f32[208,128]{1,0:T(8,128)S(1)}, f32[208,128]{1,0:T(8,128)S(1)}, u32[]{:S(2)}, u32[]{:S(2)}) collective-permute-start(f32[208,128]{1,0:T(8,128)S(1)} %get-tuple-element.31), channel_id=1, source_target_pairs={{0,3},{1,2},{2,1},{3,0},{4,7},{5,6},{6,5},{7,4},{8,11},{9,10},{10,... | collective-permute-start | bytes 319496 | tf_op jit(solution)/shard_map/ppermute | solution.py:492

commit v9 on v8

--- a/solution.py
+++ b/solution.py
@@ -25,8 +25,9 @@
         self.wide = steps + SWEEPS
         self.ring = rows + 2 * self.wide
         self.tiles = cols // LANES + 1
-        self.lines = cols + 2 * self.wide
-        self.span = self.lines // SUB
+        self.span = (cols + 2 * self.wide) // SUB
+        self.span += 1 - self.span % 2
+        self.lines = self.span * SUB
         self.blocks = LANES // PACK
         self.deep = self.ring // self.blocks
         self.groups = tasks // PACK
@@ -43,7 +44,7 @@
         assert 4 * self.wide <= LANES and self.near % SUB == 0 and self.wide % SUB == 0
         assert self.half % SUB == 0 and LANES % self.wide == 0 and self.near % 16 == 0
         assert self.band + self.wide + self.band <= LANES
-        assert self.ring % self.blocks == 0 and self.lines % SUB == 0
+        assert self.ring % self.blocks == 0
         assert tasks % PACK == 0 and self.shelf <= LANES and tasks <= LANES
         self.magic = -(-(1 << 16) // self.deep)
         assert all((r * self.magic) >> 16 == r // self.deep for r in range(self.ring))
@@ -461,7 +462,7 @@
                 for h in range(PACK):
                     at = pl.ds(i, p.blocks, stride=p.deep)
                     natural[(u * PACK + h) * last + c, at, :] = x[h * p.blocks : (h + 1) * p.blocks]
-                until = -(-p.agents * ((u * last + c) * p.deep + i + 1) // turns)
+                until = min(p.agents, -(-p.agents * 5 * ((u * last + c) * p.deep + i + 1) // (8 * turns)))
                 for a in range(fetched, until):
                     fetch(a)
                 fetched = until
@@ -477,6 +478,10 @@
                 )
                 copy.start()
                 copies.append(copy)
+    for a in range(fetched, p.agents):
+        fetch(a)
+        if (a + 1) % LANES == 0:
+            answer(a // LANES)
     for copy in copies:
         copy.wait()
 

time: 26.7 us -> 26.6 us (level)
  no operation moved by 1% of the time
where the time goes in v9:
time: 26.6 us; the launch traced here: 26.4 us
  Pallas kernels  14 us (53%)
  starting transfers between devices  7.79 us (29%)
  waiting for transfers between devices  3.98 us (15%)
  between operations  0.67 us (3%)
    pallas_call x1, Pallas kernels, on_device(): pl.pallas_call(bind(sweep_kernel), in_specs=[vmem] * 7, out_specs=[pl.Blo...  9.39 us
    ppermute x2, starting transfers between devices, shift(): lax.ppermute(value, axis, [(i, (i + steps) % count) for i in range(count)])  6.12 us
    ppermute x2, waiting for transfers between devices, shift(): lax.ppermute(value, axis, [(i, (i + steps) % count) for i in range(count)])  2.06 us
    pallas_call x1, Pallas kernels, on_device(): pl.pallas_call(bind(bands_kernel), in_specs=[pl.BlockSpec(memory_space=pl...  1.98 us
    ppermute x2, waiting for transfers between devices, swap(): lax.ppermute(value, axis, [(i, (i + (1 if i % 2 == parity else -1)) % cou...  1.92 us
    ppermute x2, starting transfers between devices, swap(): lax.ppermute(value, axis, [(i, (i + (1 if i % 2 == parity else -1)) % cou...  1.66 us
    pallas_call x1, Pallas kernels, on_device(): pl.pallas_call(bind(local_kernel), in_specs=[vmem] * 4, out_specs=[vmem]...  1.29 us
    pallas_call x1, Pallas kernels, on_device(): pl.pallas_call(bind(rewards_kernel), in_specs=[vmem] * 5, out_specs=[vmem...  1.17 us
  transfers between devices with their start and end apart: 4, of which 3 were waited for; matrix products, arithmetic and copies ran while one was open for 0% of the time, Pallas kernels for 9%

profile of v9, /device:TPU:0, one launch (start us, length us, event | category | flops | bytes accessed | tf_op | source)
XLA Modules:
  0.0 26.4 jit_solution(8786266248533233943)
XLA Ops:
  0.6 2.0 %bands.1 = (f32[176,128]{1,0:T(8,128)S(1)}, f32[176,128]{1,0:T(8,128)S(1)}, s32[16,128]{1,0:T(8,128)S(1)}, s32[16,128]{1,0:T(8,128)S(1)}, s32[256,256]{1,0:T(8,1...) custom-call(s32[16,2048]{1,0:T(8,128)} %refs_0_.1, s32[16,128]{1,0:T(8,128)} %bitcast.3, s32[256,256]{1,0:T(8,128)} %refs_2_.1, ...), custom_call_target="tpu_custom_call" | custom-call | tf_op jit(solution)/shard_map/bands/pallas_call | solution.py:522
  2.6 3.0 %collective-permute-start = (f32[176,128]{1,0:T(8,128)S(1)}, f32[176,128]{1,0:T(8,128)S(1)}, u32[]{:S(2)}, u32[]{:S(2)}) collective-permute-start(f32[176,128]{1,0:T(8,128)S(1)} %get-tuple-element.26), channel_id=1, source_target_pairs={{0,4},{4,8},{8,12},{12,16},{16,20},{20,24},{24,28},{28,0},{1,5},{5... | collective-permute-start | bytes 270344 | tf_op jit(solution)/shard_map/ppermute | solution.py:491
  5.6 3.1 %collective-permute-start.1 = (f32[176,128]{1,0:T(8,128)S(1)}, f32[176,128]{1,0:T(8,128)S(1)}, u32[]{:S(2)}, u32[]{:S(2)}) collective-permute-start(f32[176,128]{1,0:T(8,128)S(1)} %get-tuple-element.27), channel_id=1, source_target_pairs={{0,28},{4,0},{8,4},{12,8},{16,12},{20,16},{24,20},{28,24},{1,29},{... | collective-permute-start | bytes 270344 | tf_op jit(solution)/shard_map/ppermute | solution.py:491
  8.7 1.3 %local.1 = (f32[3,320,128]{2,1,0:T(8,128)S(1)}, s32[16,128]{1,0:T(8,128)S(1)}, s32[16,128]{1,0:T(8,128)S(1)}, f32[4,64,128]{2,1,0:T(8,128)S(1)}) custom-call(s32[16,128]{1,0:T(8,128)S(1)} %get-tuple-element.19.refs_0_, s32[16,128]{1,0:T(8,128)S(1)} %get-tuple-element.20.refs_1_, s32[16,128]{1,0:T(8,128)S(1)} %get-tuple-element.21.refs_2_, ...), custom_call_target="tpu_custom_call" | custom-call | tf_op jit(solution)/shard_map/local/pallas_call | solution.py:547
  10.0 1.4 %collective-permute-done.refs_2_ = f32[176,128]{1,0:T(8,128)S(1)} collective-permute-done((f32[176,128]{1,0:T(8,128)S(1)}, f32[176,128]{1,0:T(8,128)S(1)}, u32[]{:S(2)}, u32[]{:S(2)}) %collective-permute-start) | collective-permute-done | bytes 90144 | tf_op jit(solution)/shard_map/ppermute | solution.py:491
  11.4 0.7 %collective-permute-done.1.refs_3_ = f32[176,128]{1,0:T(8,128)S(1)} collective-permute-done((f32[176,128]{1,0:T(8,128)S(1)}, f32[176,128]{1,0:T(8,128)S(1)}, u32[]{:S(2)}, u32[]{:S(2)}) %collective-permute-start.1) | collective-permute-done | bytes 90144 | tf_op jit(solution)/shard_map/ppermute | solution.py:491
  12.1 0.1 across.1
  12.3 0.0 collective-permute-start.2
  12.3 1.6 %collective-permute-start.3 = (f32[208,128]{1,0:T(8,128)S(1)}, f32[208,128]{1,0:T(8,128)S(1)}, u32[]{:S(2)}, u32[]{:S(2)}) collective-permute-start(f32[208,128]{1,0:T(8,128)S(1)} %get-tuple-element.31), channel_id=1, source_target_pairs={{0,3},{1,2},{2,1},{3,0},{4,7},{5,6},{6,5},{7,4},{8,11},{9,10},{10,... | collective-permute-start | bytes 319496 | tf_op jit(solution)/shard_map/ppermute | solution.py:497
  13.9 1.2 %rewards.1 = (f32[15,320,128]{2,1,0:T(8,128)S(1)}, f32[3,32,128]{2,1,0:T(8,128)S(1)}) custom-call(f32[3,320,128]{2,1,0:T(8,128)S(1)} %get-tuple-element.24.refs_0_, s32[256,256]{1,0:T(8,128)S(1)} %get-tuple-element.25.refs_1_, f32[176,128]{1,0:T(8,128)S(1)} %collective-permute-done.refs_2_, f32[176,128]{1,0:T(8,128)S(1)} %collective-permute-done.1.refs_3_, ...), custom_call_target="tpu_custom_call" | custom-call | tf_op jit(solution)/shard_map/rewards/pallas_call | solution.py:577
  15.1 0.0 collective-permute-done.2.refs_3_
  15.1 1.9 %collective-permute-done.3.refs_4_ = f32[208,128]{1,0:T(8,128)S(1)} collective-permute-done((f32[208,128]{1,0:T(8,128)S(1)}, f32[208,128]{1,0:T(8,128)S(1)}, u32[]{:S(2)}, u32[]{:S(2)}) %collective-permute-start.3) | collective-permute-done | bytes 106528 | tf_op jit(solution)/shard_map/ppermute | solution.py:497
  17.0 9.4 %sweep.1 = (f32[4,256,256]{2,1,0:T(8,128)}, f32[16,128]{1,0:T(8,128)}, f32[15,320,128]{2,1,0:T(8,128)S(1)}) custom-call(f32[4,64,128]{2,1,0:T(8,128)S(1)} %get-tuple-element.23.refs_4_.refs_0_, f32[15,320,128]{2,1,0:T(8,128)S(1)} %get-tuple-element.28.refs_1_, f32[3,32,128]{2,1,0:T(8,128)S(1)} %get-tuple-element.29.refs_2_, ...), custom_call_target="tpu_custom_call", output_to_operand_aliasing={{2}: (1, {})} | custom-call | tf_op jit(solution)/shard_map/sweep/pallas_call | solution.py:586
Async XLA Ops:
  2.6 8.8 %collective-permute-start = (f32[176,128]{1,0:T(8,128)S(1)}, f32[176,128]{1,0:T(8,128)S(1)}, u32[]{:S(2)}, u32[]{:S(2)}) collective-permute-start(f32[176,128]{1,0:T(8,128)S(1)} %get-tuple-element.26), channel_id=1, source_target_pairs={{0,4},{4,8},{8,12},{12,16},{16,20},{20,24},{24,28},{28,0},{1,5},{5... | collective-permute-start | bytes 270344 | tf_op jit(solution)/shard_map/ppermute | solution.py:491
  5.6 6.5 %collective-permute-start.1 = (f32[176,128]{1,0:T(8,128)S(1)}, f32[176,128]{1,0:T(8,128)S(1)}, u32[]{:S(2)}, u32[]{:S(2)}) collective-permute-start(f32[176,128]{1,0:T(8,128)S(1)} %get-tuple-element.27), channel_id=1, source_target_pairs={{0,28},{4,0},{8,4},{12,8},{16,12},{20,16},{24,20},{28,24},{1,29},{... | collective-permute-start | bytes 270344 | tf_op jit(solution)/shard_map/ppermute | solution.py:491
  12.3 2.9 %collective-permute-start.2 = (f32[208,128]{1,0:T(8,128)S(1)}, f32[208,128]{1,0:T(8,128)S(1)}, u32[]{:S(2)}, u32[]{:S(2)}) collective-permute-start(f32[208,128]{1,0:T(8,128)S(1)} %get-tuple-element.30), channel_id=1, source_target_pairs={{0,1},{1,0},{2,3},{3,2},{4,5},{5,4},{6,7},{7,6},{8,9},{9,8},{10,11... | collective-permute-start | bytes 319496 | tf_op jit(solution)/shard_map/ppermute | solution.py:497
  12.3 4.7 %collective-permute-start.3 = (f32[208,128]{1,0:T(8,128)S(1)}, f32[208,128]{1,0:T(8,128)S(1)}, u32[]{:S(2)}, u32[]{:S(2)}) collective-permute-start(f32[208,128]{1,0:T(8,128)S(1)} %get-tuple-element.31), channel_id=1, source_target_pairs={{0,3},{1,2},{2,1},{3,0},{4,7},{5,6},{6,5},{7,4},{8,11},{9,10},{10,... | collective-permute-start | bytes 319496 | tf_op jit(solution)/shard_map/ppermute | solution.py:497

commit v10 on v9

--- a/solution.py
+++ b/solution.py
@@ -13,7 +13,7 @@
 LANES = 128
 SUB = 8
 PACK = 2
-UNROLL = 2
+UNROLL = 7
 TAIL = 12
 
 
@@ -61,7 +61,8 @@
 
 
 def one_hot(ids, positions):
-    return jnp.where(ids == positions, 1.0, 0.0).astype(jnp.bfloat16)
+    same = ids.astype(jnp.int16) == positions.astype(jnp.int16)
+    return jnp.where(same, jnp.bfloat16(1), jnp.bfloat16(0))
 
 
 def counted(row_hot, col_hot):

time: 26.6 us -> 26.1 us (0.981)
  Pallas kernels: 14 us -> 13.2 us
  waiting for transfers between devices: 3.98 us -> 4.28 us
    ppermute x2, waiting for transfers between devices: 2.06 us -> 2.36 us  [shift(): lax.ppermute(value, axis, [(i, (i + steps) % count) for i in range(count)])]
    pallas_call x1, Pallas kernels: 1.29 us -> 0.99 us  [on_device(): pl.pallas_call(bind(local_kernel), in_specs=[vmem] * 4, out_specs=[vmem]...]
    pallas_call x1, Pallas kernels: 9.39 us -> 9.1 us  [on_device(): pl.pallas_call(bind(sweep_kernel), in_specs=[vmem] * 7, out_specs=[pl.Blo...]
  transfers between devices with their start and end apart: 4 -> 4, of which waited for: 3 -> 3; matrix products, arithmetic and copies ran while one was open for 0% -> 0% of each run, Pallas kernels for 9% -> 8%
where the time goes in v10:
time: 26.1 us; the launch traced here: 25.9 us
  Pallas kernels  13.2 us (51%)
  starting transfers between devices  7.79 us (30%)
  waiting for transfers between devices  4.28 us (16%)
  between operations  0.67 us (3%)
    pallas_call x1, Pallas kernels, on_device(): pl.pallas_call(bind(sweep_kernel), in_specs=[vmem] * 7, out_specs=[pl.Blo...  9.1 us
    ppermute x2, starting transfers between devices, shift(): lax.ppermute(value, axis, [(i, (i + steps) % count) for i in range(count)])  6.12 us
    ppermute x2, waiting for transfers between devices, shift(): lax.ppermute(value, axis, [(i, (i + steps) % count) for i in range(count)])  2.36 us
    ppermute x2, waiting for transfers between devices, swap(): lax.ppermute(value, axis, [(i, (i + (1 if i % 2 == parity else -1)) % cou...  1.92 us
    pallas_call x1, Pallas kernels, on_device(): pl.pallas_call(bind(bands_kernel), in_specs=[pl.BlockSpec(memory_space=pl...  1.78 us
    ppermute x2, starting transfers between devices, swap(): lax.ppermute(value, axis, [(i, (i + (1 if i % 2 == parity else -1)) % cou...  1.66 us
    pallas_call x1, Pallas kernels, on_device(): pl.pallas_call(bind(rewards_kernel), in_specs=[vmem] * 5, out_specs=[vmem...  1.17 us
    pallas_call x1, Pallas kernels, on_device(): pl.pallas_call(bind(local_kernel), in_specs=[vmem] * 4, out_specs=[vmem]...  0.99 us
  transfers between devices with their start and end apart: 4, of which 3 were waited for; matrix products, arithmetic and copies ran while one was open for 0% of the time, Pallas kernels for 8%

profile of v10, /device:TPU:0, one launch (start us, length us, event | category | flops | bytes accessed | tf_op | source)
XLA Modules:
  0.0 25.9 jit_solution(11208717171827603956)
XLA Ops:
  0.6 1.8 %bands.1 = (f32[176,128]{1,0:T(8,128)S(1)}, f32[176,128]{1,0:T(8,128)S(1)}, s32[16,128]{1,0:T(8,128)S(1)}, s32[16,128]{1,0:T(8,128)S(1)}, s32[256,256]{1,0:T(8,1...) custom-call(s32[16,2048]{1,0:T(8,128)} %refs_0_.1, s32[16,128]{1,0:T(8,128)} %bitcast.3, s32[256,256]{1,0:T(8,128)} %refs_2_.1, ...), custom_call_target="tpu_custom_call" | custom-call | tf_op jit(solution)/shard_map/bands/pallas_call | solution.py:523
  2.4 3.0 %collective-permute-start = (f32[176,128]{1,0:T(8,128)S(1)}, f32[176,128]{1,0:T(8,128)S(1)}, u32[]{:S(2)}, u32[]{:S(2)}) collective-permute-start(f32[176,128]{1,0:T(8,128)S(1)} %get-tuple-element.26), channel_id=1, source_target_pairs={{0,4},{4,8},{8,12},{12,16},{16,20},{20,24},{24,28},{28,0},{1,5},{5... | collective-permute-start | bytes 270344 | tf_op jit(solution)/shard_map/ppermute | solution.py:492
  5.4 3.1 %collective-permute-start.1 = (f32[176,128]{1,0:T(8,128)S(1)}, f32[176,128]{1,0:T(8,128)S(1)}, u32[]{:S(2)}, u32[]{:S(2)}) collective-permute-start(f32[176,128]{1,0:T(8,128)S(1)} %get-tuple-element.27), channel_id=1, source_target_pairs={{0,28},{4,0},{8,4},{12,8},{16,12},{20,16},{24,20},{28,24},{1,29},{... | collective-permute-start | bytes 270344 | tf_op jit(solution)/shard_map/ppermute | solution.py:492
  8.5 1.0 %local.1 = (f32[3,320,128]{2,1,0:T(8,128)S(1)}, s32[16,128]{1,0:T(8,128)S(1)}, s32[16,128]{1,0:T(8,128)S(1)}, f32[4,64,128]{2,1,0:T(8,128)S(1)}) custom-call(s32[16,128]{1,0:T(8,128)S(1)} %get-tuple-element.19.refs_0_, s32[16,128]{1,0:T(8,128)S(1)} %get-tuple-element.20.refs_1_, s32[16,128]{1,0:T(8,128)S(1)} %get-tuple-element.21.refs_2_, ...), custom_call_target="tpu_custom_call" | custom-call | tf_op jit(solution)/shard_map/local/pallas_call | solution.py:548
  9.5 1.7 %collective-permute-done.refs_2_ = f32[176,128]{1,0:T(8,128)S(1)} collective-permute-done((f32[176,128]{1,0:T(8,128)S(1)}, f32[176,128]{1,0:T(8,128)S(1)}, u32[]{:S(2)}, u32[]{:S(2)}) %collective-permute-start) | collective-permute-done | bytes 90144 | tf_op jit(solution)/shard_map/ppermute | solution.py:492
  11.2 0.7 %collective-permute-done.1.refs_3_ = f32[176,128]{1,0:T(8,128)S(1)} collective-permute-done((f32[176,128]{1,0:T(8,128)S(1)}, f32[176,128]{1,0:T(8,128)S(1)}, u32[]{:S(2)}, u32[]{:S(2)}) %collective-permute-start.1) | collective-permute-done | bytes 90144 | tf_op jit(solution)/shard_map/ppermute | solution.py:492
  11.9 0.1 across.1
  12.0 0.0 collective-permute-start.2
  12.1 1.6 %collective-permute-start.3 = (f32[208,128]{1,0:T(8,128)S(1)}, f32[208,128]{1,0:T(8,128)S(1)}, u32[]{:S(2)}, u32[]{:S(2)}) collective-permute-start(f32[208,128]{1,0:T(8,128)S(1)} %get-tuple-element.31), channel_id=1, source_target_pairs={{0,3},{1,2},{2,1},{3,0},{4,7},{5,6},{6,5},{7,4},{8,11},{9,10},{10,... | collective-permute-start | bytes 319496 | tf_op jit(solution)/shard_map/ppermute | solution.py:498
  13.7 1.2 %rewards.1 = (f32[15,320,128]{2,1,0:T(8,128)S(1)}, f32[3,32,128]{2,1,0:T(8,128)S(1)}) custom-call(f32[3,320,128]{2,1,0:T(8,128)S(1)} %get-tuple-element.24.refs_0_, s32[256,256]{1,0:T(8,128)S(1)} %get-tuple-element.25.refs_1_, f32[176,128]{1,0:T(8,128)S(1)} %collective-permute-done.refs_2_, f32[176,128]{1,0:T(8,128)S(1)} %collective-permute-done.1.refs_3_, ...), custom_call_target="tpu_custom_call" | custom-call | tf_op jit(solution)/shard_map/rewards/pallas_call | solution.py:578
  14.9 0.0 collective-permute-done.2.refs_3_
  14.9 1.9 %collective-permute-done.3.refs_4_ = f32[208,128]{1,0:T(8,128)S(1)} collective-permute-done((f32[208,128]{1,0:T(8,128)S(1)}, f32[208,128]{1,0:T(8,128)S(1)}, u32[]{:S(2)}, u32[]{:S(2)}) %collective-permute-start.3) | collective-permute-done | bytes 106528 | tf_op jit(solution)/shard_map/ppermute | solution.py:498
  16.8 9.1 %sweep.1 = (f32[4,256,256]{2,1,0:T(8,128)}, f32[16,128]{1,0:T(8,128)}, f32[15,320,128]{2,1,0:T(8,128)S(1)}) custom-call(f32[4,64,128]{2,1,0:T(8,128)S(1)} %get-tuple-element.23.refs_4_.refs_0_, f32[15,320,128]{2,1,0:T(8,128)S(1)} %get-tuple-element.28.refs_1_, f32[3,32,128]{2,1,0:T(8,128)S(1)} %get-tuple-element.29.refs_2_, ...), custom_call_target="tpu_custom_call", output_to_operand_aliasing={{2}: (1, {})} | custom-call | tf_op jit(solution)/shard_map/sweep/pallas_call | solution.py:587
Async XLA Ops:
  2.4 8.8 %collective-permute-start = (f32[176,128]{1,0:T(8,128)S(1)}, f32[176,128]{1,0:T(8,128)S(1)}, u32[]{:S(2)}, u32[]{:S(2)}) collective-permute-start(f32[176,128]{1,0:T(8,128)S(1)} %get-tuple-element.26), channel_id=1, source_target_pairs={{0,4},{4,8},{8,12},{12,16},{16,20},{20,24},{24,28},{28,0},{1,5},{5... | collective-permute-start | bytes 270344 | tf_op jit(solution)/shard_map/ppermute | solution.py:492
  5.4 6.5 %collective-permute-start.1 = (f32[176,128]{1,0:T(8,128)S(1)}, f32[176,128]{1,0:T(8,128)S(1)}, u32[]{:S(2)}, u32[]{:S(2)}) collective-permute-start(f32[176,128]{1,0:T(8,128)S(1)} %get-tuple-element.27), channel_id=1, source_target_pairs={{0,28},{4,0},{8,4},{12,8},{16,12},{20,16},{24,20},{28,24},{1,29},{... | collective-permute-start | bytes 270344 | tf_op jit(solution)/shard_map/ppermute | solution.py:492
  12.0 2.9 %collective-permute-start.2 = (f32[208,128]{1,0:T(8,128)S(1)}, f32[208,128]{1,0:T(8,128)S(1)}, u32[]{:S(2)}, u32[]{:S(2)}) collective-permute-start(f32[208,128]{1,0:T(8,128)S(1)} %get-tuple-element.30), channel_id=1, source_target_pairs={{0,1},{1,0},{2,3},{3,2},{4,5},{5,4},{6,7},{7,6},{8,9},{9,8},{10,11... | collective-permute-start | bytes 319496 | tf_op jit(solution)/shard_map/ppermute | solution.py:498
  12.1 4.7 %collective-permute-start.3 = (f32[208,128]{1,0:T(8,128)S(1)}, f32[208,128]{1,0:T(8,128)S(1)}, u32[]{:S(2)}, u32[]{:S(2)}) collective-permute-start(f32[208,128]{1,0:T(8,128)S(1)} %get-tuple-element.31), channel_id=1, source_target_pairs={{0,3},{1,2},{2,1},{3,0},{4,7},{5,6},{6,5},{7,4},{8,11},{9,10},{10,... | collective-permute-start | bytes 319496 | tf_op jit(solution)/shard_map/ppermute | solution.py:498
